TPU v7x, 32 devices: a whole 2x2x4 slice. The times are simulated.
32 devices in a mesh: lvl: 8 (over z, y), lon: 4 (over x, core).
Axes of the slice: x: 2, y: 2, z: 4, core: 2. Of those that a mesh axis runs over, the one named last changes fastest.
Arguments:
- window: float32 [8, 16, 69, 512], P('lvl', None, None, 'lon'), may hold values from -6 to 6
- anchor: float32 [16, 69, 512], P(None, None, 'lon'), may hold values from -6 to 6
- noise: float32 [8, 16, 69, 512], P('lvl', None, None, 'lon'), may hold values from -6 to 6
- conv_in: bfloat16 [3, 3, 192, 69], replicated, may hold values from -0.25 to 0.25
- conv_out: bfloat16 [3, 3, 69, 192], replicated, may hold values from -0.15625 to 0.15625
- time_shift: float32 [192], replicated, may hold values from -4 to 4
- plan: int32 [256], replicated, may hold values from 0 to 999, as said below
- start: int32 [1], replicated, may hold values from 0 to 247
Outputs:
- advanced: float32 [8, 16, 69, 512], P('lvl', None, None, 'lon')
Inputs may be any that keep to these rules, and one draw needn't show every extreme that they name: `plan`: strictly decreasing, first entry 999.
All inputs are finite; a program needn't handle non-finite values.
Results may differ from a plain program's by a relative error of at most 0.0003.
Values may be sent and summed in bfloat16 or wider, within the bound.
No kernel may reach another device: no remote copies, remote signals or barrier semaphores. Data moves between devices by JAX's collectives and lax.ppermute only.
A program may use at most 64 MiB of HBM per device.

v0:
```python
import jax
import jax.numpy as jnp
from jax import lax
from jax.sharding import PartitionSpec as P

SWEEPS = 2


def extended(block, sides, width):
    for axis, dim in sides:
        count = lax.axis_size(axis)
        forward = [(i, i + 1) for i in range(count - 1)]
        forward.append((count - 1, 0))
        backward = [(target, source) for source, target in forward]
        low = lax.ppermute(
            lax.slice_in_dim(block, block.shape[dim] - width, None, axis=dim), axis, forward
        )
        high = lax.ppermute(lax.slice_in_dim(block, 0, width, axis=dim), axis, backward)
        block = jnp.concatenate([low, block, high], axis=dim)
    return block


def convolve(padded, weight, width_out):
    rows = padded.shape[1] - 2
    total = jnp.zeros((padded.shape[0], rows, weight.shape[2], width_out), jnp.float32)
    for a in range(3):
        for b in range(3):
            piece = padded[:, a : a + rows, :, b : b + width_out]
            total = total + jnp.einsum(
                "oc,vlcn->vlon", weight[a, b], piece, preferred_element_type=jnp.float32
            )
    return total


def pad_rows(field):
    return jnp.pad(field, ((0, 0), (1, 1), (0, 0), (0, 0)))


def exclusive_sum(values):
    running = jnp.cumsum(values, axis=0)
    return jnp.concatenate([jnp.zeros_like(values[:1]), running[:-1]], axis=0)


def body(window, anchor, noise, conv_in, conv_out, time_shift, plan, start):
    levels_here = window.shape[0]
    width = window.shape[3]
    offset = start[0] + lax.axis_index("lvl") * levels_here
    times = lax.dynamic_slice(plan, (offset,), (levels_here + 1,)).astype(jnp.float32)
    t_now = times[:-1]
    beta = 0.1 + 19.9 * t_now / 1000.0
    step = (t_now - times[1:]) / 1000.0
    beta_col = beta[:, None, None, None]
    step_col = step[:, None, None, None]
    spread = jnp.sqrt(beta * step)[:, None, None, None] * noise
    shift = (t_now / 1000.0)[:, None, None, None] * time_shift[None, None, :, None]
    states = window
    inclusive = None
    for sweep in range(SWEEPS):
        rounded = states.astype(jnp.bfloat16)
        rimmed = extended(rounded, (("lon", 3),), 1)
        pre = convolve(pad_rows(rimmed), conv_in, width)
        hidden = jax.nn.silu(pre + shift).astype(jnp.bfloat16)
        hidden_wide = extended(hidden, (("lon", 3),), 1)
        score = convolve(pad_rows(hidden_wide), conv_out, width)
        increment = (0.5 * beta_col * states + beta_col * score) * step_col + spread
        earlier = exclusive_sum(
            lax.all_to_all(increment, "lvl", split_axis=1, concat_axis=0, tiled=True)
        )
        before = lax.all_to_all(earlier, "lvl", split_axis=0, concat_axis=1, tiled=True)
        inclusive = before + increment
        states = anchor[None] + before
    return anchor[None] + inclusive


def solution(mesh):
    return jax.shard_map(
        body,
        mesh=mesh,
        in_specs=(
            P("lvl", None, None, "lon"),
            P(None, None, "lon"),
            P("lvl", None, None, "lon"),
            P(),
            P(),
            P(),
            P(),
            P(),
        ),
        out_specs=P("lvl", None, None, "lon"),
        check_vma=False,
    )
```

profile of v0, /device:TPU:0, one launch (start us, length us, event | category | flops | bytes accessed | tf_op | source)
XLA Modules:
  0.0 134.5 jit_solution(6368105280167487864)
XLA Ops:
  0.0 1.3 copy.76
  2.0 2.0 %collective-permute-start.1 = (bf16[1,16,69,1]{3,2,1,0:T(8,128)(2,1)S(1)}, bf16[1,16,69,1]{3,2,1,0:T(8,128)(2,1)S(1)}, u32[]{:S(2)}, u32[]{:S(2)}) collective-permute-start(bf16[1,16,69,1]{3,2,1,0:T(8,128)(2,1)S(1)} %get-tuple-element.14), channel_id=1, source_target_pairs={{1,0},{2,1},{3,2},{0,3},{5,4},{6,5},{7,6},{4,7},{9,8},{10,9},{11,1... | collective-permute-start | bytes 6632 | tf_op jit(solution)/shard_map/ppermute | solution.py:18
  4.7 0.6 fusion.153
  6.4 2.4 %collective-permute-done = bf16[1,16,69,1]{3,2,1,0:T(8,128)(2,1)S(1)} collective-permute-done((bf16[1,16,69,1]{3,2,1,0:T(8,128)(2,1)S(1)}, bf16[1,16,69,1]{3,2,1,0:T(8,128)(2,1)S(1)}, u32[]{:S(2)}, u32[]{:S(2)}) %collective-permute-start) | collective-permute-done | bytes 2240 | tf_op jit(solution)/shard_map/ppermute | solution.py:15
  8.9 2.4 %collective-permute-done.1 = bf16[1,16,69,1]{3,2,1,0:T(8,128)(2,1)S(1)} collective-permute-done((bf16[1,16,69,1]{3,2,1,0:T(8,128)(2,1)S(1)}, bf16[1,16,69,1]{3,2,1,0:T(8,128)(2,1)S(1)}, u32[]{:S(2)}, u32[]{:S(2)}) %collective-permute-start.1) | collective-permute-done | bytes 2240 | tf_op jit(solution)/shard_map/ppermute | solution.py:18
  14.9 1.2 fusion.8
  17.2 2.3 %collective-permute-start.3 = (bf16[1,16,192,1]{2,1,3,0:T(8,128)(2,1)S(1)}, bf16[1,16,192,1]{2,1,3,0:T(8,128)(2,1)S(1)}, u32[]{:S(2)}, u32[]{:S(2)}) collective-permute-start(bf16[1,16,192,1]{2,1,3,0:T(8,128)(2,1)S(1)} %copy.43), channel_id=1, source_target_pairs={{1,0},{2,1},{3,2},{0,3},{5,4},{6,5},{7,6},{4,7},{9,8},{10,9},{11,1... | collective-permute-start | bytes 18440 | tf_op jit(solution)/shard_map/ppermute | solution.py:18
  22.5 0.9 select_maximum_fusion.2
  25.5 0.7 convolution_add_fusion.11
  27.4 0.6 fusion.17
  28.1 0.6 copy.49
  28.6 22.1 %all_to_all.48 = f32[1,16,69,128]{3,0,2,1:T(1,128)S(1)} all-to-all(f32[1,16,69,128]{3,0,2,1:T(1,128)S(1)} %copy.49), channel_id=1, replica_groups=mesh['lvl'=8,'lon'=4] {'lvl'}, dimensions={1} | all-to-all | bytes 1130496 | tf_op jit(solution)/shard_map/all_to_all | solution.py:67
  51.4 18.8 %all_to_all.49 = f32[8,2,69,128]{3,1,2,0:T(2,128)S(1)} all-to-all(f32[8,2,69,128]{3,1,2,0:T(2,128)S(1)} %concatenate.48.clone), channel_id=1, replica_groups=mesh['lvl'=8,'lon'=4] {'lvl'}, dimensions={0} | all-to-all | bytes 1130496 | tf_op jit(solution)/shard_map/all_to_all | solution.py:69
  70.7 1.7 %collective-permute-start.5 = (bf16[1,16,69,1]{3,2,1,0:T(8,128)(2,1)S(1)}, bf16[1,16,69,1]{3,2,1,0:T(8,128)(2,1)S(1)}, u32[]{:S(2)}, u32[]{:S(2)}) collective-permute-start(bf16[1,16,69,1]{3,2,1,0:T(8,128)(2,1)S(1)} %get-tuple-element.12), channel_id=1, source_target_pairs={{1,0},{2,1},{3,2},{0,3},{5,4},{6,5},{7,6},{4,7},{9,8},{10,9},{11,1... | collective-permute-start | bytes 6632 | tf_op jit(solution)/shard_map/ppermute | solution.py:18
  72.9 6.7 %collective-permute-done.4 = bf16[1,16,69,1]{3,2,1,0:T(8,128)(2,1)S(1)} collective-permute-done((bf16[1,16,69,1]{3,2,1,0:T(8,128)(2,1)S(1)}, bf16[1,16,69,1]{3,2,1,0:T(8,128)(2,1)S(1)}, u32[]{:S(2)}, u32[]{:S(2)}) %collective-permute-start.4) | collective-permute-done | bytes 2240 | tf_op jit(solution)/shard_map/ppermute | solution.py:15
  83.1 1.2 fusion.9
  85.7 1.5 %collective-permute-start.7 = (bf16[1,16,192,1]{2,1,3,0:T(8,128)(2,1)S(1)}, bf16[1,16,192,1]{2,1,3,0:T(8,128)(2,1)S(1)}, u32[]{:S(2)}, u32[]{:S(2)}) collective-permute-start(bf16[1,16,192,1]{2,1,3,0:T(8,128)(2,1)S(1)} %copy.55), channel_id=1, source_target_pairs={{1,0},{2,1},{3,2},{0,3},{5,4},{6,5},{7,6},{4,7},{9,8},{10,9},{11,1... | collective-permute-start | bytes 18440 | tf_op jit(solution)/shard_map/ppermute | solution.py:18
  87.2 0.9 collective-permute-done.6
  89.0 0.9 select_maximum_fusion
  92.0 0.7 convolution_add_fusion.3
  94.0 0.6 copy.60
  94.6 19.2 %all_to_all.50 = f32[1,16,69,128]{3,0,2,1:T(1,128)S(1)} all-to-all(f32[1,16,69,128]{3,0,2,1:T(1,128)S(1)} %copy.60), channel_id=1, replica_groups=mesh['lvl'=8,'lon'=4] {'lvl'}, dimensions={1} | all-to-all | bytes 1130496 | tf_op jit(solution)/shard_map/all_to_all | solution.py:67
  114.5 18.8 %all_to_all.51 = f32[8,2,69,128]{3,1,2,0:T(2,128)S(1)} all-to-all(f32[8,2,69,128]{3,1,2,0:T(2,128)S(1)} %concatenate.55.clone), channel_id=1, replica_groups=mesh['lvl'=8,'lon'=4] {'lvl'}, dimensions={0} | all-to-all | bytes 1130496 | tf_op jit(solution)/shard_map/all_to_all | solution.py:69
  133.6 0.9 copy.64
  (89 shorter events, 21.6 us)
Async XLA Ops:
  0.0 4.6 %copy-start.9 = (s32[256]{0:T(256)S(1)}, s32[256]{0:T(256)}, u32[]{:S(2)}) copy-start(s32[256]{0:T(256)} %param.14) | copy-start | bytes 3076
  0.0 5.3 %copy-start.6 = (bf16[3,3,192,69]{2,3,1,0:T(8,128)(2,1)S(1)}, bf16[3,3,192,69]{2,3,1,0:T(8,128)(2,1)}, u32[]{:S(2)}) copy-start(bf16[3,3,192,69]{2,3,1,0:T(8,128)(2,1)} %param.11) | copy-start | bytes 715396
  1.3 5.1 %copy-start.8 = (f32[192]{0:T(256)S(1)}, f32[192]{0:T(256)}, u32[]{:S(2)}) copy-start(f32[192]{0:T(256)} %param.13) | copy-start | bytes 2308
  1.5 7.4 %collective-permute-start = (bf16[1,16,69,1]{3,2,1,0:T(8,128)(2,1)S(1)}, bf16[1,16,69,1]{3,2,1,0:T(8,128)(2,1)S(1)}, u32[]{:S(2)}, u32[]{:S(2)}) collective-permute-start(bf16[1,16,69,1]{3,2,1,0:T(8,128)(2,1)S(1)} %get-tuple-element.13), channel_id=1, source_target_pairs={{0,1},{1,2},{2,3},{3,0},{4,5},{5,6},{6,7},{7,4},{8,9},{9,10},{10,1... | collective-permute-start | bytes 6632 | tf_op jit(solution)/shard_map/ppermute | solution.py:15
  2.0 9.3 %collective-permute-start.1 = (bf16[1,16,69,1]{3,2,1,0:T(8,128)(2,1)S(1)}, bf16[1,16,69,1]{3,2,1,0:T(8,128)(2,1)S(1)}, u32[]{:S(2)}, u32[]{:S(2)}) collective-permute-start(bf16[1,16,69,1]{3,2,1,0:T(8,128)(2,1)S(1)} %get-tuple-element.14), channel_id=1, source_target_pairs={{1,0},{2,1},{3,2},{0,3},{5,4},{6,5},{7,6},{4,7},{9,8},{10,9},{11,1... | collective-permute-start | bytes 6632 | tf_op jit(solution)/shard_map/ppermute | solution.py:18
  16.8 4.8 %collective-permute-start.2 = (bf16[1,16,192,1]{2,1,3,0:T(8,128)(2,1)S(1)}, bf16[1,16,192,1]{2,1,3,0:T(8,128)(2,1)S(1)}, u32[]{:S(2)}, u32[]{:S(2)}) collective-permute-start(bf16[1,16,192,1]{2,1,3,0:T(8,128)(2,1)S(1)} %copy.42), channel_id=1, source_target_pairs={{0,1},{1,2},{2,3},{3,0},{4,5},{5,6},{6,7},{7,4},{8,9},{9,10},{10,1... | collective-permute-start | bytes 18440 | tf_op jit(solution)/shard_map/ppermute | solution.py:15
  17.2 4.8 %collective-permute-start.3 = (bf16[1,16,192,1]{2,1,3,0:T(8,128)(2,1)S(1)}, bf16[1,16,192,1]{2,1,3,0:T(8,128)(2,1)S(1)}, u32[]{:S(2)}, u32[]{:S(2)}) collective-permute-start(bf16[1,16,192,1]{2,1,3,0:T(8,128)(2,1)S(1)} %copy.43), channel_id=1, source_target_pairs={{1,0},{2,1},{3,2},{0,3},{5,4},{6,5},{7,6},{4,7},{9,8},{10,9},{11,1... | collective-permute-start | bytes 18440 | tf_op jit(solution)/shard_map/ppermute | solution.py:18
  22.5 1.0 copy-start.4
  26.2 1.1 copy-start
  26.2 1.2 copy-start.1
  51.2 19.0 %copy-start.2 = (f32[16,69,128]{2,0,1:T(8,128)S(1)}, f32[16,69,128]{2,0,1:T(8,128)}, u32[]{:S(2)}) copy-start(f32[16,69,128]{2,0,1:T(8,128)} %param.9) | copy-start | bytes 1695748
  70.3 2.2 %copy-start.7 = (bf16[3,3,192,69]{2,3,1,0:T(8,128)(2,1)S(1)}, bf16[3,3,192,69]{2,3,1,0:T(8,128)(2,1)}, u32[]{:S(2)}) copy-start(bf16[3,3,192,69]{2,3,1,0:T(8,128)(2,1)} %param.11) | copy-start | bytes 715396
  70.7 8.9 %collective-permute-start.4 = (bf16[1,16,69,1]{3,2,1,0:T(8,128)(2,1)S(1)}, bf16[1,16,69,1]{3,2,1,0:T(8,128)(2,1)S(1)}, u32[]{:S(2)}, u32[]{:S(2)}) collective-permute-start(bf16[1,16,69,1]{3,2,1,0:T(8,128)(2,1)S(1)} %get-tuple-element.11), channel_id=1, source_target_pairs={{0,1},{1,2},{2,3},{3,0},{4,5},{5,6},{6,7},{7,4},{8,9},{9,10},{10,1... | collective-permute-start | bytes 6632 | tf_op jit(solution)/shard_map/ppermute | solution.py:15
  70.7 8.8 %collective-permute-start.5 = (bf16[1,16,69,1]{3,2,1,0:T(8,128)(2,1)S(1)}, bf16[1,16,69,1]{3,2,1,0:T(8,128)(2,1)S(1)}, u32[]{:S(2)}, u32[]{:S(2)}) collective-permute-start(bf16[1,16,69,1]{3,2,1,0:T(8,128)(2,1)S(1)} %get-tuple-element.12), channel_id=1, source_target_pairs={{1,0},{2,1},{3,2},{0,3},{5,4},{6,5},{7,6},{4,7},{9,8},{10,9},{11,1... | collective-permute-start | bytes 6632 | tf_op jit(solution)/shard_map/ppermute | solution.py:18
  85.0 3.1 %collective-permute-start.6 = (bf16[1,16,192,1]{2,1,3,0:T(8,128)(2,1)S(1)}, bf16[1,16,192,1]{2,1,3,0:T(8,128)(2,1)S(1)}, u32[]{:S(2)}, u32[]{:S(2)}) collective-permute-start(bf16[1,16,192,1]{2,1,3,0:T(8,128)(2,1)S(1)} %copy.54), channel_id=1, source_target_pairs={{0,1},{1,2},{2,3},{3,0},{4,5},{5,6},{6,7},{7,4},{8,9},{9,10},{10,1... | collective-permute-start | bytes 18440 | tf_op jit(solution)/shard_map/ppermute | solution.py:15
  85.7 2.8 %collective-permute-start.7 = (bf16[1,16,192,1]{2,1,3,0:T(8,128)(2,1)S(1)}, bf16[1,16,192,1]{2,1,3,0:T(8,128)(2,1)S(1)}, u32[]{:S(2)}, u32[]{:S(2)}) collective-permute-start(bf16[1,16,192,1]{2,1,3,0:T(8,128)(2,1)S(1)} %copy.55), channel_id=1, source_target_pairs={{1,0},{2,1},{3,2},{0,3},{5,4},{6,5},{7,6},{4,7},{9,8},{10,9},{11,1... | collective-permute-start | bytes 18440 | tf_op jit(solution)/shard_map/ppermute | solution.py:18
  89.0 1.0 copy-start.5
  114.3 19.0 %copy-start.3 = (f32[16,69,128]{2,0,1:T(8,128)S(1)}, f32[16,69,128]{2,0,1:T(8,128)}, u32[]{:S(2)}) copy-start(f32[16,69,128]{2,0,1:T(8,128)} %param.9) | copy-start | bytes 1695748
where the time goes:
time: 135 us
  blocking collectives  78.9 us (58%)
  matrix products  17.5 us (13%)
  waiting for transfers between devices  12.5 us (9%)
  local copies, waits for them, and re-layouts  9.75 us (7%)
  starting transfers between devices  8.49 us (6%)
  between operations  3.93 us (3%)
  other arithmetic  3.51 us (3%)
    all_to_all x2, blocking collectives, body(): lax.all_to_all(increment, 'lvl', split_axis=1, concat_axis=0, tiled=True)  41.3 us
    all_to_all x2, blocking collectives, body(): lax.all_to_all(earlier, 'lvl', split_axis=0, concat_axis=1, tiled=True)  37.6 us
    dot_general x36, matrix products, convolve(): jnp.einsum('oc,vlcn->vlon', weight[a, b], piece, preferred_element_type=j...  17.5 us
    ppermute x4, waiting for transfers between devices, extended(): lax.ppermute(lax.slice_in_dim(block, block.shape[dim] - width, None, axis...  10 us
    ppermute x4, starting transfers between devices, extended(): lax.ppermute(lax.slice_in_dim(block, 0, width, axis=dim), axis, backward)  7.5 us
  transfers between devices with their start and end apart: 8, of which 4 were waited for; matrix products, arithmetic and copies ran while one was open for 2% of the time, Pallas kernels for 0%

commit v1 on v0

v1 whole, which is shorter than its diff:
```python
import functools

import jax
import jax.numpy as jnp
from jax import lax
from jax.experimental import pallas as pl
from jax.experimental.pallas import tpu as pltpu
from jax.sharding import PartitionSpec as P

GROUP = 4
EDGE = 4
ROWS = 8
PACK = 16

VM = pl.BlockSpec(memory_space=pltpu.VMEM)
SM = pl.BlockSpec(memory_space=pltpu.SMEM)
F32 = jnp.float32
BF16 = jnp.bfloat16


def up_to(value, unit):
    return -(-value // unit) * unit


def call(kernel, outs, specs, scratch, flops):
    return pl.pallas_call(
        kernel,
        out_shape=[jax.ShapeDtypeStruct(shape, F32) for shape in outs],
        in_specs=specs,
        out_specs=[VM] * len(outs),
        scratch_shapes=scratch,
        cost_estimate=pl.CostEstimate(flops=flops, bytes_accessed=4 << 20, transcendentals=0),
    )


def edges_kernel(lat, win_ref, noise_ref, anchor_ref, first_ref, last_ref):
    chans = win_ref.shape[0] // lat
    width = win_ref.shape[1]
    firsts = []
    lasts = []
    for l in range(lat):
        rows = pl.ds(l, chans, stride=lat)
        win = win_ref[rows, :]
        noise = noise_ref[rows, :]
        anchor = anchor_ref[rows, :]
        firsts += [win[:, :4], noise[:, :2], anchor[:, :2]]
        lasts += [win[:, width - 4 :], noise[:, width - 2 :], anchor[:, width - 2 :]]
    first_ref[0:chans, :] = jnp.concatenate(firsts, axis=1)
    last_ref[0:chans, :] = jnp.concatenate(lasts, axis=1)


def lat_shifted(x, strip, pitch):
    size = x.shape[1]
    lane = lax.rem(lax.broadcasted_iota(jnp.int32, x.shape, 1), strip)
    below = jnp.where(lane < pitch, 0.0, pltpu.roll(x, pitch, 1))
    above = jnp.where(lane >= strip - pitch, 0.0, pltpu.roll(x, size - pitch, 1))
    return below, above


def score_of(x, shift, w_in_ref, w_out_ref, strip, pitch):
    size = x.shape[1]
    hid = w_in_ref.shape[0] // 3
    rows = w_out_ref.shape[0] // 9
    below, above = lat_shifted(x, strip, pitch)
    stacked = jnp.concatenate([below, x, above], axis=0).astype(BF16)
    taps = jnp.dot(w_in_ref[...], stacked, preferred_element_type=F32)
    pre = taps[hid : 2 * hid] + pltpu.roll(taps[:hid], 1, 1) + pltpu.roll(taps[2 * hid :], size - 1, 1)
    value = pre + shift
    hidden = (value / (1.0 + jnp.exp(-value))).astype(BF16)
    out = jnp.dot(w_out_ref[...], hidden, preferred_element_type=F32)
    lines = []
    for a in range(3):
        left = out[(3 * a) * rows : (3 * a + 1) * rows]
        mid = out[(3 * a + 1) * rows : (3 * a + 2) * rows]
        right = out[(3 * a + 2) * rows : (3 * a + 3) * rows]
        lines.append(mid + pltpu.roll(left, 1, 1) + pltpu.roll(right, size - 1, 1))
    below, _ = lat_shifted(lines[0], strip, pitch)
    _, above = lat_shifted(lines[2], strip, pitch)
    return lines[1] + below + above


def first_kernel(
    lat, me_ref, coef_ref, win_ref, noise_ref, before_ref, after_ref, shift_ref, w_in_ref, w_out_ref,
    *refs,
):
    outs = refs[:GROUP]
    waves = refs[GROUP : 2 * GROUP]
    x_ref, u_ref, inc_ref, wave_ref = refs[2 * GROUP :]
    chans = win_ref.shape[0] // lat
    width = win_ref.shape[1]
    sub = width // GROUP
    pitch = sub + 2 * EDGE
    strip = lat * pitch
    me = me_ref[0]
    half, drift, spread = coef_ref[0], coef_ref[1], coef_ref[2]
    x_ref[...] = jnp.zeros_like(x_ref)
    u_ref[...] = jnp.zeros_like(u_ref)
    blank = jnp.zeros((chans, 2), F32)
    for l in range(lat):
        rows = pl.ds(l, chans, stride=lat)
        win = win_ref[rows, :]
        noise = noise_ref[rows, :] * spread
        low = before_ref[0:chans, 8 * l : 8 * l + 8]
        high = after_ref[0:chans, 8 * l : 8 * l + 8]
        wide = jnp.concatenate([low[:, :4], win, high[:, :4]], axis=1)
        other = jnp.concatenate([blank, low[:, 4:6] * spread, noise, high[:, 4:6] * spread, blank], axis=1)
        total = wide * half + other
        for q in range(GROUP):
            lanes = slice(q * strip + l * pitch, q * strip + (l + 1) * pitch)
            x_ref[0:chans, lanes] = wide[:, q * sub : q * sub + pitch]
            u_ref[0:chans, lanes] = total[:, q * sub : q * sub + pitch]
            wave_ref[q, 0:chans, l * sub : (l + 1) * sub] = noise[:, q * sub : (q + 1) * sub]
    shift = shift_ref[...] * coef_ref[3]
    rows = u_ref.shape[0]
    step = 2 * strip
    for part in range(GROUP // 2):
        lanes = slice(part * step, (part + 1) * step)
        score = score_of(x_ref[:, lanes], shift, w_in_ref, w_out_ref, strip, pitch)
        inc = u_ref[:, lanes] + drift * score
        for i in range(2):
            inc_ref[2 * part + i] = inc[:, i * strip : (i + 1) * strip]
    for m in range(GROUP):
        outs[m][...] = inc_ref[lax.bitwise_xor(me, m)]
        waves[m][...] = wave_ref[lax.bitwise_xor(me, m)]


def second_kernel(
    lat, me_ref, coef_ref, anchor_ref, before_ref, after_ref, shift_ref, w_in_ref, w_out_ref, carry_ref,
    *refs,
):
    incs = refs[:GROUP]
    waves = refs[GROUP : 2 * GROUP]
    outs = refs[2 * GROUP : 3 * GROUP]
    total_ref, anc_ref, x_ref, inc_ref, wave_ref, part_ref = refs[3 * GROUP :]
    chans = anchor_ref.shape[0] // lat
    width = anchor_ref.shape[1]
    sub = width // GROUP
    pitch = sub + 2 * EDGE
    strip = lat * pitch
    me = me_ref[0]
    rows = carry_ref.shape[0]
    anc_ref[...] = jnp.zeros_like(anc_ref)
    x_ref[...] = jnp.zeros_like(x_ref)
    for l in range(lat):
        anchor = pltpu.roll(
            jnp.concatenate([anchor_ref[pl.ds(l, chans, stride=lat), :]], axis=1), lax.rem(width - me * sub, width), 1
        )
        low = jnp.where(me == 0, before_ref[0:chans, 8 * l + 6 : 8 * l + 8], anchor[:, width - 2 :])
        high = jnp.where(me == GROUP - 1, after_ref[0:chans, 8 * l + 6 : 8 * l + 8], anchor[:, sub : sub + 2])
        piece = jnp.concatenate([low, anchor[:, :sub], high], axis=1)
        anc_ref[0:chans, l * pitch + 2 : (l + 1) * pitch - 2] = piece
    for m in range(GROUP):
        inc_ref[lax.bitwise_xor(me, m)] = incs[m][...]
        wave_ref[lax.bitwise_xor(me, m)] = waves[m][...]
    state = anc_ref[...] + carry_ref[...]
    for j in range(GROUP):
        x_ref[0:rows, j * strip : (j + 1) * strip] = state
        if j + 1 < GROUP:
            state = state + inc_ref[j]
    step = 2 * strip
    for part in range(GROUP // 2):
        lanes = slice(part * step, (part + 1) * step)
        base = coef_ref.shape[0] // GROUP
        shift = jnp.concatenate(
            [
                jnp.broadcast_to(shift_ref[...] * coef_ref[(2 * part + i) * base + 3], (shift_ref.shape[0], strip))
                for i in range(2)
            ],
            axis=1,
        )
        x = x_ref[:, lanes]
        score = score_of(x, shift, w_in_ref, w_out_ref, strip, pitch)
        for i in range(2):
            level = 2 * part + i
            mine = slice(i * strip, (i + 1) * strip)
            part_ref[level] = x[0:rows, mine] * coef_ref[level * base] + score[:, mine] * coef_ref[level * base + 1]
    def compact(block):
        return jnp.concatenate([block[:, l * pitch + EDGE : l * pitch + EDGE + sub] for l in range(lat)], axis=1)

    start = compact(anc_ref[...])
    running = jnp.zeros_like(start)
    for j in range(GROUP):
        running = running + (compact(part_ref[j]) + wave_ref[j])
        wave_ref[j] = start + running
    total_ref[...] = running
    for m in range(GROUP):
        outs[m][...] = wave_ref[lax.bitwise_xor(me, m)]


def last_kernel(lat, me_ref, *refs):
    parts = refs[:GROUP]
    out_ref, all_ref = refs[GROUP:]
    chans = out_ref.shape[0] // lat
    sub = out_ref.shape[1] // GROUP
    me = me_ref[0]
    for m in range(GROUP):
        all_ref[lax.bitwise_xor(me, m)] = parts[m][...]
    for l in range(lat):
        line = jnp.concatenate([all_ref[q, 0:chans, l * sub : (l + 1) * sub] for q in range(GROUP)], axis=1)
        out_ref[pl.ds(l, chans, stride=lat), :] = line


def exchange(pieces):
    count = lax.axis_size("lvl")
    got = [pieces[0]]
    for m in range(1, GROUP):
        got.append(lax.ppermute(pieces[m], "lvl", [(k, k ^ m) for k in range(count)]))
    return got


def carried(total, block):
    count = lax.axis_size("lvl")
    blocks = count // GROUP
    carry = jnp.zeros_like(total)
    for s in range(1, blocks):
        moved = lax.ppermute(total, "lvl", [(k, (k + s * GROUP) % count) for k in range(count)])
        carry = carry + jnp.where(block >= s, moved, 0.0)
    return carry


def body(window, anchor, noise, conv_in, conv_out, time_shift, plan, start):
    _, lat, chans, width = window.shape
    hid = conv_in.shape[2]
    level = lax.axis_index("lvl")
    me = lax.rem(level, GROUP)
    block = level // GROUP
    sub = width // GROUP
    pitch = sub + 2 * EDGE
    strip = lat * pitch
    rows = up_to(chans, ROWS)
    deep = up_to(chans, PACK)

    offset = start[0] + block * GROUP
    times = lax.dynamic_slice(plan, (offset,), (GROUP + 1,)).astype(F32)
    t_now = times[:-1]
    beta = 0.1 + 19.9 * t_now / 1000.0
    step = (t_now - times[1:]) / 1000.0
    coefs = jnp.stack([0.5 * beta * step, beta * step, jnp.sqrt(beta * step), t_now / 1000.0], axis=1)
    mine = lax.dynamic_slice(coefs, (me, 0), (1, 4)).reshape(-1)
    coefs = coefs.reshape(-1)
    me_arr = me.astype(jnp.int32).reshape(1)

    def native(x):
        return jnp.transpose(x.reshape(lat, chans, width), (1, 0, 2)).reshape(chans * lat, width)

    win = native(window)
    noi = native(noise)
    anc = native(anchor)
    w_in = jnp.pad(jnp.transpose(conv_in, (1, 2, 0, 3)), ((0, 0), (0, 0), (0, 0), (0, deep - chans)))
    w_in = w_in.reshape(3 * hid, 3 * deep)
    w_out = jnp.pad(conv_out, ((0, 0), (0, 0), (0, rows - chans), (0, 0))).reshape(9 * rows, hid)
    column = time_shift.reshape(hid, 1)

    edge = (rows, 8 * lat)
    first, last = call(functools.partial(edges_kernel, lat), [edge, edge], [VM] * 3, [], 1 << 20)(win, noi, anc)
    count = lax.axis_size("lon")
    before = lax.ppermute(last, "lon", [(k, (k + 1) % count) for k in range(count)])
    after = lax.ppermute(first, "lon", [((k + 1) % count, k) for k in range(count)])

    wide = (rows, strip)
    tight = (rows, lat * sub)
    flops = 2 * 9 * chans * hid * 2 * lat * width
    made = call(
        functools.partial(first_kernel, lat),
        [wide] * GROUP + [tight] * GROUP,
        [SM, SM] + [VM] * 7,
        [
            pltpu.VMEM((deep, GROUP * strip), F32),
            pltpu.VMEM((rows, GROUP * strip), F32),
            pltpu.VMEM((GROUP,) + wide, F32),
            pltpu.VMEM((GROUP,) + tight, F32),
        ],
        flops,
    )(me_arr, mine, win, noi, before, after, column, w_in, w_out)
    incs = exchange(made[:GROUP])
    total = incs[0] + incs[1] + incs[2] + incs[3]
    carry = carried(total, block)
    waves = exchange(made[GROUP:])
    done = call(
        functools.partial(second_kernel, lat),
        [tight] * (GROUP + 1),
        [SM, SM] + [VM] * (7 + 2 * GROUP),
        [
            pltpu.VMEM(wide, F32),
            pltpu.VMEM((deep, GROUP * strip), F32),
            pltpu.VMEM((GROUP,) + wide, F32),
            pltpu.VMEM((GROUP,) + tight, F32),
            pltpu.VMEM((GROUP,) + wide, F32),
        ],
        flops,
    )(me_arr, coefs, anc, before, after, column, w_in, w_out, carry, *incs, *waves)
    carry = carried(done[GROUP], block)
    parts = exchange([part + carry for part in done[:GROUP]])
    (out,) = call(
        functools.partial(last_kernel, lat),
        [(chans * lat, width)],
        [SM] + [VM] * GROUP,
        [pltpu.VMEM((GROUP,) + tight, F32)],
        1 << 20,
    )(me_arr, *parts)
    return jnp.transpose(out.reshape(chans, lat, width), (1, 0, 2))[None]


def solution(mesh):
    return jax.shard_map(
        body,
        mesh=mesh,
        in_specs=(
            P("lvl", None, None, "lon"),
            P(None, None, "lon"),
            P("lvl", None, None, "lon"),
            P(),
            P(),
            P(),
            P(),
            P(),
        ),
        out_specs=P("lvl", None, None, "lon"),
        check_vma=False,
    )
```

time: 135 us -> 86.8 us (0.64)
  blocking collectives: 78.9 us -> 0 us
  Pallas kernels: 0 us -> 28.6 us
  matrix products: 17.5 us -> 0 us
  waiting for transfers between devices: 12.5 us -> 28.2 us
  starting transfers between devices: 8.49 us -> 16.6 us
  between operations: 3.93 us -> 0.76 us
    all_to_all x4 -> x0, blocking collectives: 78.9 us -> none  [the longest x2 41.3 us: body(): lax.all_to_all(increment, 'lvl', split_axis=1, concat_axis=0, tiled=True)]
    pallas_call x0 -> x4, Pallas kernels: none -> 28.6 us  [the longest x1 11.7 us: body(): call(functools.partial(second_kernel, lat), [tight] * (GROUP + 1), [SM, S...]
    dot_general x36 -> x0, matrix products: 17.5 us -> none  [convolve(): jnp.einsum('oc,vlcn->vlon', weight[a, b], piece, preferred_element_type=j...]
    ppermute x8 -> x13, waiting for transfers between devices: 12.5 us -> 28.2 us  [the longest x9 16.8 us: exchange(): lax.ppermute(pieces[m], 'lvl', [(k, k ^ m) for k in range(count)])]
    ppermute x8 -> x13, starting transfers between devices: 8.49 us -> 16.6 us  [the longest x9 11 us: exchange(): lax.ppermute(pieces[m], 'lvl', [(k, k ^ m) for k in range(count)])]
    slice x11 -> x0, local copies, waits for them, and re-layouts: 3.19 us -> none  [the longest x6 1.71 us: extended(): lax.slice_in_dim(block, block.shape[dim] - width, None, axis=dim)]
    add x1 -> x2, other arithmetic: 0.25 us -> 2.93 us  [the longest x1 1.84 us: body(): parts = exchange([part + carry for part in done[:GROUP]])]
    concatenate x4 -> x0, other arithmetic: 2.58 us -> none  [extended(): block = jnp.concatenate([low, block, high], axis=dim)]
  transfers between devices with their start and end apart: 8 -> 13, of which waited for: 4 -> 9; matrix products, arithmetic and copies ran while one was open for 2% -> 6% of each run, Pallas kernels for 0% -> 0%
where the time goes in v1:
time: 86.8 us; the launch traced here: 86.5 us
  Pallas kernels  28.6 us (33%)
  waiting for transfers between devices  28.2 us (32%)
  starting transfers between devices  16.6 us (19%)
  local copies, waits for them, and re-layouts  8.59 us (10%)
  other arithmetic  3.79 us (4%)
    ppermute x9, waiting for transfers between devices, exchange(): lax.ppermute(pieces[m], 'lvl', [(k, k ^ m) for k in range(count)])  16.8 us
    pallas_call x1, Pallas kernels, body(): call(functools.partial(second_kernel, lat), [tight] * (GROUP + 1), [SM, S...  11.7 us
    ppermute x2, waiting for transfers between devices, carried(): lax.ppermute(total, 'lvl', [(k, (k + s * GROUP) % count) for k in range(c...  11.4 us
    ppermute x9, starting transfers between devices, exchange(): lax.ppermute(pieces[m], 'lvl', [(k, k ^ m) for k in range(count)])  11 us
    pallas_call x1, Pallas kernels, body(): call(functools.partial(first_kernel, lat), [wide] * GROUP + [tight] * GRO...  10.9 us
    unnamed x37, local copies, waits for them, and re-layouts  4.3 us
    pallas_call x1, Pallas kernels, body(): call(functools.partial(edges_kernel, lat), [edge, edge], [VM] * 3, [], 1...  3.44 us
    ppermute x2, starting transfers between devices, carried(): lax.ppermute(total, 'lvl', [(k, (k + s * GROUP) % count) for k in range(c...  3.2 us
  transfers between devices with their start and end apart: 13, of which 9 were waited for; matrix products, arithmetic and copies ran while one was open for 6% of the time, Pallas kernels for 0%

profile of v1, /device:TPU:0, one launch (start us, length us, event | category | flops | bytes accessed | tf_op | source)
XLA Modules:
  0.0 86.5 jit_solution(18073253812461495818)
XLA Ops:
  0.0 3.4 %shard_map.82 = (f32[72,128]{1,0:T(8,128)}, f32[72,128]{1,0:T(8,128)}) custom-call(f32[1104,128]{1,0:T(8,128)} %bitcast.31, f32[1104,128]{1,0:T(8,128)} %bitcast.33, f32[1104,128]{1,0:T(8,128)} %bitcast.35), custom_call_target="tpu_custom_call" | custom-call | flops 1048576 | bytes 4194304 | tf_op jit(solution)/shard_map/pallas_call | solution.py:255
  3.9 1.9 %collective-permute-start.1 = (f32[72,128]{1,0:T(8,128)}, f32[72,128]{1,0:T(8,128)S(1)}, u32[]{:S(2)}, u32[]{:S(2)}) collective-permute-start(f32[72,128]{1,0:T(8,128)} %get-tuple-element.21), channel_id=1, source_target_pairs={{1,0},{2,1},{3,2},{0,3},{5,4},{6,5},{7,6},{4,7},{9,8},{10,9},{11,1... | collective-permute-start | bytes 110600 | tf_op jit(solution)/shard_map/ppermute | solution.py:258
  9.8 0.8 pad.9
  10.9 1.0 %reshape.48.w_in_ref = bf16[576,240]{1,0:T(8,128)(2,1)} reshape(bf16[3,192,3,80]{3,2,1,0:T(4,128)(2,1)S(1)} %pad.8.clone) | data formatting | bytes 552960 | tf_op jit(solution)/shard_map/reshape | solution.py:250
  13.2 10.9 %shard_map.83 = (f32[72,640]{1,0:T(8,128)}, f32[72,640]{1,0:T(8,128)}, f32[72,640]{1,0:T(8,128)}, f32[72,640]{1,0:T(8,128)}, f32[72,512]{1,0:T(8,128)}, /*index=...) custom-call(s32[1]{0:T(128)} %bitcast.me_ref, f32[4]{0:T(128)} %dynamic-slice_reduce_fusion.coef_ref, ...), custom_call_target="tpu_custom_call" | custom-call | flops 976748544 | bytes 4194304 | tf_op jit(solution)/shard_map/pallas_call | solution.py:263
  24.1 2.4 %collective-permute-start.2 = (f32[72,640]{1,0:T(8,128)}, f32[72,640]{1,0:T(8,128)S(1)}, u32[]{:S(2)}, u32[]{:S(2)}) collective-permute-start(f32[72,640]{1,0:T(8,128)} %get-tuple-element.23), channel_id=1, source_target_pairs={{0,4},{4,0},{8,12},{12,8},{16,20},{20,16},{24,28},{28,24},{1,5},{5... | collective-permute-start | bytes 552968 | tf_op jit(solution)/shard_map/ppermute | solution.py:207
  26.5 1.6 %collective-permute-start.3 = (f32[72,640]{1,0:T(8,128)}, f32[72,640]{1,0:T(8,128)S(1)}, u32[]{:S(2)}, u32[]{:S(2)}) collective-permute-start(f32[72,640]{1,0:T(8,128)} %get-tuple-element.24), channel_id=1, source_target_pairs={{0,8},{4,12},{8,0},{12,4},{16,24},{20,28},{24,16},{28,20},{1,9},{5... | collective-permute-start | bytes 552968 | tf_op jit(solution)/shard_map/ppermute | solution.py:207
  28.1 3.5 %collective-permute-done.2.refs_1_ = f32[72,640]{1,0:T(8,128)S(1)} collective-permute-done((f32[72,640]{1,0:T(8,128)}, f32[72,640]{1,0:T(8,128)S(1)}, u32[]{:S(2)}, u32[]{:S(2)}) %collective-permute-start.2) | collective-permute-done | bytes 184352 | tf_op jit(solution)/shard_map/ppermute | solution.py:207
  31.6 2.6 %collective-permute-done.3.refs_2_ = f32[72,640]{1,0:T(8,128)S(1)} collective-permute-done((f32[72,640]{1,0:T(8,128)}, f32[72,640]{1,0:T(8,128)S(1)}, u32[]{:S(2)}, u32[]{:S(2)}) %collective-permute-start.3) | collective-permute-done | bytes 184352 | tf_op jit(solution)/shard_map/ppermute | solution.py:207
  34.3 2.5 %collective-permute-done.4.refs_3_ = f32[72,640]{1,0:T(8,128)S(1)} collective-permute-done((f32[72,640]{1,0:T(8,128)}, f32[72,640]{1,0:T(8,128)S(1)}, u32[]{:S(2)}, u32[]{:S(2)}) %collective-permute-start.4) | collective-permute-done | bytes 184352 | tf_op jit(solution)/shard_map/ppermute | solution.py:207
  36.8 1.1 %add_add_fusion = f32[72,640]{1,0:T(8,128)S(1)} fusion(f32[72,640]{1,0:T(8,128)S(1)} %collective-permute-done.4.refs_3_, f32[72,640]{1,0:T(8,128)S(1)} %collective-permute-done.3.refs_2_, f32[72,640]{1,0:T(8,128)} %get-tuple-element.22.refs_0_, f32[72,640]{1,0:T(8,128)S(1)} %collective-permute-done.2.refs_1_), kind=kLoop, calls=%fused_computation | loop fusion | flops 138240 | bytes 921600 | tf_op jit(solution)/shard_map/add | solution.py:276
  37.9 2.7 %collective-permute-start.5 = (f32[72,640]{1,0:T(8,128)S(1)}, f32[72,640]{1,0:T(8,128)S(1)}, u32[]{:S(2)}, u32[]{:S(2)}) collective-permute-start(f32[72,640]{1,0:T(8,128)S(1)} %add_add_fusion), channel_id=1, source_target_pairs={{0,16},{4,20},{8,24},{12,28},{16,0},{20,4},{24,8},{28,12},{1,17},{... | collective-permute-start | bytes 552968 | tf_op jit(solution)/shard_map/ppermute | solution.py:216
  41.2 1.5 %collective-permute-start.6 = (f32[72,512]{1,0:T(8,128)S(1)}, f32[72,512]{1,0:T(8,128)S(1)}, u32[]{:S(2)}, u32[]{:S(2)}) collective-permute-start(f32[72,512]{1,0:T(8,128)S(1)} %copy-done.11), channel_id=1, source_target_pairs={{0,4},{4,0},{8,12},{12,8},{16,20},{20,16},{24,28},{28,24},{1,5},{5... | collective-permute-start | bytes 442376 | tf_op jit(solution)/shard_map/ppermute | solution.py:207
  42.8 1.6 %collective-permute-start.7 = (f32[72,512]{1,0:T(8,128)S(1)}, f32[72,512]{1,0:T(8,128)S(1)}, u32[]{:S(2)}, u32[]{:S(2)}) collective-permute-start(f32[72,512]{1,0:T(8,128)S(1)} %copy-done.10), channel_id=1, source_target_pairs={{0,8},{4,12},{8,0},{12,4},{16,24},{20,28},{24,16},{28,20},{1,9},{5... | collective-permute-start | bytes 442376 | tf_op jit(solution)/shard_map/ppermute | solution.py:207
  44.7 3.9 %collective-permute-done.5 = f32[72,640]{1,0:T(8,128)S(1)} collective-permute-done((f32[72,640]{1,0:T(8,128)S(1)}, f32[72,640]{1,0:T(8,128)S(1)}, u32[]{:S(2)}, u32[]{:S(2)}) %collective-permute-start.5) | collective-permute-done | bytes 184352 | tf_op jit(solution)/shard_map/ppermute | solution.py:216
  49.3 1.8 %collective-permute-done.7.refs_6_ = f32[72,512]{1,0:T(8,128)S(1)} collective-permute-done((f32[72,512]{1,0:T(8,128)S(1)}, f32[72,512]{1,0:T(8,128)S(1)}, u32[]{:S(2)}, u32[]{:S(2)}) %collective-permute-start.7) | collective-permute-done | bytes 147488 | tf_op jit(solution)/shard_map/ppermute | solution.py:207
  51.1 1.4 %collective-permute-done.8.refs_7_ = f32[72,512]{1,0:T(8,128)S(1)} collective-permute-done((f32[72,512]{1,0:T(8,128)S(1)}, f32[72,512]{1,0:T(8,128)S(1)}, u32[]{:S(2)}, u32[]{:S(2)}) %collective-permute-start.8) | collective-permute-done | bytes 147488 | tf_op jit(solution)/shard_map/ppermute | solution.py:207
  53.2 11.7 %shard_map.84 = (f32[72,512]{1,0:T(8,128)}, f32[72,512]{1,0:T(8,128)}, f32[72,512]{1,0:T(8,128)}, f32[72,512]{1,0:T(8,128)}, f32[72,512]{1,0:T(8,128)}) custom-call(s32[1]{0:T(128)} %bitcast.me_ref, f32[16]{0:T(128)} %reshape.37.coef_ref, f32[1104,128]{1,0:T(8,128)} %bitcast.36, f32[72,128]{1,0:T(8,128)} %copy-done.15, f32[72,128]{1,0:T(8,128)} %copy-done.16, ...), custom_call_target="tpu_custom_call" | custom-call | flops 976748544 | bytes 4194304 | tf_op jit(solution)/shard_map/pallas_call | solution.py:279
  65.4 7.5 %collective-permute-done.9 = f32[72,512]{1,0:T(8,128)S(1)} collective-permute-done((f32[72,512]{1,0:T(8,128)}, f32[72,512]{1,0:T(8,128)S(1)}, u32[]{:S(2)}, u32[]{:S(2)}) %collective-permute-start.9) | collective-permute-done | bytes 147488 | tf_op jit(solution)/shard_map/ppermute | solution.py:216
  73.0 1.8 %select_add_fusion = (f32[72,512]{1,0:T(8,128)S(1)}, f32[72,512]{1,0:T(8,128)S(1)}, f32[72,512]{1,0:T(8,128)S(1)}, f32[72,512]{1,0:T(8,128)}) fusion(f32[72,512]{1,0:T(8,128)} %get-tuple-element.34, f32[72,512]{1,0:T(8,128)S(1)} %collective-permute-done.9, pred[]{:T(512)S(6)} %ge.4, f32[72,512]{1,0:T(8,128)} %get-tuple-element.32, ...), kind=kLoop, calls=%fused_computation.1 | loop fusion | flops 184320 | bytes 1327105 | tf_op jit(solution)/shard_map/add | solution.py:293
  75.7 2.6 %collective-permute-start.11 = (f32[72,512]{1,0:T(8,128)S(1)}, f32[72,512]{1,0:T(8,128)S(1)}, u32[]{:S(2)}, u32[]{:S(2)}) collective-permute-start(f32[72,512]{1,0:T(8,128)S(1)} %get-tuple-element.39), channel_id=1, source_target_pairs={{0,8},{4,12},{8,0},{12,4},{16,24},{20,28},{24,16},{28,20},{1,9},{5... | collective-permute-start | bytes 442376 | tf_op jit(solution)/shard_map/ppermute | solution.py:207
  78.3 3.6 %collective-permute-done.12.refs_3_ = f32[72,512]{1,0:T(8,128)S(1)} collective-permute-done((f32[72,512]{1,0:T(8,128)S(1)}, f32[72,512]{1,0:T(8,128)S(1)}, u32[]{:S(2)}, u32[]{:S(2)}) %collective-permute-start.12) | collective-permute-done | bytes 147488 | tf_op jit(solution)/shard_map/ppermute | solution.py:207
  81.9 1.2 %collective-permute-done.10.refs_1_ = f32[72,512]{1,0:T(8,128)S(1)} collective-permute-done((f32[72,512]{1,0:T(8,128)S(1)}, f32[72,512]{1,0:T(8,128)S(1)}, u32[]{:S(2)}, u32[]{:S(2)}) %collective-permute-start.10) | collective-permute-done | bytes 147488 | tf_op jit(solution)/shard_map/ppermute | solution.py:207
  83.9 2.6 %shard_map.85 = f32[1104,128]{1,0:T(8,128)} custom-call(s32[1]{0:T(128)} %bitcast.me_ref, f32[72,512]{1,0:T(8,128)} %get-tuple-element.40.refs_0_, f32[72,512]{1,0:T(8,128)} %copy-done.6, f32[72,512]{1,0:T(8,128)} %copy-done.7, f32[72,512]{1,0:T(8,128)} %copy-done.5), custom_call_target="tpu_custom_call" | custom-call | flops 1048576 | bytes 4194304 | tf_op jit(solution)/shard_map/pallas_call | solution.py:294
  (56 shorter events, 10.0 us)
Async XLA Ops:
  0.0 8.8 %copy-start = (bf16[3,3,192,69]{2,3,1,0:T(8,128)(2,1)S(1)}, bf16[3,3,192,69]{2,3,1,0:T(8,128)(2,1)}, u32[]{:S(2)}) copy-start(bf16[3,3,192,69]{2,3,1,0:T(8,128)(2,1)} %param.11) | copy-start | bytes 715396
  3.4 9.2 %collective-permute-start = (f32[72,128]{1,0:T(8,128)}, f32[72,128]{1,0:T(8,128)S(1)}, u32[]{:S(2)}, u32[]{:S(2)}) collective-permute-start(f32[72,128]{1,0:T(8,128)} %get-tuple-element.20), channel_id=1, source_target_pairs={{0,1},{1,2},{2,3},{3,0},{4,5},{5,6},{6,7},{7,4},{8,9},{9,10},{10,1... | collective-permute-start | bytes 110600 | tf_op jit(solution)/shard_map/ppermute | solution.py:257
  3.9 8.7 %collective-permute-start.1 = (f32[72,128]{1,0:T(8,128)}, f32[72,128]{1,0:T(8,128)S(1)}, u32[]{:S(2)}, u32[]{:S(2)}) collective-permute-start(f32[72,128]{1,0:T(8,128)} %get-tuple-element.21), channel_id=1, source_target_pairs={{1,0},{2,1},{3,2},{0,3},{5,4},{6,5},{7,6},{4,7},{9,8},{10,9},{11,1... | collective-permute-start | bytes 110600 | tf_op jit(solution)/shard_map/ppermute | solution.py:258
  8.8 1.0 %copy-start.1 = (bf16[3,3,69,192]{3,2,1,0:T(8,128)(2,1)S(1)}, bf16[3,3,69,192]{3,2,1,0:T(8,128)(2,1)}, u32[]{:S(2)}) copy-start(bf16[3,3,69,192]{3,2,1,0:T(8,128)(2,1)} %param.12) | copy-start | bytes 715396
  24.1 7.5 %collective-permute-start.2 = (f32[72,640]{1,0:T(8,128)}, f32[72,640]{1,0:T(8,128)S(1)}, u32[]{:S(2)}, u32[]{:S(2)}) collective-permute-start(f32[72,640]{1,0:T(8,128)} %get-tuple-element.23), channel_id=1, source_target_pairs={{0,4},{4,0},{8,12},{12,8},{16,20},{20,16},{24,28},{28,24},{1,5},{5... | collective-permute-start | bytes 552968 | tf_op jit(solution)/shard_map/ppermute | solution.py:207
  26.5 7.7 %collective-permute-start.3 = (f32[72,640]{1,0:T(8,128)}, f32[72,640]{1,0:T(8,128)S(1)}, u32[]{:S(2)}, u32[]{:S(2)}) collective-permute-start(f32[72,640]{1,0:T(8,128)} %get-tuple-element.24), channel_id=1, source_target_pairs={{0,8},{4,12},{8,0},{12,4},{16,24},{20,28},{24,16},{28,20},{1,9},{5... | collective-permute-start | bytes 552968 | tf_op jit(solution)/shard_map/ppermute | solution.py:207
  28.1 8.7 %collective-permute-start.4 = (f32[72,640]{1,0:T(8,128)}, f32[72,640]{1,0:T(8,128)S(1)}, u32[]{:S(2)}, u32[]{:S(2)}) collective-permute-start(f32[72,640]{1,0:T(8,128)} %get-tuple-element.25), channel_id=1, source_target_pairs={{0,12},{4,8},{8,4},{12,0},{16,28},{20,24},{24,20},{28,16},{1,13},{... | collective-permute-start | bytes 552968 | tf_op jit(solution)/shard_map/ppermute | solution.py:207
  31.6 6.2 %copy-start.2 = (f32[72,640]{1,0:T(8,128)}, f32[72,640]{1,0:T(8,128)S(1)}, u32[]{:S(2)}) copy-start(f32[72,640]{1,0:T(8,128)S(1)} %collective-permute-done.2.refs_1_) | copy-start | bytes 552964
  34.2 3.6 %copy-start.3 = (f32[72,640]{1,0:T(8,128)}, f32[72,640]{1,0:T(8,128)S(1)}, u32[]{:S(2)}) copy-start(f32[72,640]{1,0:T(8,128)S(1)} %collective-permute-done.3.refs_2_) | copy-start | bytes 552964
  36.8 1.1 %copy-start.4 = (f32[72,640]{1,0:T(8,128)}, f32[72,640]{1,0:T(8,128)S(1)}, u32[]{:S(2)}) copy-start(f32[72,640]{1,0:T(8,128)S(1)} %collective-permute-done.4.refs_3_) | copy-start | bytes 552964
  36.8 4.5 %copy-start.11 = (f32[72,512]{1,0:T(8,128)S(1)}, f32[72,512]{1,0:T(8,128)}, u32[]{:S(2)}) copy-start(f32[72,512]{1,0:T(8,128)} %get-tuple-element.27) | copy-start | bytes 442372
  36.8 6.0 %copy-start.10 = (f32[72,512]{1,0:T(8,128)S(1)}, f32[72,512]{1,0:T(8,128)}, u32[]{:S(2)}) copy-start(f32[72,512]{1,0:T(8,128)} %get-tuple-element.28) | copy-start | bytes 442372
  36.8 7.6 %copy-start.9 = (f32[72,512]{1,0:T(8,128)S(1)}, f32[72,512]{1,0:T(8,128)}, u32[]{:S(2)}) copy-start(f32[72,512]{1,0:T(8,128)} %get-tuple-element.29) | copy-start | bytes 442372
  37.9 10.7 %collective-permute-start.5 = (f32[72,640]{1,0:T(8,128)S(1)}, f32[72,640]{1,0:T(8,128)S(1)}, u32[]{:S(2)}, u32[]{:S(2)}) collective-permute-start(f32[72,640]{1,0:T(8,128)S(1)} %add_add_fusion), channel_id=1, source_target_pairs={{0,16},{4,20},{8,24},{12,28},{16,0},{20,4},{24,8},{28,12},{1,17},{... | collective-permute-start | bytes 552968 | tf_op jit(solution)/shard_map/ppermute | solution.py:216
  41.2 8.1 %collective-permute-start.6 = (f32[72,512]{1,0:T(8,128)S(1)}, f32[72,512]{1,0:T(8,128)S(1)}, u32[]{:S(2)}, u32[]{:S(2)}) collective-permute-start(f32[72,512]{1,0:T(8,128)S(1)} %copy-done.11), channel_id=1, source_target_pairs={{0,4},{4,0},{8,12},{12,8},{16,20},{20,16},{24,28},{28,24},{1,5},{5... | collective-permute-start | bytes 442376 | tf_op jit(solution)/shard_map/ppermute | solution.py:207
  42.8 8.4 %collective-permute-start.7 = (f32[72,512]{1,0:T(8,128)S(1)}, f32[72,512]{1,0:T(8,128)S(1)}, u32[]{:S(2)}, u32[]{:S(2)}) collective-permute-start(f32[72,512]{1,0:T(8,128)S(1)} %copy-done.10), channel_id=1, source_target_pairs={{0,8},{4,12},{8,0},{12,4},{16,24},{20,28},{24,16},{28,20},{1,9},{5... | collective-permute-start | bytes 442376 | tf_op jit(solution)/shard_map/ppermute | solution.py:207
  44.3 8.2 %collective-permute-start.8 = (f32[72,512]{1,0:T(8,128)S(1)}, f32[72,512]{1,0:T(8,128)S(1)}, u32[]{:S(2)}, u32[]{:S(2)}) collective-permute-start(f32[72,512]{1,0:T(8,128)S(1)} %copy-done.9), channel_id=1, source_target_pairs={{0,12},{4,8},{8,4},{12,0},{16,28},{20,24},{24,20},{28,16},{1,13},{... | collective-permute-start | bytes 442376 | tf_op jit(solution)/shard_map/ppermute | solution.py:207
  49.3 3.3 %copy-start.12 = (f32[72,512]{1,0:T(8,128)}, f32[72,512]{1,0:T(8,128)S(1)}, u32[]{:S(2)}) copy-start(f32[72,512]{1,0:T(8,128)S(1)} %collective-permute-done.6.refs_5_) | copy-start | bytes 442372
  51.1 1.5 %copy-start.13 = (f32[72,512]{1,0:T(8,128)}, f32[72,512]{1,0:T(8,128)S(1)}, u32[]{:S(2)}) copy-start(f32[72,512]{1,0:T(8,128)S(1)} %collective-permute-done.7.refs_6_) | copy-start | bytes 442372
  64.9 8.1 %collective-permute-start.9 = (f32[72,512]{1,0:T(8,128)}, f32[72,512]{1,0:T(8,128)S(1)}, u32[]{:S(2)}, u32[]{:S(2)}) collective-permute-start(f32[72,512]{1,0:T(8,128)} %get-tuple-element.31), channel_id=1, source_target_pairs={{0,16},{4,20},{8,24},{12,28},{16,0},{20,4},{24,8},{28,12},{1,17},{... | collective-permute-start | bytes 442376 | tf_op jit(solution)/shard_map/ppermute | solution.py:216
  74.8 7.1 %collective-permute-start.12 = (f32[72,512]{1,0:T(8,128)S(1)}, f32[72,512]{1,0:T(8,128)S(1)}, u32[]{:S(2)}, u32[]{:S(2)}) collective-permute-start(f32[72,512]{1,0:T(8,128)S(1)} %get-tuple-element.37), channel_id=1, source_target_pairs={{0,12},{4,8},{8,4},{12,0},{16,28},{20,24},{24,20},{28,16},{1,13},{... | collective-permute-start | bytes 442376 | tf_op jit(solution)/shard_map/ppermute | solution.py:207
  75.0 8.2 %collective-permute-start.10 = (f32[72,512]{1,0:T(8,128)S(1)}, f32[72,512]{1,0:T(8,128)S(1)}, u32[]{:S(2)}, u32[]{:S(2)}) collective-permute-start(f32[72,512]{1,0:T(8,128)S(1)} %get-tuple-element.38), channel_id=1, source_target_pairs={{0,4},{4,0},{8,12},{12,8},{16,20},{20,16},{24,28},{28,24},{1,5},{5... | collective-permute-start | bytes 442376 | tf_op jit(solution)/shard_map/ppermute | solution.py:207
  75.7 7.5 %collective-permute-start.11 = (f32[72,512]{1,0:T(8,128)S(1)}, f32[72,512]{1,0:T(8,128)S(1)}, u32[]{:S(2)}, u32[]{:S(2)}) collective-permute-start(f32[72,512]{1,0:T(8,128)S(1)} %get-tuple-element.39), channel_id=1, source_target_pairs={{0,8},{4,12},{8,0},{12,4},{16,24},{20,28},{24,16},{28,20},{1,9},{5... | collective-permute-start | bytes 442376 | tf_op jit(solution)/shard_map/ppermute | solution.py:207
  81.9 1.3 %copy-start.5 = (f32[72,512]{1,0:T(8,128)}, f32[72,512]{1,0:T(8,128)S(1)}, u32[]{:S(2)}) copy-start(f32[72,512]{1,0:T(8,128)S(1)} %collective-permute-done.12.refs_3_) | copy-start | bytes 442372
  (7 other events, 4.6 us)

commit v2 on v1

--- a/solution.py
+++ b/solution.py
@@ -7,6 +7,7 @@
 from jax.experimental.pallas import tpu as pltpu
 from jax.sharding import PartitionSpec as P
 
+
 GROUP = 4
 EDGE = 4
 ROWS = 8
@@ -22,15 +23,42 @@
     return -(-value // unit) * unit
 
 
-def call(kernel, outs, specs, scratch, flops):
+def call(kernel, outs, specs, scratch, flops, limit):
+    outs = [out if isinstance(out, jax.ShapeDtypeStruct) else jax.ShapeDtypeStruct(out, F32) for out in outs]
     return pl.pallas_call(
         kernel,
-        out_shape=[jax.ShapeDtypeStruct(shape, F32) for shape in outs],
+        out_shape=outs,
         in_specs=specs,
         out_specs=[VM] * len(outs),
         scratch_shapes=scratch,
+        compiler_params=pltpu.CompilerParams(vmem_limit_bytes=limit << 20),
         cost_estimate=pl.CostEstimate(flops=flops, bytes_accessed=4 << 20, transcendentals=0),
     )
+
+
+def weights_kernel(conv_in_ref, conv_out_ref, time_ref, w_in_ref, w_out_ref, column_ref, in_ref, out_ref):
+    chans, hid = conv_in_ref.shape[2:]
+    deep = in_ref.shape[0] // 3
+    rows = out_ref.shape[0] // 9
+    in_ref[...] = jnp.zeros_like(in_ref)
+    out_ref[...] = jnp.zeros_like(out_ref)
+    for b in range(3):
+        for a in range(3):
+            in_ref[a * deep : a * deep + chans, :] = conv_in_ref[a, b].astype(F32)
+            tap = 3 * a + b
+            out_ref[tap * rows : tap * rows + chans, :] = conv_out_ref[a, b].astype(F32)
+        w_in_ref[b * hid : (b + 1) * hid, :] = jnp.transpose(in_ref[...]).astype(BF16)
+    w_out_ref[...] = out_ref[...].astype(BF16)
+    column_ref[...] = jnp.transpose(jnp.broadcast_to(time_ref[...], (ROWS, hid)))[:, :1]
+
+
+def coefs_of(plan_ref, entry):
+    now = plan_ref[entry].astype(F32)
+    later = plan_ref[entry + 1].astype(F32)
+    beta = 0.1 + 19.9 * now / 1000.0
+    step = (now - later) / 1000.0
+    spread = jnp.sqrt(jnp.full((1, 1), beta * step, F32))
+    return 0.5 * beta * step, beta * step, spread, now / 1000.0
 
 
 def edges_kernel(lat, win_ref, noise_ref, anchor_ref, first_ref, last_ref):
@@ -80,7 +108,7 @@
 
 
 def first_kernel(
-    lat, me_ref, coef_ref, win_ref, noise_ref, before_ref, after_ref, shift_ref, w_in_ref, w_out_ref,
+    lat, where_ref, plan_ref, win_ref, noise_ref, before_ref, after_ref, shift_ref, w_in_ref, w_out_ref,
     *refs,
 ):
     outs = refs[:GROUP]
@@ -91,8 +119,8 @@
     sub = width // GROUP
     pitch = sub + 2 * EDGE
     strip = lat * pitch
-    me = me_ref[0]
-    half, drift, spread = coef_ref[0], coef_ref[1], coef_ref[2]
+    me = where_ref[0]
+    half, drift, spread, time = coefs_of(plan_ref, where_ref[1] + me)
     x_ref[...] = jnp.zeros_like(x_ref)
     u_ref[...] = jnp.zeros_like(u_ref)
     blank = jnp.zeros((chans, 2), F32)
@@ -110,8 +138,7 @@
             x_ref[0:chans, lanes] = wide[:, q * sub : q * sub + pitch]
             u_ref[0:chans, lanes] = total[:, q * sub : q * sub + pitch]
             wave_ref[q, 0:chans, l * sub : (l + 1) * sub] = noise[:, q * sub : (q + 1) * sub]
-    shift = shift_ref[...] * coef_ref[3]
-    rows = u_ref.shape[0]
+    shift = shift_ref[...] * time
     step = 2 * strip
     for part in range(GROUP // 2):
         lanes = slice(part * step, (part + 1) * step)
@@ -125,7 +152,7 @@
 
 
 def second_kernel(
-    lat, me_ref, coef_ref, anchor_ref, before_ref, after_ref, shift_ref, w_in_ref, w_out_ref, carry_ref,
+    lat, where_ref, plan_ref, anchor_ref, before_ref, after_ref, shift_ref, w_in_ref, w_out_ref, carry_ref,
     *refs,
 ):
     incs = refs[:GROUP]
@@ -137,7 +164,8 @@
     sub = width // GROUP
     pitch = sub + 2 * EDGE
     strip = lat * pitch
-    me = me_ref[0]
+    me = where_ref[0]
+    coefs = [coefs_of(plan_ref, where_ref[1] + j) for j in range(GROUP)]
     rows = carry_ref.shape[0]
     anc_ref[...] = jnp.zeros_like(anc_ref)
     x_ref[...] = jnp.zeros_like(x_ref)
@@ -160,10 +188,9 @@
     step = 2 * strip
     for part in range(GROUP // 2):
         lanes = slice(part * step, (part + 1) * step)
-        base = coef_ref.shape[0] // GROUP
         shift = jnp.concatenate(
             [
-                jnp.broadcast_to(shift_ref[...] * coef_ref[(2 * part + i) * base + 3], (shift_ref.shape[0], strip))
+                jnp.broadcast_to(shift_ref[...] * coefs[2 * part + i][3], (shift_ref.shape[0], strip))
                 for i in range(2)
             ],
             axis=1,
@@ -173,7 +200,8 @@
         for i in range(2):
             level = 2 * part + i
             mine = slice(i * strip, (i + 1) * strip)
-            part_ref[level] = x[0:rows, mine] * coef_ref[level * base] + score[:, mine] * coef_ref[level * base + 1]
+            part_ref[level] = x[0:rows, mine] * coefs[level][0] + score[:, mine] * coefs[level][1]
+
     def compact(block):
         return jnp.concatenate([block[:, l * pitch + EDGE : l * pitch + EDGE + sub] for l in range(lat)], axis=1)
 
@@ -187,12 +215,12 @@
         outs[m][...] = wave_ref[lax.bitwise_xor(me, m)]
 
 
-def last_kernel(lat, me_ref, *refs):
+def last_kernel(lat, where_ref, *refs):
     parts = refs[:GROUP]
     out_ref, all_ref = refs[GROUP:]
     chans = out_ref.shape[0] // lat
     sub = out_ref.shape[1] // GROUP
-    me = me_ref[0]
+    me = where_ref[0]
     for m in range(GROUP):
         all_ref[lax.bitwise_xor(me, m)] = parts[m][...]
     for l in range(lat):
@@ -230,15 +258,7 @@
     rows = up_to(chans, ROWS)
     deep = up_to(chans, PACK)
 
-    offset = start[0] + block * GROUP
-    times = lax.dynamic_slice(plan, (offset,), (GROUP + 1,)).astype(F32)
-    t_now = times[:-1]
-    beta = 0.1 + 19.9 * t_now / 1000.0
-    step = (t_now - times[1:]) / 1000.0
-    coefs = jnp.stack([0.5 * beta * step, beta * step, jnp.sqrt(beta * step), t_now / 1000.0], axis=1)
-    mine = lax.dynamic_slice(coefs, (me, 0), (1, 4)).reshape(-1)
-    coefs = coefs.reshape(-1)
-    me_arr = me.astype(jnp.int32).reshape(1)
+    where = jnp.stack([me, start[0] + block * GROUP]).astype(jnp.int32)
 
     def native(x):
         return jnp.transpose(x.reshape(lat, chans, width), (1, 0, 2)).reshape(chans * lat, width)
@@ -246,13 +266,21 @@
     win = native(window)
     noi = native(noise)
     anc = native(anchor)
-    w_in = jnp.pad(jnp.transpose(conv_in, (1, 2, 0, 3)), ((0, 0), (0, 0), (0, 0), (0, deep - chans)))
-    w_in = w_in.reshape(3 * hid, 3 * deep)
-    w_out = jnp.pad(conv_out, ((0, 0), (0, 0), (0, rows - chans), (0, 0))).reshape(9 * rows, hid)
-    column = time_shift.reshape(hid, 1)
+    w_in, w_out, column = call(
+        weights_kernel,
+        [
+            jax.ShapeDtypeStruct((3 * hid, 3 * deep), BF16),
+            jax.ShapeDtypeStruct((9 * rows, hid), BF16),
+            jax.ShapeDtypeStruct((hid, 1), F32),
+        ],
+        [VM] * 3,
+        [pltpu.VMEM((3 * deep, hid), F32), pltpu.VMEM((9 * rows, hid), F32)],
+        1 << 24,
+        8,
+    )(jnp.swapaxes(conv_in, 2, 3), conv_out, time_shift.reshape(1, hid))
 
     edge = (rows, 8 * lat)
-    first, last = call(functools.partial(edges_kernel, lat), [edge, edge], [VM] * 3, [], 1 << 20)(win, noi, anc)
+    first, last = call(functools.partial(edges_kernel, lat), [edge, edge], [VM] * 3, [], 1 << 20, 8)(win, noi, anc)
     count = lax.axis_size("lon")
     before = lax.ppermute(last, "lon", [(k, (k + 1) % count) for k in range(count)])
     after = lax.ppermute(first, "lon", [((k + 1) % count, k) for k in range(count)])
@@ -271,7 +299,8 @@
             pltpu.VMEM((GROUP,) + tight, F32),
         ],
         flops,
-    )(me_arr, mine, win, noi, before, after, column, w_in, w_out)
+        24,
+    )(where, plan, win, noi, before, after, column, w_in, w_out)
     incs = exchange(made[:GROUP])
     total = incs[0] + incs[1] + incs[2] + incs[3]
     carry = carried(total, block)
@@ -288,7 +317,8 @@
             pltpu.VMEM((GROUP,) + wide, F32),
         ],
         flops,
-    )(me_arr, coefs, anc, before, after, column, w_in, w_out, carry, *incs, *waves)
+        24,
+    )(where, plan, anc, before, after, column, w_in, w_out, carry, *incs, *waves)
     carry = carried(done[GROUP], block)
     parts = exchange([part + carry for part in done[:GROUP]])
     (out,) = call(
@@ -297,7 +327,8 @@
         [SM] + [VM] * GROUP,
         [pltpu.VMEM((GROUP,) + tight, F32)],
         1 << 20,
-    )(me_arr, *parts)
+        8,
+    )(where, *parts)
     return jnp.transpose(out.reshape(chans, lat, width), (1, 0, 2))[None]
 
 

time: 86.8 us -> 77.7 us (0.90)
  Pallas kernels: 28.6 us -> 22.4 us
  local copies, waits for them, and re-layouts: 8.59 us -> 3.86 us
  waiting for transfers between devices: 28.2 us -> 32.3 us
  other arithmetic: 3.79 us -> 0.22 us
  starting transfers between devices: 16.6 us -> 18 us
    reshape x3 -> x0, local copies, waits for them, and re-layouts: 2.37 us -> none  [the longest x1 1 us: body(): w_in = w_in.reshape(3 * hid, 3 * deep)]
    ppermute x2, waiting for transfers between devices: 11.4 us -> 13.5 us  [carried(): lax.ppermute(total, 'lvl', [(k, (k + s * GROUP) % count) for k in range(c...]
    pallas_call x1, Pallas kernels: 11.7 us -> 9.57 us  [body(): call(functools.partial(second_kernel, lat), [tight] * (GROUP + 1), [SM, S...]
    pallas_call x1, Pallas kernels: 3.44 us -> 1.42 us  [body(): call(functools.partial(edges_kernel, lat), [edge, edge], [VM] * 3, [], 1...]
    pallas_call x1, Pallas kernels: 10.9 us -> 9.06 us  [body(): call(functools.partial(first_kernel, lat), [wide] * GROUP + [tight] * GRO...]
    add x1, other arithmetic: 1.84 us -> 0.06 us  [body(): parts = exchange([part + carry for part in done[:GROUP]])]
    ppermute x2, starting transfers between devices: 3.2 us -> 4.64 us  [carried(): lax.ppermute(total, 'lvl', [(k, (k + s * GROUP) % count) for k in range(c...]
    ppermute x9, waiting for transfers between devices: 16.8 us -> 18.1 us  [exchange(): lax.ppermute(pieces[m], 'lvl', [(k, k ^ m) for k in range(count)])]
  transfers between devices with their start and end apart: 13 -> 13, of which waited for: 9 -> 12; matrix products, arithmetic and copies ran while one was open for 6% -> 0% of each run, Pallas kernels for 0% -> 0%
where the time goes in v2:
time: 77.7 us; the launch traced here: 77.5 us
  waiting for transfers between devices  32.3 us (42%)
  Pallas kernels  22.4 us (29%)
  starting transfers between devices  18 us (23%)
  local copies, waits for them, and re-layouts  3.86 us (5%)
    ppermute x9, waiting for transfers between devices, exchange(): lax.ppermute(pieces[m], 'lvl', [(k, k ^ m) for k in range(count)])  18.1 us
    ppermute x2, waiting for transfers between devices, carried(): lax.ppermute(total, 'lvl', [(k, (k + s * GROUP) % count) for k in range(c...  13.5 us
    ppermute x9, starting transfers between devices, exchange(): lax.ppermute(pieces[m], 'lvl', [(k, k ^ m) for k in range(count)])  10.8 us
    pallas_call x1, Pallas kernels, body(): call(functools.partial(second_kernel, lat), [tight] * (GROUP + 1), [SM, S...  9.57 us
    pallas_call x1, Pallas kernels, body(): call(functools.partial(first_kernel, lat), [wide] * GROUP + [tight] * GRO...  9.06 us
    ppermute x2, starting transfers between devices, carried(): lax.ppermute(total, 'lvl', [(k, (k + s * GROUP) % count) for k in range(c...  4.64 us
    unnamed x20, local copies, waits for them, and re-layouts  3.86 us
    pallas_call x1, Pallas kernels, body(): call(functools.partial(last_kernel, lat), [(chans * lat, width)], [SM] +...  2.03 us
  transfers between devices with their start and end apart: 13, of which 12 were waited for; matrix products, arithmetic and copies ran while one was open for 0% of the time, Pallas kernels for 0%

profile of v2, /device:TPU:0, one launch (start us, length us, event | category | flops | bytes accessed | tf_op | source)
XLA Modules:
  0.0 77.5 jit_solution(18286139566765355231)
XLA Ops:
  0.0 1.1 %copy-done = f32[1,16,69,128]{3,1,2,0:T(8,128)S(1)} copy-done((f32[1,16,69,128]{3,1,2,0:T(8,128)S(1)}, f32[1,16,69,128]{3,1,2,0:T(8,128)}, u32[]{:S(2)}) %copy-start) | copy-done | bytes 565272
  1.1 1.1 %copy-done.2 = f32[1,16,69,128]{3,1,2,0:T(8,128)S(1)} copy-done((f32[1,16,69,128]{3,1,2,0:T(8,128)S(1)}, f32[1,16,69,128]{3,1,2,0:T(8,128)}, u32[]{:S(2)}) %copy-start.2) | copy-done | bytes 565272
  2.1 1.1 %copy-done.4 = f32[16,69,128]{2,0,1:T(8,128)S(1)} copy-done((f32[16,69,128]{2,0,1:T(8,128)S(1)}, f32[16,69,128]{2,0,1:T(8,128)}, u32[]{:S(2)}) %copy-start.4) | copy-done | bytes 565272
  3.2 1.4 %shard_map.82 = (f32[72,128]{1,0:T(8,128)S(1)}, f32[72,128]{1,0:T(8,128)S(1)}) custom-call(f32[1104,128]{1,0:T(8,128)S(1)} %bitcast.24, f32[1104,128]{1,0:T(8,128)S(1)} %bitcast.26, f32[1104,128]{1,0:T(8,128)S(1)} %bitcast.28), custom_call_target="tpu_custom_call" | custom-call | flops 1048576 | bytes 4194304 | tf_op jit(solution)/shard_map/pallas_call | solution.py:283
  5.2 2.0 %collective-permute-start.1 = (f32[72,128]{1,0:T(8,128)S(1)}, f32[72,128]{1,0:T(8,128)S(1)}, u32[]{:S(2)}, u32[]{:S(2)}) collective-permute-start(f32[72,128]{1,0:T(8,128)S(1)} %get-tuple-element.24), channel_id=1, source_target_pairs={{1,0},{2,1},{3,2},{0,3},{5,4},{6,5},{7,6},{4,7},{9,8},{10,9},{11,1... | collective-permute-start | bytes 110600 | tf_op jit(solution)/shard_map/ppermute | solution.py:286
  9.6 9.1 %shard_map.84 = (f32[72,640]{1,0:T(8,128)S(1)}, f32[72,640]{1,0:T(8,128)S(1)}, f32[72,640]{1,0:T(8,128)S(1)}, f32[72,640]{1,0:T(8,128)S(1)}, f32[72,512]{1,0:T(8...) custom-call(s32[2]{0:T(128)S(1)} %pad_add_fusion.where_ref, s32[256]{0:T(256)S(1)} %copy-done.9, ...), custom_call_target="tpu_custom_call" | custom-call | flops 976748544 | bytes 4194304 | tf_op jit(solution)/shard_map/pallas_call | solution.py:291
  18.7 2.2 %collective-permute-start.2 = (f32[72,640]{1,0:T(8,128)S(1)}, f32[72,640]{1,0:T(8,128)S(1)}, u32[]{:S(2)}, u32[]{:S(2)}) collective-permute-start(f32[72,640]{1,0:T(8,128)S(1)} %get-tuple-element.29), channel_id=1, source_target_pairs={{0,4},{4,0},{8,12},{12,8},{16,20},{20,16},{24,28},{28,24},{1,5},{5... | collective-permute-start | bytes 552968 | tf_op jit(solution)/shard_map/ppermute | solution.py:235
  20.9 1.6 %collective-permute-start.3 = (f32[72,640]{1,0:T(8,128)S(1)}, f32[72,640]{1,0:T(8,128)S(1)}, u32[]{:S(2)}, u32[]{:S(2)}) collective-permute-start(f32[72,640]{1,0:T(8,128)S(1)} %get-tuple-element.30), channel_id=1, source_target_pairs={{0,8},{4,12},{8,0},{12,4},{16,24},{20,28},{24,16},{28,20},{1,9},{5... | collective-permute-start | bytes 552968 | tf_op jit(solution)/shard_map/ppermute | solution.py:235
  22.4 2.8 %collective-permute-done.2.refs_1_ = f32[72,640]{1,0:T(8,128)S(1)} collective-permute-done((f32[72,640]{1,0:T(8,128)S(1)}, f32[72,640]{1,0:T(8,128)S(1)}, u32[]{:S(2)}, u32[]{:S(2)}) %collective-permute-start.2) | collective-permute-done | bytes 184352 | tf_op jit(solution)/shard_map/ppermute | solution.py:235
  25.3 2.8 %collective-permute-done.3.refs_2_ = f32[72,640]{1,0:T(8,128)S(1)} collective-permute-done((f32[72,640]{1,0:T(8,128)S(1)}, f32[72,640]{1,0:T(8,128)S(1)}, u32[]{:S(2)}, u32[]{:S(2)}) %collective-permute-start.3) | collective-permute-done | bytes 184352 | tf_op jit(solution)/shard_map/ppermute | solution.py:235
  28.0 3.0 %collective-permute-done.4.refs_3_ = f32[72,640]{1,0:T(8,128)S(1)} collective-permute-done((f32[72,640]{1,0:T(8,128)S(1)}, f32[72,640]{1,0:T(8,128)S(1)}, u32[]{:S(2)}, u32[]{:S(2)}) %collective-permute-start.4) | collective-permute-done | bytes 184352 | tf_op jit(solution)/shard_map/ppermute | solution.py:235
  31.1 3.5 %collective-permute-start.5 = (f32[72,640]{1,0:T(8,128)S(1)}, f32[72,640]{1,0:T(8,128)S(1)}, u32[]{:S(2)}, u32[]{:S(2)}) collective-permute-start(f32[72,640]{1,0:T(8,128)S(1)} %add_add_fusion), channel_id=1, source_target_pairs={{0,16},{4,20},{8,24},{12,28},{16,0},{20,4},{24,8},{28,12},{1,17},{... | collective-permute-start | bytes 552968 | tf_op jit(solution)/shard_map/ppermute | solution.py:244
  34.6 1.5 %collective-permute-start.6 = (f32[72,512]{1,0:T(8,128)S(1)}, f32[72,512]{1,0:T(8,128)S(1)}, u32[]{:S(2)}, u32[]{:S(2)}) collective-permute-start(f32[72,512]{1,0:T(8,128)S(1)} %get-tuple-element.33), channel_id=1, source_target_pairs={{0,4},{4,0},{8,12},{12,8},{16,20},{20,16},{24,28},{28,24},{1,5},{5... | collective-permute-start | bytes 442376 | tf_op jit(solution)/shard_map/ppermute | solution.py:235
  36.2 1.6 %collective-permute-start.7 = (f32[72,512]{1,0:T(8,128)S(1)}, f32[72,512]{1,0:T(8,128)S(1)}, u32[]{:S(2)}, u32[]{:S(2)}) collective-permute-start(f32[72,512]{1,0:T(8,128)S(1)} %get-tuple-element.34), channel_id=1, source_target_pairs={{0,8},{4,12},{8,0},{12,4},{16,24},{20,28},{24,16},{28,20},{1,9},{5... | collective-permute-start | bytes 442376 | tf_op jit(solution)/shard_map/ppermute | solution.py:235
  38.1 5.5 %collective-permute-done.5 = f32[72,640]{1,0:T(8,128)S(1)} collective-permute-done((f32[72,640]{1,0:T(8,128)S(1)}, f32[72,640]{1,0:T(8,128)S(1)}, u32[]{:S(2)}, u32[]{:S(2)}) %collective-permute-start.5) | collective-permute-done | bytes 184352 | tf_op jit(solution)/shard_map/ppermute | solution.py:244
  43.7 2.0 %collective-permute-done.7.refs_6_ = f32[72,512]{1,0:T(8,128)S(1)} collective-permute-done((f32[72,512]{1,0:T(8,128)S(1)}, f32[72,512]{1,0:T(8,128)S(1)}, u32[]{:S(2)}, u32[]{:S(2)}) %collective-permute-start.7) | collective-permute-done | bytes 147488 | tf_op jit(solution)/shard_map/ppermute | solution.py:235
  45.7 1.8 %collective-permute-done.8.refs_7_ = f32[72,512]{1,0:T(8,128)S(1)} collective-permute-done((f32[72,512]{1,0:T(8,128)S(1)}, f32[72,512]{1,0:T(8,128)S(1)}, u32[]{:S(2)}, u32[]{:S(2)}) %collective-permute-start.8) | collective-permute-done | bytes 147488 | tf_op jit(solution)/shard_map/ppermute | solution.py:235
  47.5 9.6 %shard_map.85 = (f32[72,512]{1,0:T(8,128)S(1)}, f32[72,512]{1,0:T(8,128)S(1)}, f32[72,512]{1,0:T(8,128)S(1)}, f32[72,512]{1,0:T(8,128)S(1)}, f32[72,512]{1,0:T(8,128)S(1)}) custom-call(s32[2]{0:T(128)S(1)} %pad_add_fusion.where_ref, s32[256]{0:T(256)S(1)} %copy-done.9, f32[1104,128]{1,0:T(8,128)S(1)} %bitcast.29, ...), custom_call_target="tpu_custom_call" | custom-call | flops 976748544 | bytes 4194304 | tf_op jit(solution)/shard_map/pallas_call | solution.py:308
  57.0 1.1 %collective-permute-start.9 = (f32[72,512]{1,0:T(8,128)S(1)}, f32[72,512]{1,0:T(8,128)S(1)}, u32[]{:S(2)}, u32[]{:S(2)}) collective-permute-start(f32[72,512]{1,0:T(8,128)S(1)} %get-tuple-element.37), channel_id=1, source_target_pairs={{0,16},{4,20},{8,24},{12,28},{16,0},{20,4},{24,8},{28,12},{1,17},{... | collective-permute-start | bytes 442376 | tf_op jit(solution)/shard_map/ppermute | solution.py:244
  58.2 7.9 %collective-permute-done.9 = f32[72,512]{1,0:T(8,128)S(1)} collective-permute-done((f32[72,512]{1,0:T(8,128)S(1)}, f32[72,512]{1,0:T(8,128)S(1)}, u32[]{:S(2)}, u32[]{:S(2)}) %collective-permute-start.9) | collective-permute-done | bytes 147488 | tf_op jit(solution)/shard_map/ppermute | solution.py:244
  66.3 1.1 %collective-permute-start.10 = (f32[72,512]{1,0:T(8,128)S(1)}, f32[72,512]{1,0:T(8,128)S(1)}, u32[]{:S(2)}, u32[]{:S(2)}) collective-permute-start(f32[72,512]{1,0:T(8,128)S(1)} %get-tuple-element.42), channel_id=1, source_target_pairs={{0,4},{4,0},{8,12},{12,8},{16,20},{20,16},{24,28},{28,24},{1,5},{5... | collective-permute-start | bytes 442376 | tf_op jit(solution)/shard_map/ppermute | solution.py:235
  67.4 2.4 %collective-permute-start.11 = (f32[72,512]{1,0:T(8,128)S(1)}, f32[72,512]{1,0:T(8,128)S(1)}, u32[]{:S(2)}, u32[]{:S(2)}) collective-permute-start(f32[72,512]{1,0:T(8,128)S(1)} %get-tuple-element.43), channel_id=1, source_target_pairs={{0,8},{4,12},{8,0},{12,4},{16,24},{20,28},{24,16},{28,20},{1,9},{5... | collective-permute-start | bytes 442376 | tf_op jit(solution)/shard_map/ppermute | solution.py:235
  69.8 4.0 %collective-permute-done.12.refs_3_ = f32[72,512]{1,0:T(8,128)S(1)} collective-permute-done((f32[72,512]{1,0:T(8,128)S(1)}, f32[72,512]{1,0:T(8,128)S(1)}, u32[]{:S(2)}, u32[]{:S(2)}) %collective-permute-start.12) | collective-permute-done | bytes 147488 | tf_op jit(solution)/shard_map/ppermute | solution.py:235
  75.4 2.0 %shard_map.86 = f32[1104,128]{1,0:T(8,128)} custom-call(s32[2]{0:T(128)S(1)} %pad_add_fusion.where_ref, f32[72,512]{1,0:T(8,128)S(1)} %get-tuple-element.44.refs_0_, f32[72,512]{1,0:T(8,128)S(1)} %collective-permute-done.10.refs_1_, f32[72,512]{1,0:T(8,128)S(1)} %collective-permute-done.11.refs_2_, f32[72,512]{1,0:T(8,128)S(1)} %collective-permute-done.12.refs_3_), custom_call_target="tpu_custom_call" | custom-call | flops 1048576 | bytes 4194304 | tf_op jit(solution)/shard_map/pallas_call | solution.py:324
  (31 shorter events, 4.6 us)
Async XLA Ops:
  0.0 1.1 %copy-start = (f32[1,16,69,128]{3,1,2,0:T(8,128)S(1)}, f32[1,16,69,128]{3,1,2,0:T(8,128)}, u32[]{:S(2)}) copy-start(f32[1,16,69,128]{3,1,2,0:T(8,128)} %param.8) | copy-start | bytes 1695748
  1.1 1.1 %copy-start.2 = (f32[1,16,69,128]{3,1,2,0:T(8,128)S(1)}, f32[1,16,69,128]{3,1,2,0:T(8,128)}, u32[]{:S(2)}) copy-start(f32[1,16,69,128]{3,1,2,0:T(8,128)} %param.10) | copy-start | bytes 1695748
  2.1 1.1 %copy-start.4 = (f32[16,69,128]{2,0,1:T(8,128)S(1)}, f32[16,69,128]{2,0,1:T(8,128)}, u32[]{:S(2)}) copy-start(f32[16,69,128]{2,0,1:T(8,128)} %param.9) | copy-start | bytes 1695748
  3.2 4.7 %copy-start.6 = (bf16[3,3,192,69]{2,3,1,0:T(8,128)(2,1)S(1)}, bf16[3,3,192,69]{2,3,1,0:T(8,128)(2,1)}, u32[]{:S(2)}) copy-start(bf16[3,3,192,69]{2,3,1,0:T(8,128)(2,1)} %param.11) | copy-start | bytes 715396
  3.2 4.7 %copy-start.7 = (bf16[3,3,69,192]{3,2,1,0:T(8,128)(2,1)S(1)}, bf16[3,3,69,192]{3,2,1,0:T(8,128)(2,1)}, u32[]{:S(2)}) copy-start(bf16[3,3,69,192]{3,2,1,0:T(8,128)(2,1)} %conv_out_ref.1) | copy-start | bytes 715396
  3.2 4.7 %copy-start.8 = (f32[192]{0:T(256)S(1)}, f32[192]{0:T(256)}, u32[]{:S(2)}) copy-start(f32[192]{0:T(256)} %param.13) | copy-start | bytes 2308
  3.2 5.8 %copy-start.3 = (f32[1,16,69,128]{3,1,2,0:T(8,128)S(1)}, f32[1,16,69,128]{3,1,2,0:T(8,128)}, u32[]{:S(2)}) copy-start(f32[1,16,69,128]{3,1,2,0:T(8,128)} %param.10) | copy-start | bytes 1695748
  4.6 4.3 %copy-start.1 = (f32[1,16,69,128]{3,1,2,0:T(8,128)S(1)}, f32[1,16,69,128]{3,1,2,0:T(8,128)}, u32[]{:S(2)}) copy-start(f32[1,16,69,128]{3,1,2,0:T(8,128)} %param.8) | copy-start | bytes 1695748
  4.6 4.1 %collective-permute-start = (f32[72,128]{1,0:T(8,128)S(1)}, f32[72,128]{1,0:T(8,128)S(1)}, u32[]{:S(2)}, u32[]{:S(2)}) collective-permute-start(f32[72,128]{1,0:T(8,128)S(1)} %get-tuple-element.23), channel_id=1, source_target_pairs={{0,1},{1,2},{2,3},{3,0},{4,5},{5,6},{6,7},{7,4},{8,9},{9,10},{10,1... | collective-permute-start | bytes 110600 | tf_op jit(solution)/shard_map/ppermute | solution.py:285
  5.2 3.8 %collective-permute-start.1 = (f32[72,128]{1,0:T(8,128)S(1)}, f32[72,128]{1,0:T(8,128)S(1)}, u32[]{:S(2)}, u32[]{:S(2)}) collective-permute-start(f32[72,128]{1,0:T(8,128)S(1)} %get-tuple-element.24), channel_id=1, source_target_pairs={{1,0},{2,1},{3,2},{0,3},{5,4},{6,5},{7,6},{4,7},{9,8},{10,9},{11,1... | collective-permute-start | bytes 110600 | tf_op jit(solution)/shard_map/ppermute | solution.py:286
  8.9 0.7 copy-start.9
  18.7 6.6 %collective-permute-start.2 = (f32[72,640]{1,0:T(8,128)S(1)}, f32[72,640]{1,0:T(8,128)S(1)}, u32[]{:S(2)}, u32[]{:S(2)}) collective-permute-start(f32[72,640]{1,0:T(8,128)S(1)} %get-tuple-element.29), channel_id=1, source_target_pairs={{0,4},{4,0},{8,12},{12,8},{16,20},{20,16},{24,28},{28,24},{1,5},{5... | collective-permute-start | bytes 552968 | tf_op jit(solution)/shard_map/ppermute | solution.py:235
  20.9 7.2 %collective-permute-start.3 = (f32[72,640]{1,0:T(8,128)S(1)}, f32[72,640]{1,0:T(8,128)S(1)}, u32[]{:S(2)}, u32[]{:S(2)}) collective-permute-start(f32[72,640]{1,0:T(8,128)S(1)} %get-tuple-element.30), channel_id=1, source_target_pairs={{0,8},{4,12},{8,0},{12,4},{16,24},{20,28},{24,16},{28,20},{1,9},{5... | collective-permute-start | bytes 552968 | tf_op jit(solution)/shard_map/ppermute | solution.py:235
  22.4 8.6 %collective-permute-start.4 = (f32[72,640]{1,0:T(8,128)S(1)}, f32[72,640]{1,0:T(8,128)S(1)}, u32[]{:S(2)}, u32[]{:S(2)}) collective-permute-start(f32[72,640]{1,0:T(8,128)S(1)} %get-tuple-element.31), channel_id=1, source_target_pairs={{0,12},{4,8},{8,4},{12,0},{16,28},{20,24},{24,20},{28,16},{1,13},{... | collective-permute-start | bytes 552968 | tf_op jit(solution)/shard_map/ppermute | solution.py:235
  31.1 16.4 %copy-start.5 = (f32[16,69,128]{2,0,1:T(8,128)S(1)}, f32[16,69,128]{2,0,1:T(8,128)}, u32[]{:S(2)}) copy-start(f32[16,69,128]{2,0,1:T(8,128)} %param.9) | copy-start | bytes 1695748
  31.1 12.5 %collective-permute-start.5 = (f32[72,640]{1,0:T(8,128)S(1)}, f32[72,640]{1,0:T(8,128)S(1)}, u32[]{:S(2)}, u32[]{:S(2)}) collective-permute-start(f32[72,640]{1,0:T(8,128)S(1)} %add_add_fusion), channel_id=1, source_target_pairs={{0,16},{4,20},{8,24},{12,28},{16,0},{20,4},{24,8},{28,12},{1,17},{... | collective-permute-start | bytes 552968 | tf_op jit(solution)/shard_map/ppermute | solution.py:244
  34.6 9.1 %collective-permute-start.6 = (f32[72,512]{1,0:T(8,128)S(1)}, f32[72,512]{1,0:T(8,128)S(1)}, u32[]{:S(2)}, u32[]{:S(2)}) collective-permute-start(f32[72,512]{1,0:T(8,128)S(1)} %get-tuple-element.33), channel_id=1, source_target_pairs={{0,4},{4,0},{8,12},{12,8},{16,20},{20,16},{24,28},{28,24},{1,5},{5... | collective-permute-start | bytes 442376 | tf_op jit(solution)/shard_map/ppermute | solution.py:235
  36.2 9.5 %collective-permute-start.7 = (f32[72,512]{1,0:T(8,128)S(1)}, f32[72,512]{1,0:T(8,128)S(1)}, u32[]{:S(2)}, u32[]{:S(2)}) collective-permute-start(f32[72,512]{1,0:T(8,128)S(1)} %get-tuple-element.34), channel_id=1, source_target_pairs={{0,8},{4,12},{8,0},{12,4},{16,24},{20,28},{24,16},{28,20},{1,9},{5... | collective-permute-start | bytes 442376 | tf_op jit(solution)/shard_map/ppermute | solution.py:235
  37.7 9.7 %collective-permute-start.8 = (f32[72,512]{1,0:T(8,128)S(1)}, f32[72,512]{1,0:T(8,128)S(1)}, u32[]{:S(2)}, u32[]{:S(2)}) collective-permute-start(f32[72,512]{1,0:T(8,128)S(1)} %get-tuple-element.35), channel_id=1, source_target_pairs={{0,12},{4,8},{8,4},{12,0},{16,28},{20,24},{24,20},{28,16},{1,13},{... | collective-permute-start | bytes 442376 | tf_op jit(solution)/shard_map/ppermute | solution.py:235
  57.0 9.1 %collective-permute-start.9 = (f32[72,512]{1,0:T(8,128)S(1)}, f32[72,512]{1,0:T(8,128)S(1)}, u32[]{:S(2)}, u32[]{:S(2)}) collective-permute-start(f32[72,512]{1,0:T(8,128)S(1)} %get-tuple-element.37), channel_id=1, source_target_pairs={{0,16},{4,20},{8,24},{12,28},{16,0},{20,4},{24,8},{28,12},{1,17},{... | collective-permute-start | bytes 442376 | tf_op jit(solution)/shard_map/ppermute | solution.py:244
  66.2 7.6 %collective-permute-start.12 = (f32[72,512]{1,0:T(8,128)S(1)}, f32[72,512]{1,0:T(8,128)S(1)}, u32[]{:S(2)}, u32[]{:S(2)}) collective-permute-start(f32[72,512]{1,0:T(8,128)S(1)} %get-tuple-element.41), channel_id=1, source_target_pairs={{0,12},{4,8},{8,4},{12,0},{16,28},{20,24},{24,20},{28,16},{1,13},{... | collective-permute-start | bytes 442376 | tf_op jit(solution)/shard_map/ppermute | solution.py:235
  66.3 8.2 %collective-permute-start.10 = (f32[72,512]{1,0:T(8,128)S(1)}, f32[72,512]{1,0:T(8,128)S(1)}, u32[]{:S(2)}, u32[]{:S(2)}) collective-permute-start(f32[72,512]{1,0:T(8,128)S(1)} %get-tuple-element.42), channel_id=1, source_target_pairs={{0,4},{4,0},{8,12},{12,8},{16,20},{20,16},{24,28},{28,24},{1,5},{5... | collective-permute-start | bytes 442376 | tf_op jit(solution)/shard_map/ppermute | solution.py:235
  67.4 8.1 %collective-permute-start.11 = (f32[72,512]{1,0:T(8,128)S(1)}, f32[72,512]{1,0:T(8,128)S(1)}, u32[]{:S(2)}, u32[]{:S(2)}) collective-permute-start(f32[72,512]{1,0:T(8,128)S(1)} %get-tuple-element.43), channel_id=1, source_target_pairs={{0,8},{4,12},{8,0},{12,4},{16,24},{20,28},{24,16},{28,20},{1,9},{5... | collective-permute-start | bytes 442376 | tf_op jit(solution)/shard_map/ppermute | solution.py:235

commit v3 on v0

v3 whole, which is shorter than its diff:
```python
import functools

import jax
import jax.numpy as jnp
from jax import lax
from jax.experimental import pallas as pl
from jax.experimental.pallas import tpu as pltpu
from jax.sharding import PartitionSpec as P


GROUP = 4
EDGE = 4
SLOT = 2 * EDGE
ROWS = 8
PACK = 16
COEFS = 8

VM = pl.BlockSpec(memory_space=pltpu.VMEM)
SM = pl.BlockSpec(memory_space=pltpu.SMEM)
ANY = pl.BlockSpec(memory_space=pl.ANY)
F32 = jnp.float32
BF16 = jnp.bfloat16


def up_to(value, unit):
    return -(-value // unit) * unit


def call(kernel, outs, specs, scratch, flops, limit, out_specs=None):
    outs = [out if isinstance(out, jax.ShapeDtypeStruct) else jax.ShapeDtypeStruct(out, F32) for out in outs]
    return pl.pallas_call(
        kernel,
        out_shape=outs,
        in_specs=specs,
        out_specs=out_specs or [VM] * len(outs),
        scratch_shapes=scratch,
        compiler_params=pltpu.CompilerParams(vmem_limit_bytes=limit << 20),
        cost_estimate=pl.CostEstimate(flops=flops, bytes_accessed=4 << 20, transcendentals=0),
    )


def roll(x, shift):
    shift = shift % x.shape[1]
    return pltpu.roll(x, shift, 1) if shift else x


def lanes_of(x):
    return lax.broadcasted_iota(jnp.int32, x.shape, 1)


def between(lane, low, high):
    return jnp.logical_and(lane >= low, lane < high)


def swapped(arrays):
    count = len(arrays)
    sub = arrays[0].shape[1] // count
    block = lanes_of(arrays[0]) // sub
    turned = []
    for r in range(count):
        mixed = arrays[r]
        for j in range(1, count):
            mixed = jnp.where(block == j, arrays[(j + r) % count], mixed)
        turned.append(roll(mixed, r * sub))
    outs = []
    for j in range(count):
        mixed = turned[(0 - j) % count]
        for i in range(1, count):
            mixed = jnp.where(block == i, turned[(i - j) % count], mixed)
        outs.append(mixed)
    return outs


def edges_kernel(lat, win_any, noise_any, anchor_any, first_ref, last_ref, win_ref, noise_ref, anchor_ref, sems):
    copies = [
        pltpu.make_async_copy(source, target, sems.at[i])
        for i, (source, target) in enumerate(
            [(win_any, win_ref), (noise_any, noise_ref), (anchor_any, anchor_ref)]
        )
    ]
    for copy in copies:
        copy.start()
    chans = win_ref.shape[0] // lat
    tiles = []
    for copy, ref, shift, skip in zip(copies, (win_ref, noise_ref, anchor_ref), (4, 6, 8), (0, 0, 6)):
        copy.wait()
        tile = roll(ref[pl.ds(0, chans, stride=lat), :], shift)
        width = tile.shape[1]
        slot = lax.rem(lanes_of(tile) + width - skip, width) // SLOT
        for l in range(1, lat):
            tile = jnp.where(slot == l, roll(ref[pl.ds(l, chans, stride=lat), :], SLOT * l + shift), tile)
        tiles.append(tile)
    win, noise, anchor = tiles
    spot = lax.rem(lanes_of(win), SLOT)
    last = jnp.where(spot < 4, win, jnp.where(spot < 6, noise, anchor))
    first = jnp.where(spot < 2, roll(noise, -6), jnp.where(spot < 4, roll(anchor, -6), win))
    for ref, value in ((first_ref, first), (last_ref, last)):
        ref[...] = jnp.zeros_like(ref)
        ref[0:chans, :] = value


def tiled(rolled, pitch, turn):
    lat = len(rolled)
    width = rolled[0].shape[1]
    lane = lanes_of(rolled[0])
    tiles = []
    for t in range(lat * pitch // width):
        tile = None
        for slot in range(lat):
            low = slot * pitch - t * width
            if low >= width or low + pitch <= 0:
                continue
            piece = rolled[(slot - turn) % lat]
            tile = piece if tile is None else jnp.where(lane >= low, piece, tile)
        tiles.append(tile)
    return tiles


def turn_of(pitch, sub, width):
    return next(k for k in range(width) if (pitch * k) % width == sub)


def coefs_of(plan_ref, entry):
    now = plan_ref[entry].astype(F32)
    later = plan_ref[entry + 1].astype(F32)
    beta = 0.1 + 19.9 * now / 1000.0
    step = (now - later) / 1000.0
    return [0.5 * beta * step, beta * step, jnp.sqrt(jnp.full((1, 1), beta * step, F32)), now / 1000.0]


def build_kernel(
    lat, start_ref, plan_ref, conv_in_ref, conv_out_ref, time_ref, win_ref, noise_ref,
    w_in_ref, w_out_ref, column_ref, coef_ref, x_ref, n_ref, *refs,
):
    waves = refs[:GROUP]
    in_ref, out_ref, wave_ref = refs[GROUP:]
    chans, hid = conv_in_ref.shape[2:]
    width = win_ref.shape[1]
    deep = in_ref.shape[0] // 9
    rows = n_ref.shape[1]
    in_ref[...] = jnp.zeros_like(in_ref)
    out_ref[...] = jnp.zeros_like(out_ref)
    for b in range(3):
        for a in range(3):
            tap = 3 * b + a
            in_ref[tap * deep : tap * deep + chans, :] = conv_in_ref[a, b].astype(F32)
            out_ref[a * rows : a * rows + chans, b * hid : (b + 1) * hid] = conv_out_ref[a, b].astype(F32)
    w_in_ref[...] = jnp.transpose(in_ref[...]).astype(BF16)
    w_out_ref[...] = out_ref[...].astype(BF16)
    column_ref[...] = jnp.transpose(jnp.broadcast_to(time_ref[...], (ROWS, hid)))[:, :1]

    level = lax.axis_index("lvl")
    me = lax.rem(level, GROUP)
    entries = [level] + [level - me + j for j in range(GROUP)]
    for i, entry in enumerate(entries):
        values = coefs_of(plan_ref, start_ref[0] + entry)
        for r, value in enumerate(values):
            coef_ref[COEFS * i + r : COEFS * i + r + 1, :] = jnp.broadcast_to(
                value if r == 2 else jnp.full((1, 1), value, F32), (1, coef_ref.shape[1])
            )
    sub = width // GROUP
    pitch = sub + 2 * EDGE
    turn = turn_of(pitch, sub, width)
    for source, target in ((win_ref, x_ref), (noise_ref, n_ref)):
        target[:, chans // ROWS * ROWS :, :] = jnp.zeros_like(target[:, chans // ROWS * ROWS :, :])
        rolled = [roll(source[pl.ds(l, chans, stride=lat), :], pitch * l + EDGE) for l in range(lat)]
        for q in range(GROUP):
            for t, tile in enumerate(tiled(rolled, pitch, turn * q)):
                target[q, 0:chans, t * width : (t + 1) * width] = tile
    spread = coef_ref[2:3, 0:1]
    wave_ref[:, chans // ROWS * ROWS :, :] = jnp.zeros_like(wave_ref[:, chans // ROWS * ROWS :, :])
    for t in range(lat // GROUP):
        lines = [noise_ref[pl.ds(GROUP * t + i, chans, stride=lat), :] * spread for i in range(GROUP)]
        for q, line in enumerate(swapped(lines)):
            wave_ref[q, 0:chans, t * width : (t + 1) * width] = line
    for m in range(GROUP):
        waves[m][...] = wave_ref[lax.bitwise_xor(me, m)]


def lat_shifted(x, pitch, first):
    lane = lanes_of(x)
    slots = x.shape[1] // pitch
    zero = jnp.zeros_like(x)
    final = (first - 1) % slots
    below = jnp.where(between(lane, first * pitch, (first + 1) * pitch), zero, roll(x, pitch))
    above = jnp.where(between(lane, final * pitch, (final + 1) * pitch), zero, roll(x, -pitch))
    return below, above


def scores_of(strips, shifts, firsts, w_in_ref, w_out_ref, pitch):
    strip = strips[0].shape[1]
    rows = w_out_ref.shape[0] // 3
    stacks = []
    for x, first in zip(strips, firsts):
        x = x.astype(BF16)
        stack = []
        for moved in (roll(x, 1), x, roll(x, -1)):
            below, above = lat_shifted(moved, pitch, first)
            stack += [below, moved, above]
        stacks.append(jnp.concatenate(stack, axis=0))
    pre = jnp.dot(w_in_ref[...], jnp.concatenate(stacks, axis=1), preferred_element_type=F32)
    hiddens = []
    for i, shift in enumerate(shifts):
        value = pre[:, i * strip : (i + 1) * strip] + shift
        hidden = (value / (1.0 + jnp.exp(-value))).astype(BF16)
        hiddens.append(jnp.concatenate([roll(hidden, 1), hidden, roll(hidden, -1)], axis=0))
    out = jnp.dot(w_out_ref[...], jnp.concatenate(hiddens, axis=1), preferred_element_type=F32)
    scores = []
    for i, first in enumerate(firsts):
        lines = out[:, i * strip : (i + 1) * strip]
        below, _ = lat_shifted(lines[:rows], pitch, first)
        _, above = lat_shifted(lines[2 * rows :], pitch, first)
        scores.append(lines[rows : 2 * rows] + below + above)
    return scores


def edged(strip, edges, pitch, turn, source, target, count, chosen=None):
    width = edges.shape[1]
    lat = strip.shape[1] // pitch
    lane = lanes_of(strip)
    moves = {}
    for l in range(lat):
        slot = (l + turn) % lat
        moves.setdefault((slot * pitch + target - SLOT * l - source) % width, []).append(slot)
    for shift, slots in moves.items():
        moved = jnp.concatenate([roll(edges, shift)] * (strip.shape[1] // width), axis=1)
        mask = None
        for slot in slots:
            here = between(lane, slot * pitch + target, slot * pitch + target + count)
            mask = here if mask is None else jnp.logical_or(mask, here)
        if chosen is not None:
            mask = jnp.logical_and(mask, chosen)
        strip = jnp.where(mask, moved, strip)
    return strip


def first_kernel(lat, coef_ref, x_ref, n_ref, before_ref, after_ref, column_ref, w_in_ref, w_out_ref, *refs):
    outs = refs[:GROUP]
    (inc_ref,) = refs[GROUP:]
    rows = n_ref.shape[1]
    strip = n_ref.shape[2]
    width = before_ref.shape[1]
    sub = width // GROUP
    pitch = strip // lat
    turn = turn_of(pitch, sub, width)
    me = lax.rem(lax.axis_index("lvl"), GROUP)
    half, drift, spread, time = [coef_ref[r : r + 1, 0:1] for r in range(4)]
    shift = column_ref[...] * time
    before = before_ref[...]
    after = after_ref[...]
    tail = x_ref.shape[1] - rows
    for part in range(GROUP // 2):
        quarters = (2 * part, 2 * part + 1)
        strips = []
        others = []
        for q in quarters:
            x = x_ref[q, 0:rows]
            noise = n_ref[q]
            if q == 0:
                x = edged(x, before, pitch, turn * q, 0, 0, 4)
                noise = edged(noise, before, pitch, turn * q, 4, 2, 2)
            if q == GROUP - 1:
                x = edged(x, after, pitch, turn * q, 4, pitch - EDGE, 4)
                noise = edged(noise, after, pitch, turn * q, 0, pitch - EDGE, 2)
            strips.append(jnp.concatenate([x, jnp.zeros((tail, strip), F32)], axis=0))
            others.append(x * half + noise * spread)
        firsts = [(turn * q) % lat for q in quarters]
        scores = scores_of(strips, [shift, shift], firsts, w_in_ref, w_out_ref, pitch)
        for q, score, other in zip(quarters, scores, others):
            inc_ref[q] = roll(other + drift * score, -pitch * turn * q)
    for m in range(GROUP):
        outs[m][...] = inc_ref[lax.bitwise_xor(me, m)]


def base_kernel(lat, anchor_ref, before_ref, after_ref, *refs):
    incs = refs[:GROUP]
    base_ref, tight_ref, inc_ref, anc_ref = refs[GROUP:]
    chans = anchor_ref.shape[0] // lat
    width = anchor_ref.shape[1]
    sub = width // GROUP
    strip = base_ref.shape[2]
    pitch = strip // lat
    me = lax.rem(lax.axis_index("lvl"), GROUP)
    for m in range(GROUP):
        inc_ref[lax.bitwise_xor(me, m)] = incs[m][...]
    anc_ref[chans // ROWS * ROWS :, :] = jnp.zeros_like(anc_ref[chans // ROWS * ROWS :, :])
    tight_ref[chans // ROWS * ROWS :, :] = jnp.zeros_like(tight_ref[chans // ROWS * ROWS :, :])
    turned = []
    for l in range(lat):
        turned.append(pltpu.roll(anchor_ref[pl.ds(l, chans, stride=lat), :], lax.rem(width - me * sub, width), 1))
    for t, tile in enumerate(tiled([roll(line, pitch * l + EDGE) for l, line in enumerate(turned)], pitch, 0)):
        anc_ref[0:chans, t * width : (t + 1) * width] = tile
    block = lanes_of(turned[0]) // sub
    for t in range(lat // GROUP):
        tile = turned[GROUP * t]
        for i in range(1, GROUP):
            tile = jnp.where(block == i, roll(turned[GROUP * t + i], i * sub), tile)
        tight_ref[0:chans, t * width : (t + 1) * width] = tile
    state = edged(anc_ref[...], before_ref[...], pitch, 0, 6, 2, 2, me == 0)
    state = edged(state, after_ref[...], pitch, 0, 2, pitch - EDGE, 2, me == GROUP - 1)
    for j in range(GROUP):
        base_ref[j] = state
        if j + 1 < GROUP:
            state = state + inc_ref[j]


def second_kernel(
    lat, coef_ref, base_ref, tight_ref, column_ref, w_in_ref, w_out_ref, carry_ref, *refs,
):
    waves = refs[:GROUP]
    outs = refs[GROUP : 2 * GROUP]
    total_ref, wave_ref = refs[2 * GROUP :]
    rows, strip = carry_ref.shape
    pitch = strip // lat
    width = coef_ref.shape[1]
    sub = width // GROUP
    me = lax.rem(lax.axis_index("lvl"), GROUP)
    for m in range(GROUP):
        wave_ref[lax.bitwise_xor(me, m)] = waves[m][...]
    tail = w_in_ref.shape[1] // 9 - rows
    carry = carry_ref[...]

    def packed(block):
        tiles = [block[:, t * width : (t + 1) * width] for t in range(strip // width)]
        lane = lanes_of(tiles[0])
        outs = []
        for l in range(lat):
            low = l * pitch + EDGE
            piece = tiles[low // width]
            if (low + sub - 1) // width != low // width:
                piece = jnp.where(lane >= low % width, piece, tiles[low // width + 1])
            moved = roll(piece, (l % GROUP) * sub - low)
            outs.append(moved if l % GROUP == 0 else jnp.where(lane >= (l % GROUP) * sub, moved, outs.pop()))
        return jnp.concatenate(outs, axis=1)

    running = jnp.zeros_like(total_ref)
    for part in range(GROUP // 2):
        levels = (2 * part, 2 * part + 1)
        states = [base_ref[j] + carry for j in levels]
        strips = [jnp.concatenate([x, jnp.zeros((tail, strip), F32)], axis=0) for x in states]
        coefs = [[coef_ref[COEFS * (j + 1) + r : COEFS * (j + 1) + r + 1, 0:1] for r in range(4)] for j in levels]
        shifts = [column_ref[...] * coef[3] for coef in coefs]
        scores = scores_of(strips, shifts, [0, 0], w_in_ref, w_out_ref, pitch)
        for j, x, score, coef in zip(levels, states, scores, coefs):
            running = running + (packed(x * coef[0] + score * coef[1]) + wave_ref[j])
            wave_ref[j] = tight_ref[...] + running
    total_ref[...] = running
    for m in range(GROUP):
        outs[m][...] = wave_ref[lax.bitwise_xor(me, m)]


def last_kernel(lat, *refs):
    parts = refs[:GROUP]
    out_any, all_ref, line_ref, sems = refs[GROUP:]
    chans = line_ref.shape[0] // lat
    width = line_ref.shape[1]
    me = lax.rem(lax.axis_index("lvl"), GROUP)
    for m in range(GROUP):
        all_ref[lax.bitwise_xor(me, m)] = parts[m][...]
    size = up_to(-(-chans // 3), ROWS)
    copies = []
    for i, low in enumerate(range(0, chans, size)):
        high = min(low + size, chans)
        for t in range(lat // GROUP):
            lanes = slice(t * width, (t + 1) * width)
            lines = swapped([all_ref[q, low:high, lanes] for q in range(GROUP)])
            for k, line in enumerate(lines):
                line_ref[pl.ds(low * lat + GROUP * t + k, high - low, stride=lat), :] = line
        spot = pl.ds(low * lat, (high - low) * lat)
        copies.append(pltpu.make_async_copy(line_ref.at[spot], out_any.at[spot], sems.at[i]))
        copies[-1].start()
    for copy in copies:
        copy.wait()


def exchange(pieces):
    count = lax.axis_size("lvl")
    got = [pieces[0]]
    for m in range(1, GROUP):
        got.append(lax.ppermute(pieces[m], "lvl", [(k, k ^ m) for k in range(count)]))
    return got


def carried(total, block):
    count = lax.axis_size("lvl")
    blocks = count // GROUP
    carry = jnp.zeros_like(total)
    for s in range(1, blocks):
        moved = lax.ppermute(total, "lvl", [(k, (k + s * GROUP) % count) for k in range(count)])
        carry = carry + jnp.where(block >= s, moved, 0.0)
    return carry


def body(window, anchor, noise, conv_in, conv_out, time_shift, plan, start):
    _, lat, chans, width = window.shape
    hid = conv_in.shape[2]
    block = lax.axis_index("lvl") // GROUP
    sub = width // GROUP
    strip = lat * (sub + 2 * EDGE)
    rows = up_to(chans, ROWS)
    deep = up_to(chans, PACK)

    def native(x):
        return jnp.transpose(x.reshape(lat, chans, width), (1, 0, 2)).reshape(chans * lat, width)

    win = native(window)
    noi = native(noise)
    anc = native(anchor)
    edge = (rows, SLOT * lat)
    wide = (rows, strip)
    tight = (rows, lat * sub)
    flops = 2 * 9 * chans * hid * 2 * lat * width
    whole = pltpu.VMEM((chans * lat, width), F32)

    first, last = call(
        functools.partial(edges_kernel, lat),
        [edge, edge],
        [ANY] * 3,
        [whole] * 3 + [pltpu.SemaphoreType.DMA((3,))],
        1 << 20,
        8,
    )(win, noi, anc)
    count = lax.axis_size("lon")
    before = lax.ppermute(last, "lon", [(k, (k + 1) % count) for k in range(count)])
    after = lax.ppermute(first, "lon", [((k + 1) % count, k) for k in range(count)])
    w_in, w_out, column, coefs, x, n, *waves = call(
        functools.partial(build_kernel, lat),
        [
            jax.ShapeDtypeStruct((hid, 9 * deep), BF16),
            jax.ShapeDtypeStruct((3 * rows, 3 * hid), BF16),
            jax.ShapeDtypeStruct((hid, 1), F32),
            (COEFS * (GROUP + 1), width),
            (GROUP, deep, strip),
            (GROUP,) + wide,
        ]
        + [tight] * GROUP,
        [SM, SM] + [VM] * 5,
        [pltpu.VMEM((9 * deep, hid), F32), pltpu.VMEM((3 * rows, 3 * hid), F32), pltpu.VMEM((GROUP,) + tight, F32)],
        flops // 4,
        12,
    )(start, plan, jnp.swapaxes(conv_in, 2, 3), conv_out, time_shift.reshape(1, hid), win, noi)
    incs = call(
        functools.partial(first_kernel, lat),
        [wide] * GROUP,
        [VM] * 8,
        [pltpu.VMEM((GROUP,) + wide, F32)],
        flops,
        20,
    )(coefs, x, n, before, after, column, w_in, w_out)
    incs = exchange(incs)
    total = incs[0] + incs[1] + incs[2] + incs[3]
    carry = carried(total, block)
    waves = exchange(waves)
    base, packed = call(
        functools.partial(base_kernel, lat),
        [(GROUP,) + wide, tight],
        [VM] * (3 + GROUP),
        [pltpu.VMEM((GROUP,) + wide, F32), pltpu.VMEM(wide, F32)],
        flops // 4,
        12,
    )(anc, before, after, *incs)
    done = call(
        functools.partial(second_kernel, lat),
        [tight] * (GROUP + 1),
        [VM] * (7 + GROUP),
        [pltpu.VMEM((GROUP,) + tight, F32)],
        flops,
        20,
    )(coefs, base, packed, column, w_in, w_out, carry, *waves)
    carry = carried(done[GROUP], block)
    parts = exchange([part + carry for part in done[:GROUP]])
    (out,) = call(
        functools.partial(last_kernel, lat),
        [(chans * lat, width)],
        [VM] * GROUP,
        [pltpu.VMEM((GROUP,) + tight, F32), whole, pltpu.SemaphoreType.DMA((3,))],
        1 << 20,
        8,
        [ANY],
    )(*parts)
    return jnp.transpose(out.reshape(chans, lat, width), (1, 0, 2))[None]


def solution(mesh):
    return jax.shard_map(
        body,
        mesh=mesh,
        in_specs=(
            P("lvl", None, None, "lon"),
            P(None, None, "lon"),
            P("lvl", None, None, "lon"),
            P(),
            P(),
            P(),
            P(),
            P(),
        ),
        out_specs=P("lvl", None, None, "lon"),
        check_vma=False,
    )
```

time: 135 us -> 62.8 us (0.47)
  blocking collectives: 78.9 us -> 0 us
  matrix products: 17.5 us -> 0 us
  waiting for transfers between devices: 12.5 us -> 27.8 us
  Pallas kernels: 0 us -> 11.7 us
  starting transfers between devices: 8.49 us -> 17.1 us
  local copies, waits for them, and re-layouts: 9.75 us -> 4.79 us
  other arithmetic: 3.51 us -> 0.16 us
  between operations: 3.93 us -> 0.8 us
    all_to_all x4 -> x0, blocking collectives: 78.9 us -> none  [the longest x2 41.3 us: body(): lax.all_to_all(increment, 'lvl', split_axis=1, concat_axis=0, tiled=True)]
    dot_general x36 -> x0, matrix products: 17.5 us -> none  [convolve(): jnp.einsum('oc,vlcn->vlon', weight[a, b], piece, preferred_element_type=j...]
    ppermute x8 -> x13, waiting for transfers between devices: 12.5 us -> 27.8 us  [the longest x9 17.2 us: exchange(): lax.ppermute(pieces[m], 'lvl', [(k, k ^ m) for k in range(count)])]
    pallas_call x0 -> x6, Pallas kernels: none -> 11.7 us  [the longest x1 3.86 us: body(): call(functools.partial(second_kernel, lat), [tight] * (GROUP + 1), [VM] *...]
    ppermute x8 -> x13, starting transfers between devices: 8.49 us -> 17.1 us  [the longest x9 11 us: exchange(): lax.ppermute(pieces[m], 'lvl', [(k, k ^ m) for k in range(count)])]
    slice x11 -> x0, local copies, waits for them, and re-layouts: 3.19 us -> none  [the longest x6 1.71 us: extended(): lax.slice_in_dim(block, block.shape[dim] - width, None, axis=dim)]
    concatenate x4 -> x0, other arithmetic: 2.58 us -> none  [extended(): block = jnp.concatenate([low, block, high], axis=dim)]
    unnamed x23 -> x20, local copies, waits for them, and re-layouts: 2.25 us -> 4.79 us
  transfers between devices with their start and end apart: 8 -> 13, of which waited for: 4 -> 10; matrix products, arithmetic and copies ran while one was open for 2% -> 0% of each run, Pallas kernels for 0% -> 4%
where the time goes in v3:
time: 62.8 us; the launch traced here: 62.5 us
  waiting for transfers between devices  27.8 us (44%)
  starting transfers between devices  17.1 us (27%)
  Pallas kernels  11.7 us (19%)
  local copies, waits for them, and re-layouts  4.79 us (8%)
  between operations  0.8 us (1%)
    ppermute x9, waiting for transfers between devices, exchange(): lax.ppermute(pieces[m], 'lvl', [(k, k ^ m) for k in range(count)])  17.2 us
    ppermute x9, starting transfers between devices, exchange(): lax.ppermute(pieces[m], 'lvl', [(k, k ^ m) for k in range(count)])  11 us
    ppermute x2, waiting for transfers between devices, carried(): lax.ppermute(total, 'lvl', [(k, (k + s * GROUP) % count) for k in range(c...  10.7 us
    unnamed x20, local copies, waits for them, and re-layouts  4.79 us
    pallas_call x1, Pallas kernels, body(): call(functools.partial(second_kernel, lat), [tight] * (GROUP + 1), [VM] *...  3.86 us
    ppermute x2, starting transfers between devices, carried(): lax.ppermute(total, 'lvl', [(k, (k + s * GROUP) % count) for k in range(c...  3.64 us
    pallas_call x1, Pallas kernels, body(): call(functools.partial(first_kernel, lat), [wide] * GROUP, [VM] * 8, [plt...  3.44 us
    ppermute x1, starting transfers between devices, body(): lax.ppermute(first, 'lon', [((k + 1) % count, k) for k in range(count)])  1.98 us
  transfers between devices with their start and end apart: 13, of which 10 were waited for; matrix products, arithmetic and copies ran while one was open for 0% of the time, Pallas kernels for 4%

profile of v3, /device:TPU:0, one launch (start us, length us, event | category | flops | bytes accessed | tf_op | source)
XLA Modules:
  0.0 62.5 jit_solution(15621855182956317455)
XLA Ops:
  0.0 1.1 %copy-done = f32[1,16,69,128]{3,1,2,0:T(8,128)S(1)} copy-done((f32[1,16,69,128]{3,1,2,0:T(8,128)S(1)}, f32[1,16,69,128]{3,1,2,0:T(8,128)}, u32[]{:S(2)}) %copy-start) | copy-done | bytes 565272
  1.1 1.1 %copy-done.2 = f32[1,16,69,128]{3,1,2,0:T(8,128)S(1)} copy-done((f32[1,16,69,128]{3,1,2,0:T(8,128)S(1)}, f32[1,16,69,128]{3,1,2,0:T(8,128)}, u32[]{:S(2)}) %copy-start.2) | copy-done | bytes 565272
  2.1 1.1 %copy-done.4 = f32[16,69,128]{2,0,1:T(8,128)S(1)} copy-done((f32[16,69,128]{2,0,1:T(8,128)S(1)}, f32[16,69,128]{2,0,1:T(8,128)}, u32[]{:S(2)}) %copy-start.4) | copy-done | bytes 565272
  3.2 1.1 %shard_map.83 = (f32[72,128]{1,0:T(8,128)S(1)}, f32[72,128]{1,0:T(8,128)S(1)}) custom-call(f32[1104,128]{1,0:T(8,128)S(1)} %bitcast.20, f32[1104,128]{1,0:T(8,128)S(1)} %bitcast.22, f32[1104,128]{1,0:T(8,128)S(1)} %bitcast.24), custom_call_target="tpu_custom_call" | custom-call | flops 1048576 | bytes 4194304 | tf_op jit(solution)/shard_map/pallas_call | solution.py:415
  4.8 2.0 %collective-permute-start.1 = (f32[72,128]{1,0:T(8,128)S(1)}, f32[72,128]{1,0:T(8,128)S(1)}, u32[]{:S(2)}, u32[]{:S(2)}) collective-permute-start(f32[72,128]{1,0:T(8,128)S(1)} %get-tuple-element.30), channel_id=1, source_target_pairs={{1,0},{2,1},{3,2},{0,3},{5,4},{6,5},{7,6},{4,7},{9,8},{10,9},{11,1... | collective-permute-start | bytes 110600 | tf_op jit(solution)/shard_map/ppermute | solution.py:425
  9.1 1.7 %shard_map.82 = (bf16[192,720]{1,0:T(8,128)(2,1)S(1)}, bf16[216,576]{1,0:T(8,128)(2,1)S(1)}, f32[192,1]{1,0:T(8,128)S(1)}, f32[40,128]{1,0:T(8,128)S(1)}, f32[4,...) custom-call(s32[1]{0:T(128)S(6)} %copy.9.start_ref, ...), custom_call_target="tpu_custom_call" | custom-call | flops 244187136 | bytes 4194304 | tf_op jit(solution)/shard_map/pallas_call | solution.py:426
  10.8 3.4 %shard_map.84 = (f32[72,640]{1,0:T(8,128)S(1)}, f32[72,640]{1,0:T(8,128)S(1)}, f32[72,640]{1,0:T(8,128)S(1)}, f32[72,640]{1,0:T(8,128)S(1)}) custom-call(f32[40,128]{1,0:T(8,128)S(1)} %get-tuple-element.28.coef_ref, f32[4,80,640]{2,1,0:T(8,128)S(1)} %get-tuple-element.31.x_ref, f32[4,72,640]{2,1,0:T(8,128)S(1)} %get-tuple-element.32.n_ref, ...), custom_call_target="tpu_custom_call" | custom-call | flops 976748544 | bytes 4194304 | tf_op jit(solution)/shard_map/pallas_call | solution.py:442
  14.3 2.3 %collective-permute-start.2 = (f32[72,640]{1,0:T(8,128)S(1)}, f32[72,640]{1,0:T(8,128)S(1)}, u32[]{:S(2)}, u32[]{:S(2)}) collective-permute-start(f32[72,640]{1,0:T(8,128)S(1)} %get-tuple-element.37), channel_id=1, source_target_pairs={{0,4},{4,0},{8,12},{12,8},{16,20},{20,16},{24,28},{28,24},{1,5},{5... | collective-permute-start | bytes 552968 | tf_op jit(solution)/shard_map/ppermute | solution.py:380
  16.6 1.6 %collective-permute-start.3 = (f32[72,640]{1,0:T(8,128)S(1)}, f32[72,640]{1,0:T(8,128)S(1)}, u32[]{:S(2)}, u32[]{:S(2)}) collective-permute-start(f32[72,640]{1,0:T(8,128)S(1)} %get-tuple-element.38), channel_id=1, source_target_pairs={{0,8},{4,12},{8,0},{12,4},{16,24},{20,28},{24,16},{28,20},{1,9},{5... | collective-permute-start | bytes 552968 | tf_op jit(solution)/shard_map/ppermute | solution.py:380
  18.2 3.3 %collective-permute-done.2.refs_1_ = f32[72,640]{1,0:T(8,128)S(1)} collective-permute-done((f32[72,640]{1,0:T(8,128)S(1)}, f32[72,640]{1,0:T(8,128)S(1)}, u32[]{:S(2)}, u32[]{:S(2)}) %collective-permute-start.2) | collective-permute-done | bytes 184352 | tf_op jit(solution)/shard_map/ppermute | solution.py:380
  21.5 2.6 %collective-permute-done.3.refs_2_ = f32[72,640]{1,0:T(8,128)S(1)} collective-permute-done((f32[72,640]{1,0:T(8,128)S(1)}, f32[72,640]{1,0:T(8,128)S(1)}, u32[]{:S(2)}, u32[]{:S(2)}) %collective-permute-start.3) | collective-permute-done | bytes 184352 | tf_op jit(solution)/shard_map/ppermute | solution.py:380
  24.1 2.5 %collective-permute-done.4.refs_3_ = f32[72,640]{1,0:T(8,128)S(1)} collective-permute-done((f32[72,640]{1,0:T(8,128)S(1)}, f32[72,640]{1,0:T(8,128)S(1)}, u32[]{:S(2)}, u32[]{:S(2)}) %collective-permute-start.4) | collective-permute-done | bytes 184352 | tf_op jit(solution)/shard_map/ppermute | solution.py:380
  26.7 2.7 %collective-permute-start.5 = (f32[72,640]{1,0:T(8,128)S(1)}, f32[72,640]{1,0:T(8,128)S(1)}, u32[]{:S(2)}, u32[]{:S(2)}) collective-permute-start(f32[72,640]{1,0:T(8,128)S(1)} %add_add_fusion), channel_id=1, source_target_pairs={{0,16},{4,20},{8,24},{12,28},{16,0},{20,4},{24,8},{28,12},{1,17},{... | collective-permute-start | bytes 552968 | tf_op jit(solution)/shard_map/ppermute | solution.py:389
  29.4 1.5 %collective-permute-start.6 = (f32[72,512]{1,0:T(8,128)S(1)}, f32[72,512]{1,0:T(8,128)S(1)}, u32[]{:S(2)}, u32[]{:S(2)}) collective-permute-start(f32[72,512]{1,0:T(8,128)S(1)} %get-tuple-element.43), channel_id=1, source_target_pairs={{0,4},{4,0},{8,12},{12,8},{16,20},{20,16},{24,28},{28,24},{1,5},{5... | collective-permute-start | bytes 442376 | tf_op jit(solution)/shard_map/ppermute | solution.py:380
  30.9 1.6 %collective-permute-start.7 = (f32[72,512]{1,0:T(8,128)S(1)}, f32[72,512]{1,0:T(8,128)S(1)}, u32[]{:S(2)}, u32[]{:S(2)}) collective-permute-start(f32[72,512]{1,0:T(8,128)S(1)} %get-tuple-element.44), channel_id=1, source_target_pairs={{0,8},{4,12},{8,0},{12,4},{16,24},{20,28},{24,16},{28,20},{1,9},{5... | collective-permute-start | bytes 442376 | tf_op jit(solution)/shard_map/ppermute | solution.py:380
  33.5 3.8 %collective-permute-done.5 = f32[72,640]{1,0:T(8,128)S(1)} collective-permute-done((f32[72,640]{1,0:T(8,128)S(1)}, f32[72,640]{1,0:T(8,128)S(1)}, u32[]{:S(2)}, u32[]{:S(2)}) %collective-permute-start.5) | collective-permute-done | bytes 184352 | tf_op jit(solution)/shard_map/ppermute | solution.py:389
  37.3 2.2 %collective-permute-done.7.refs_2_ = f32[72,512]{1,0:T(8,128)S(1)} collective-permute-done((f32[72,512]{1,0:T(8,128)S(1)}, f32[72,512]{1,0:T(8,128)S(1)}, u32[]{:S(2)}, u32[]{:S(2)}) %collective-permute-start.7) | collective-permute-done | bytes 147488 | tf_op jit(solution)/shard_map/ppermute | solution.py:380
  39.6 1.4 %collective-permute-done.8.refs_3_ = f32[72,512]{1,0:T(8,128)S(1)} collective-permute-done((f32[72,512]{1,0:T(8,128)S(1)}, f32[72,512]{1,0:T(8,128)S(1)}, u32[]{:S(2)}, u32[]{:S(2)}) %collective-permute-start.8) | collective-permute-done | bytes 147488 | tf_op jit(solution)/shard_map/ppermute | solution.py:380
  40.9 3.9 %shard_map.86 = (f32[72,512]{1,0:T(8,128)S(1)}, f32[72,512]{1,0:T(8,128)S(1)}, f32[72,512]{1,0:T(8,128)S(1)}, f32[72,512]{1,0:T(8,128)S(1)}, f32[72,512]{1,0:T(8,128)S(1)}) custom-call(f32[40,128]{1,0:T(8,128)S(1)} %get-tuple-element.28.coef_ref, f32[4,72,640]{2,1,0:T(8,128)S(1)} %get-tuple-element.40.base_ref, f32[72,512]{1,0:T(8,128)S(1)} %get-tuple-element.41.tight_ref, ...), custom_call_target="tpu_custom_call" | custom-call | flops 976748544 | bytes 4194304 | tf_op jit(solution)/shard_map/pallas_call | solution.py:462
  45.8 6.9 %collective-permute-done.9 = f32[72,512]{1,0:T(8,128)S(1)} collective-permute-done((f32[72,512]{1,0:T(8,128)S(1)}, f32[72,512]{1,0:T(8,128)S(1)}, u32[]{:S(2)}, u32[]{:S(2)}) %collective-permute-start.9) | collective-permute-done | bytes 147488 | tf_op jit(solution)/shard_map/ppermute | solution.py:389
  52.7 1.4 %collective-permute-start.10 = (f32[72,512]{1,0:T(8,128)S(1)}, f32[72,512]{1,0:T(8,128)S(1)}, u32[]{:S(2)}, u32[]{:S(2)}) collective-permute-start(f32[72,512]{1,0:T(8,128)S(1)} %get-tuple-element.52), channel_id=1, source_target_pairs={{0,4},{4,0},{8,12},{12,8},{16,20},{20,16},{24,28},{28,24},{1,5},{5... | collective-permute-start | bytes 442376 | tf_op jit(solution)/shard_map/ppermute | solution.py:380
  54.2 2.1 %collective-permute-start.12 = (f32[72,512]{1,0:T(8,128)S(1)}, f32[72,512]{1,0:T(8,128)S(1)}, u32[]{:S(2)}, u32[]{:S(2)}) collective-permute-start(f32[72,512]{1,0:T(8,128)S(1)} %get-tuple-element.51), channel_id=1, source_target_pairs={{0,12},{4,8},{8,4},{12,0},{16,28},{20,24},{24,20},{28,16},{1,13},{... | collective-permute-start | bytes 442376 | tf_op jit(solution)/shard_map/ppermute | solution.py:380
  56.3 3.2 %collective-permute-done.10.refs_1_ = f32[72,512]{1,0:T(8,128)S(1)} collective-permute-done((f32[72,512]{1,0:T(8,128)S(1)}, f32[72,512]{1,0:T(8,128)S(1)}, u32[]{:S(2)}, u32[]{:S(2)}) %collective-permute-start.10) | collective-permute-done | bytes 147488 | tf_op jit(solution)/shard_map/ppermute | solution.py:380
  60.0 1.4 %collective-permute-done.12.refs_3_ = f32[72,512]{1,0:T(8,128)S(1)} collective-permute-done((f32[72,512]{1,0:T(8,128)S(1)}, f32[72,512]{1,0:T(8,128)S(1)}, u32[]{:S(2)}, u32[]{:S(2)}) %collective-permute-start.12) | collective-permute-done | bytes 147488 | tf_op jit(solution)/shard_map/ppermute | solution.py:380
  (31 shorter events, 5.9 us)
Async XLA Ops:
  0.0 1.1 %copy-start = (f32[1,16,69,128]{3,1,2,0:T(8,128)S(1)}, f32[1,16,69,128]{3,1,2,0:T(8,128)}, u32[]{:S(2)}) copy-start(f32[1,16,69,128]{3,1,2,0:T(8,128)} %param.8) | copy-start | bytes 1695748
  1.1 1.1 %copy-start.2 = (f32[1,16,69,128]{3,1,2,0:T(8,128)S(1)}, f32[1,16,69,128]{3,1,2,0:T(8,128)}, u32[]{:S(2)}) copy-start(f32[1,16,69,128]{3,1,2,0:T(8,128)} %param.10) | copy-start | bytes 1695748
  2.1 1.1 %copy-start.4 = (f32[16,69,128]{2,0,1:T(8,128)S(1)}, f32[16,69,128]{2,0,1:T(8,128)}, u32[]{:S(2)}) copy-start(f32[16,69,128]{2,0,1:T(8,128)} %param.9) | copy-start | bytes 1695748
  3.2 4.3 %copy-start.1 = (f32[1,16,69,128]{3,1,2,0:T(8,128)S(1)}, f32[1,16,69,128]{3,1,2,0:T(8,128)}, u32[]{:S(2)}) copy-start(f32[1,16,69,128]{3,1,2,0:T(8,128)} %param.8) | copy-start | bytes 1695748
  3.2 4.3 %copy-start.3 = (f32[1,16,69,128]{3,1,2,0:T(8,128)S(1)}, f32[1,16,69,128]{3,1,2,0:T(8,128)}, u32[]{:S(2)}) copy-start(f32[1,16,69,128]{3,1,2,0:T(8,128)} %param.10) | copy-start | bytes 1695748
  3.2 4.3 %copy-start.6 = (bf16[3,3,192,69]{2,3,1,0:T(8,128)(2,1)S(1)}, bf16[3,3,192,69]{2,3,1,0:T(8,128)(2,1)}, u32[]{:S(2)}) copy-start(bf16[3,3,192,69]{2,3,1,0:T(8,128)(2,1)} %param.11) | copy-start | bytes 715396
  3.2 4.3 %copy-start.9 = (f32[192]{0:T(256)S(1)}, f32[192]{0:T(256)}, u32[]{:S(2)}) copy-start(f32[192]{0:T(256)} %param.13) | copy-start | bytes 2308
  4.3 6.5 %collective-permute-start = (f32[72,128]{1,0:T(8,128)S(1)}, f32[72,128]{1,0:T(8,128)S(1)}, u32[]{:S(2)}, u32[]{:S(2)}) collective-permute-start(f32[72,128]{1,0:T(8,128)S(1)} %get-tuple-element.29), channel_id=1, source_target_pairs={{0,1},{1,2},{2,3},{3,0},{4,5},{5,6},{6,7},{7,4},{8,9},{9,10},{10,1... | collective-permute-start | bytes 110600 | tf_op jit(solution)/shard_map/ppermute | solution.py:424
  4.8 6.0 %collective-permute-start.1 = (f32[72,128]{1,0:T(8,128)S(1)}, f32[72,128]{1,0:T(8,128)S(1)}, u32[]{:S(2)}, u32[]{:S(2)}) collective-permute-start(f32[72,128]{1,0:T(8,128)S(1)} %get-tuple-element.30), channel_id=1, source_target_pairs={{1,0},{2,1},{3,2},{0,3},{5,4},{6,5},{7,6},{4,7},{9,8},{10,9},{11,1... | collective-permute-start | bytes 110600 | tf_op jit(solution)/shard_map/ppermute | solution.py:425
  7.4 0.7 %copy-start.8 = (s32[256]{0:T(256)S(1)}, s32[256]{0:T(256)}, u32[]{:S(2)}) copy-start(s32[256]{0:T(256)} %plan_ref.1) | copy-start | bytes 3076
  8.1 1.0 %copy-start.7 = (bf16[3,3,69,192]{3,2,1,0:T(8,128)(2,1)S(1)}, bf16[3,3,69,192]{3,2,1,0:T(8,128)(2,1)}, u32[]{:S(2)}) copy-start(bf16[3,3,69,192]{3,2,1,0:T(8,128)(2,1)} %conv_out_ref.1) | copy-start | bytes 715396
  14.3 18.6 %copy-start.5 = (f32[16,69,128]{2,0,1:T(8,128)S(1)}, f32[16,69,128]{2,0,1:T(8,128)}, u32[]{:S(2)}) copy-start(f32[16,69,128]{2,0,1:T(8,128)} %param.9) | copy-start | bytes 1695748
  14.3 7.2 %collective-permute-start.2 = (f32[72,640]{1,0:T(8,128)S(1)}, f32[72,640]{1,0:T(8,128)S(1)}, u32[]{:S(2)}, u32[]{:S(2)}) collective-permute-start(f32[72,640]{1,0:T(8,128)S(1)} %get-tuple-element.37), channel_id=1, source_target_pairs={{0,4},{4,0},{8,12},{12,8},{16,20},{20,16},{24,28},{28,24},{1,5},{5... | collective-permute-start | bytes 552968 | tf_op jit(solution)/shard_map/ppermute | solution.py:380
  16.6 7.5 %collective-permute-start.3 = (f32[72,640]{1,0:T(8,128)S(1)}, f32[72,640]{1,0:T(8,128)S(1)}, u32[]{:S(2)}, u32[]{:S(2)}) collective-permute-start(f32[72,640]{1,0:T(8,128)S(1)} %get-tuple-element.38), channel_id=1, source_target_pairs={{0,8},{4,12},{8,0},{12,4},{16,24},{20,28},{24,16},{28,20},{1,9},{5... | collective-permute-start | bytes 552968 | tf_op jit(solution)/shard_map/ppermute | solution.py:380
  18.2 8.4 %collective-permute-start.4 = (f32[72,640]{1,0:T(8,128)S(1)}, f32[72,640]{1,0:T(8,128)S(1)}, u32[]{:S(2)}, u32[]{:S(2)}) collective-permute-start(f32[72,640]{1,0:T(8,128)S(1)} %get-tuple-element.39), channel_id=1, source_target_pairs={{0,12},{4,8},{8,4},{12,0},{16,28},{20,24},{24,20},{28,16},{1,13},{... | collective-permute-start | bytes 552968 | tf_op jit(solution)/shard_map/ppermute | solution.py:380
  26.7 10.6 %collective-permute-start.5 = (f32[72,640]{1,0:T(8,128)S(1)}, f32[72,640]{1,0:T(8,128)S(1)}, u32[]{:S(2)}, u32[]{:S(2)}) collective-permute-start(f32[72,640]{1,0:T(8,128)S(1)} %add_add_fusion), channel_id=1, source_target_pairs={{0,16},{4,20},{8,24},{12,28},{16,0},{20,4},{24,8},{28,12},{1,17},{... | collective-permute-start | bytes 552968 | tf_op jit(solution)/shard_map/ppermute | solution.py:389
  29.4 8.0 %collective-permute-start.6 = (f32[72,512]{1,0:T(8,128)S(1)}, f32[72,512]{1,0:T(8,128)S(1)}, u32[]{:S(2)}, u32[]{:S(2)}) collective-permute-start(f32[72,512]{1,0:T(8,128)S(1)} %get-tuple-element.43), channel_id=1, source_target_pairs={{0,4},{4,0},{8,12},{12,8},{16,20},{20,16},{24,28},{28,24},{1,5},{5... | collective-permute-start | bytes 442376 | tf_op jit(solution)/shard_map/ppermute | solution.py:380
  30.9 8.7 %collective-permute-start.7 = (f32[72,512]{1,0:T(8,128)S(1)}, f32[72,512]{1,0:T(8,128)S(1)}, u32[]{:S(2)}, u32[]{:S(2)}) collective-permute-start(f32[72,512]{1,0:T(8,128)S(1)} %get-tuple-element.44), channel_id=1, source_target_pairs={{0,8},{4,12},{8,0},{12,4},{16,24},{20,28},{24,16},{28,20},{1,9},{5... | collective-permute-start | bytes 442376 | tf_op jit(solution)/shard_map/ppermute | solution.py:380
  32.5 8.5 %collective-permute-start.8 = (f32[72,512]{1,0:T(8,128)S(1)}, f32[72,512]{1,0:T(8,128)S(1)}, u32[]{:S(2)}, u32[]{:S(2)}) collective-permute-start(f32[72,512]{1,0:T(8,128)S(1)} %get-tuple-element.45), channel_id=1, source_target_pairs={{0,12},{4,8},{8,4},{12,0},{16,28},{20,24},{24,20},{28,16},{1,13},{... | collective-permute-start | bytes 442376 | tf_op jit(solution)/shard_map/ppermute | solution.py:380
  44.8 7.9 %collective-permute-start.9 = (f32[72,512]{1,0:T(8,128)S(1)}, f32[72,512]{1,0:T(8,128)S(1)}, u32[]{:S(2)}, u32[]{:S(2)}) collective-permute-start(f32[72,512]{1,0:T(8,128)S(1)} %get-tuple-element.47), channel_id=1, source_target_pairs={{0,16},{4,20},{8,24},{12,28},{16,0},{20,4},{24,8},{28,12},{1,17},{... | collective-permute-start | bytes 442376 | tf_op jit(solution)/shard_map/ppermute | solution.py:389
  52.7 6.8 %collective-permute-start.10 = (f32[72,512]{1,0:T(8,128)S(1)}, f32[72,512]{1,0:T(8,128)S(1)}, u32[]{:S(2)}, u32[]{:S(2)}) collective-permute-start(f32[72,512]{1,0:T(8,128)S(1)} %get-tuple-element.52), channel_id=1, source_target_pairs={{0,4},{4,0},{8,12},{12,8},{16,20},{20,16},{24,28},{28,24},{1,5},{5... | collective-permute-start | bytes 442376 | tf_op jit(solution)/shard_map/ppermute | solution.py:380
  54.2 5.8 %collective-permute-start.11 = (f32[72,512]{1,0:T(8,128)S(1)}, f32[72,512]{1,0:T(8,128)S(1)}, u32[]{:S(2)}, u32[]{:S(2)}) collective-permute-start(f32[72,512]{1,0:T(8,128)S(1)} %get-tuple-element.53), channel_id=1, source_target_pairs={{0,8},{4,12},{8,0},{12,4},{16,24},{20,28},{24,16},{28,20},{1,9},{5... | collective-permute-start | bytes 442376 | tf_op jit(solution)/shard_map/ppermute | solution.py:380
  54.2 7.3 %collective-permute-start.12 = (f32[72,512]{1,0:T(8,128)S(1)}, f32[72,512]{1,0:T(8,128)S(1)}, u32[]{:S(2)}, u32[]{:S(2)}) collective-permute-start(f32[72,512]{1,0:T(8,128)S(1)} %get-tuple-element.51), channel_id=1, source_target_pairs={{0,12},{4,8},{8,4},{12,0},{16,28},{20,24},{24,20},{28,16},{1,13},{... | collective-permute-start | bytes 442376 | tf_op jit(solution)/shard_map/ppermute | solution.py:380

commit v4 on v3

--- a/solution.py
+++ b/solution.py
@@ -17,7 +17,7 @@
 
 VM = pl.BlockSpec(memory_space=pltpu.VMEM)
 SM = pl.BlockSpec(memory_space=pltpu.SMEM)
-ANY = pl.BlockSpec(memory_space=pl.ANY)
+HBM = pl.BlockSpec(memory_space=pltpu.HBM)
 F32 = jnp.float32
 BF16 = jnp.bfloat16
 
@@ -34,7 +34,7 @@
         in_specs=specs,
         out_specs=out_specs or [VM] * len(outs),
         scratch_shapes=scratch,
-        compiler_params=pltpu.CompilerParams(vmem_limit_bytes=limit << 20),
+        compiler_params=pltpu.CompilerParams(vmem_limit_bytes=int(limit * (1 << 20))),
         cost_estimate=pl.CostEstimate(flops=flops, bytes_accessed=4 << 20, transcendentals=0),
     )
 
@@ -71,15 +71,41 @@
     return outs
 
 
-def edges_kernel(lat, win_any, noise_any, anchor_any, first_ref, last_ref, win_ref, noise_ref, anchor_ref, sems):
-    copies = [
-        pltpu.make_async_copy(source, target, sems.at[i])
-        for i, (source, target) in enumerate(
-            [(win_any, win_ref), (noise_any, noise_ref), (anchor_any, anchor_ref)]
-        )
+def coefs_of(plan_ref, entry):
+    now = plan_ref[entry].astype(F32)
+    later = plan_ref[entry + 1].astype(F32)
+    beta = 0.1 + 19.9 * now / 1000.0
+    step = (now - later) / 1000.0
+    return [0.5 * beta * step, beta * step, jnp.sqrt(jnp.full((1, 1), beta * step, F32)), now / 1000.0]
+
+
+def edges_kernel(
+    lat, start_ref, plan_hbm, win_hbm, noise_hbm, anchor_hbm, conv_in_hbm, conv_out_hbm, time_hbm,
+    first_ref, last_ref, coef_ref, win_ref, noise_ref, anchor_ref, conv_in_ref, conv_out_ref, time_ref,
+    plan_ref, sems,
+):
+    pairs = [
+        (plan_hbm, plan_ref),
+        (win_hbm, win_ref),
+        (noise_hbm, noise_ref),
+        (anchor_hbm, anchor_ref),
+        (conv_in_hbm, conv_in_ref),
+        (conv_out_hbm, conv_out_ref),
+        (time_hbm, time_ref),
     ]
+    copies = [pltpu.make_async_copy(source, target, sems.at[i]) for i, (source, target) in enumerate(pairs)]
     for copy in copies:
         copy.start()
+    copies[0].wait()
+    copies = copies[1:]
+    level = lax.axis_index("lvl")
+    entries = [level] + [level - lax.rem(level, GROUP) + j for j in range(GROUP)]
+    for i, entry in enumerate(entries):
+        values = coefs_of(plan_ref, start_ref[0] + entry)
+        for r, value in enumerate(values):
+            coef_ref[COEFS * i + r : COEFS * i + r + 1, :] = jnp.broadcast_to(
+                value if r == 2 else jnp.full((1, 1), value, F32), (1, coef_ref.shape[1])
+            )
     chans = win_ref.shape[0] // lat
     tiles = []
     for copy, ref, shift, skip in zip(copies, (win_ref, noise_ref, anchor_ref), (4, 6, 8), (0, 0, 6)):
@@ -97,6 +123,8 @@
     for ref, value in ((first_ref, first), (last_ref, last)):
         ref[...] = jnp.zeros_like(ref)
         ref[0:chans, :] = value
+    for copy in copies[3:]:
+        copy.wait()
 
 
 def tiled(rolled, pitch, turn):
@@ -120,17 +148,9 @@
     return next(k for k in range(width) if (pitch * k) % width == sub)
 
 
-def coefs_of(plan_ref, entry):
-    now = plan_ref[entry].astype(F32)
-    later = plan_ref[entry + 1].astype(F32)
-    beta = 0.1 + 19.9 * now / 1000.0
-    step = (now - later) / 1000.0
-    return [0.5 * beta * step, beta * step, jnp.sqrt(jnp.full((1, 1), beta * step, F32)), now / 1000.0]
-
-
 def build_kernel(
-    lat, start_ref, plan_ref, conv_in_ref, conv_out_ref, time_ref, win_ref, noise_ref,
-    w_in_ref, w_out_ref, column_ref, coef_ref, x_ref, n_ref, *refs,
+    lat, coef_ref, conv_in_ref, conv_out_ref, time_ref, win_ref, noise_ref,
+    w_in_ref, w_out_ref, column_ref, x_ref, n_ref, *refs,
 ):
     waves = refs[:GROUP]
     in_ref, out_ref, wave_ref = refs[GROUP:]
@@ -138,6 +158,16 @@
     width = win_ref.shape[1]
     deep = in_ref.shape[0] // 9
     rows = n_ref.shape[1]
+    sub = width // GROUP
+    pitch = sub + 2 * EDGE
+    turn = turn_of(pitch, sub, width)
+    for source, target in ((win_ref, x_ref), (noise_ref, n_ref)):
+        target[:, chans // ROWS * ROWS :, :] = jnp.zeros_like(target[:, chans // ROWS * ROWS :, :])
+        rolled = [roll(source[pl.ds(l, chans, stride=lat), :], pitch * l + EDGE) for l in range(lat)]
+        for q in range(GROUP):
+            for t, tile in enumerate(tiled(rolled, pitch, turn * q)):
+                target[q, 0:chans, t * width : (t + 1) * width] = tile
+    me = lax.rem(lax.axis_index("lvl"), GROUP)
     in_ref[...] = jnp.zeros_like(in_ref)
     out_ref[...] = jnp.zeros_like(out_ref)
     for b in range(3):
@@ -149,24 +179,6 @@
     w_out_ref[...] = out_ref[...].astype(BF16)
     column_ref[...] = jnp.transpose(jnp.broadcast_to(time_ref[...], (ROWS, hid)))[:, :1]
 
-    level = lax.axis_index("lvl")
-    me = lax.rem(level, GROUP)
-    entries = [level] + [level - me + j for j in range(GROUP)]
-    for i, entry in enumerate(entries):
-        values = coefs_of(plan_ref, start_ref[0] + entry)
-        for r, value in enumerate(values):
-            coef_ref[COEFS * i + r : COEFS * i + r + 1, :] = jnp.broadcast_to(
-                value if r == 2 else jnp.full((1, 1), value, F32), (1, coef_ref.shape[1])
-            )
-    sub = width // GROUP
-    pitch = sub + 2 * EDGE
-    turn = turn_of(pitch, sub, width)
-    for source, target in ((win_ref, x_ref), (noise_ref, n_ref)):
-        target[:, chans // ROWS * ROWS :, :] = jnp.zeros_like(target[:, chans // ROWS * ROWS :, :])
-        rolled = [roll(source[pl.ds(l, chans, stride=lat), :], pitch * l + EDGE) for l in range(lat)]
-        for q in range(GROUP):
-            for t, tile in enumerate(tiled(rolled, pitch, turn * q)):
-                target[q, 0:chans, t * width : (t + 1) * width] = tile
     spread = coef_ref[2:3, 0:1]
     wave_ref[:, chans // ROWS * ROWS :, :] = jnp.zeros_like(wave_ref[:, chans // ROWS * ROWS :, :])
     for t in range(lat // GROUP):
@@ -304,19 +316,11 @@
             state = state + inc_ref[j]
 
 
-def second_kernel(
-    lat, coef_ref, base_ref, tight_ref, column_ref, w_in_ref, w_out_ref, carry_ref, *refs,
-):
-    waves = refs[:GROUP]
-    outs = refs[GROUP : 2 * GROUP]
-    total_ref, wave_ref = refs[2 * GROUP :]
+def second_kernel(lat, coef_ref, base_ref, column_ref, w_in_ref, w_out_ref, carry_ref, sum_ref):
     rows, strip = carry_ref.shape
     pitch = strip // lat
     width = coef_ref.shape[1]
     sub = width // GROUP
-    me = lax.rem(lax.axis_index("lvl"), GROUP)
-    for m in range(GROUP):
-        wave_ref[lax.bitwise_xor(me, m)] = waves[m][...]
     tail = w_in_ref.shape[1] // 9 - rows
     carry = carry_ref[...]
 
@@ -333,7 +337,7 @@
             outs.append(moved if l % GROUP == 0 else jnp.where(lane >= (l % GROUP) * sub, moved, outs.pop()))
         return jnp.concatenate(outs, axis=1)
 
-    running = jnp.zeros_like(total_ref)
+    running = jnp.zeros(sum_ref.shape[1:], F32)
     for part in range(GROUP // 2):
         levels = (2 * part, 2 * part + 1)
         states = [base_ref[j] + carry for j in levels]
@@ -342,9 +346,23 @@
         shifts = [column_ref[...] * coef[3] for coef in coefs]
         scores = scores_of(strips, shifts, [0, 0], w_in_ref, w_out_ref, pitch)
         for j, x, score, coef in zip(levels, states, scores, coefs):
-            running = running + (packed(x * coef[0] + score * coef[1]) + wave_ref[j])
-            wave_ref[j] = tight_ref[...] + running
-    total_ref[...] = running
+            running = running + packed(x * coef[0] + score * coef[1])
+            sum_ref[j] = running
+
+
+def share_kernel(tight_ref, sum_ref, *refs):
+    waves = refs[:GROUP]
+    outs = refs[GROUP : 2 * GROUP]
+    total_ref, wave_ref = refs[2 * GROUP :]
+    me = lax.rem(lax.axis_index("lvl"), GROUP)
+    for m in range(GROUP):
+        wave_ref[lax.bitwise_xor(me, m)] = waves[m][...]
+    noise = jnp.zeros(total_ref.shape, F32)
+    for j in range(GROUP):
+        noise = noise + wave_ref[j]
+        share = sum_ref[j] + noise
+        wave_ref[j] = tight_ref[...] + share
+    total_ref[...] = share
     for m in range(GROUP):
         outs[m][...] = wave_ref[lax.bitwise_xor(me, m)]
 
@@ -403,42 +421,58 @@
     def native(x):
         return jnp.transpose(x.reshape(lat, chans, width), (1, 0, 2)).reshape(chans * lat, width)
 
-    win = native(window)
-    noi = native(noise)
-    anc = native(anchor)
     edge = (rows, SLOT * lat)
     wide = (rows, strip)
     tight = (rows, lat * sub)
     flops = 2 * 9 * chans * hid * 2 * lat * width
-    whole = pltpu.VMEM((chans * lat, width), F32)
-
-    first, last = call(
+    taps = jax.ShapeDtypeStruct((3, 3, chans, hid), BF16)
+    first, last, coefs, win, noi, anc, taps_in, taps_out, time = call(
         functools.partial(edges_kernel, lat),
-        [edge, edge],
-        [ANY] * 3,
-        [whole] * 3 + [pltpu.SemaphoreType.DMA((3,))],
+        [edge, edge, (COEFS * (GROUP + 1), width)] + [(chans * lat, width)] * 3 + [taps, taps, (1, hid)],
+        [SM] + [HBM] * 7,
+        [
+            pltpu.SMEM(plan.shape, plan.dtype),
+            pltpu.SemaphoreType.DMA((7,)),
+        ],
         1 << 20,
         8,
-    )(win, noi, anc)
+    )(
+        start,
+        *(
+            pltpu.with_memory_space_constraint(x, pltpu.HBM)
+            for x in (
+                plan,
+                native(window),
+                native(noise),
+                native(anchor),
+                jnp.swapaxes(conv_in, 2, 3),
+                conv_out,
+                time_shift.reshape(1, hid),
+            )
+        )
+    )
     count = lax.axis_size("lon")
     before = lax.ppermute(last, "lon", [(k, (k + 1) % count) for k in range(count)])
     after = lax.ppermute(first, "lon", [((k + 1) % count, k) for k in range(count)])
-    w_in, w_out, column, coefs, x, n, *waves = call(
+    w_in, w_out, column, x, n, *waves = call(
         functools.partial(build_kernel, lat),
         [
             jax.ShapeDtypeStruct((hid, 9 * deep), BF16),
             jax.ShapeDtypeStruct((3 * rows, 3 * hid), BF16),
             jax.ShapeDtypeStruct((hid, 1), F32),
-            (COEFS * (GROUP + 1), width),
             (GROUP, deep, strip),
             (GROUP,) + wide,
         ]
         + [tight] * GROUP,
-        [SM, SM] + [VM] * 5,
-        [pltpu.VMEM((9 * deep, hid), F32), pltpu.VMEM((3 * rows, 3 * hid), F32), pltpu.VMEM((GROUP,) + tight, F32)],
+        [VM] * 6,
+        [
+            pltpu.VMEM((9 * deep, hid), F32),
+            pltpu.VMEM((3 * rows, 3 * hid), F32),
+            pltpu.VMEM((GROUP,) + tight, F32),
+        ],
         flops // 4,
         12,
-    )(start, plan, jnp.swapaxes(conv_in, 2, 3), conv_out, time_shift.reshape(1, hid), win, noi)
+    )(coefs, taps_in, taps_out, time, win, noi)
     incs = call(
         functools.partial(first_kernel, lat),
         [wide] * GROUP,
@@ -459,24 +493,32 @@
         flops // 4,
         12,
     )(anc, before, after, *incs)
-    done = call(
+    (sums,) = call(
         functools.partial(second_kernel, lat),
-        [tight] * (GROUP + 1),
-        [VM] * (7 + GROUP),
-        [pltpu.VMEM((GROUP,) + tight, F32)],
+        [(GROUP,) + tight],
+        [VM] * 6,
+        [],
         flops,
         20,
-    )(coefs, base, packed, column, w_in, w_out, carry, *waves)
+    )(coefs, base, column, w_in, w_out, carry)
+    done = call(
+        share_kernel,
+        [tight] * (GROUP + 1),
+        [VM] * (2 + GROUP),
+        [pltpu.VMEM((GROUP,) + tight, F32)],
+        1 << 20,
+        4,
+    )(packed, sums, *waves)
     carry = carried(done[GROUP], block)
     parts = exchange([part + carry for part in done[:GROUP]])
     (out,) = call(
         functools.partial(last_kernel, lat),
         [(chans * lat, width)],
         [VM] * GROUP,
-        [pltpu.VMEM((GROUP,) + tight, F32), whole, pltpu.SemaphoreType.DMA((3,))],
+        [pltpu.VMEM((GROUP,) + tight, F32), pltpu.VMEM((chans * lat, width), F32), pltpu.SemaphoreType.DMA((3,))],
         1 << 20,
         8,
-        [ANY],
+        [HBM],
     )(*parts)
     return jnp.transpose(out.reshape(chans, lat, width), (1, 0, 2))[None]
 

time: 62.8 us -> 59 us (0.939)
  local copies, waits for them, and re-layouts: 4.79 us -> 0 us
  starting transfers between devices: 17.1 us -> 17.9 us
  Pallas kernels: 11.7 us -> 12.4 us
    unnamed x20 -> x0, local copies, waits for them, and re-layouts: 4.79 us -> none
    ppermute x9, waiting for transfers between devices: 17.2 us -> 14 us  [exchange(): lax.ppermute(pieces[m], 'lvl', [(k, k ^ m) for k in range(count)])]
    ppermute x2, waiting for transfers between devices: 10.7 us -> 13.2 us  [carried(): lax.ppermute(total, 'lvl', [(k, (k + s * GROUP) % count) for k in range(c...]
    pallas_call x2 -> x3, Pallas kernels: 4.94 us -> 5.93 us  [the longest x1 3.79 us: body(): call(functools.partial(second_kernel, lat), [(GROUP,) + tight], [VM] * 6,...]
    ppermute x2, starting transfers between devices: 3.64 us -> 4.6 us  [carried(): lax.ppermute(total, 'lvl', [(k, (k + s * GROUP) % count) for k in range(c...]
  transfers between devices with their start and end apart: 13 -> 13, of which waited for: 10 -> 9; matrix products, arithmetic and copies ran while one was open for 0% -> 0% of each run, Pallas kernels for 4% -> 10%
where the time goes in v4:
time: 59 us; the launch traced here: 58.9 us
  waiting for transfers between devices  27.6 us (47%)
  starting transfers between devices  17.9 us (30%)
  Pallas kernels  12.4 us (21%)
  between operations  0.74 us (1%)
    ppermute x9, waiting for transfers between devices, exchange(): lax.ppermute(pieces[m], 'lvl', [(k, k ^ m) for k in range(count)])  14 us
    ppermute x2, waiting for transfers between devices, carried(): lax.ppermute(total, 'lvl', [(k, (k + s * GROUP) % count) for k in range(c...  13.2 us
    ppermute x9, starting transfers between devices, exchange(): lax.ppermute(pieces[m], 'lvl', [(k, k ^ m) for k in range(count)])  10.8 us
    ppermute x2, starting transfers between devices, carried(): lax.ppermute(total, 'lvl', [(k, (k + s * GROUP) % count) for k in range(c...  4.6 us
    pallas_call x1, Pallas kernels, body(): call(functools.partial(second_kernel, lat), [(GROUP,) + tight], [VM] * 6,...  3.79 us
    pallas_call x1, Pallas kernels, body(): call(functools.partial(first_kernel, lat), [wide] * GROUP, [VM] * 8, [plt...  3.48 us
    ppermute x1, starting transfers between devices, body(): lax.ppermute(first, 'lon', [((k + 1) % count, k) for k in range(count)])  1.98 us
    pallas_call x1, Pallas kernels, body(): call(functools.partial(edges_kernel, lat), [edge, edge, (COEFS * (GROUP +...  1.92 us
  transfers between devices with their start and end apart: 13, of which 9 were waited for; matrix products, arithmetic and copies ran while one was open for 0% of the time, Pallas kernels for 10%

profile of v4, /device:TPU:0, one launch (start us, length us, event | category | flops | bytes accessed | tf_op | source)
XLA Modules:
  0.0 58.9 jit_solution(4240802454079871441)
XLA Ops:
  0.7 1.9 %shard_map.82 = (f32[72,128]{1,0:T(8,128)S(1)}, f32[72,128]{1,0:T(8,128)S(1)}, f32[40,128]{1,0:T(8,128)S(1)}, f32[1104,128]{1,0:T(8,128)S(1)}, f32[1104,128]{1,0...) custom-call(s32[1]{0:T(128)S(6)} %copy.9.start_ref, ...), custom_call_target="tpu_custom_call" | custom-call | flops 1048576 | bytes 4194304 | tf_op jit(solution)/shard_map/pallas_call | solution.py:429
  2.6 0.5 collective-permute-start
  3.1 2.0 %collective-permute-start.1 = (f32[72,128]{1,0:T(8,128)S(1)}, f32[72,128]{1,0:T(8,128)S(1)}, u32[]{:S(2)}, u32[]{:S(2)}) collective-permute-start(f32[72,128]{1,0:T(8,128)S(1)} %get-tuple-element.36), channel_id=1, source_target_pairs={{1,0},{2,1},{3,2},{0,3},{5,4},{6,5},{7,6},{4,7},{9,8},{10,9},{11,1... | collective-permute-start | bytes 110600 | tf_op jit(solution)/shard_map/ppermute | solution.py:456
  5.1 1.3 %shard_map.83 = (bf16[192,720]{1,0:T(8,128)(2,1)S(1)}, bf16[216,576]{1,0:T(8,128)(2,1)S(1)}, f32[192,1]{1,0:T(8,128)S(1)}, f32[4,80,640]{2,1,0:T(8,128)S(1)}, f3...) custom-call(f32[40,128]{1,0:T(8,128)S(1)} %get-tuple-element.37.coef, ...), custom_call_target="tpu_custom_call" | custom-call | flops 244187136 | bytes 4194304 | tf_op jit(solution)/shard_map/pallas_call | solution.py:457
  6.9 3.5 %shard_map.84 = (f32[72,640]{1,0:T(8,128)S(1)}, f32[72,640]{1,0:T(8,128)S(1)}, f32[72,640]{1,0:T(8,128)S(1)}, f32[72,640]{1,0:T(8,128)S(1)}) custom-call(f32[40,128]{1,0:T(8,128)S(1)} %get-tuple-element.37.coef_ref, f32[4,80,640]{2,1,0:T(8,128)S(1)} %get-tuple-element.43.x_ref, f32[4,72,640]{2,1,0:T(8,128)S(1)} %get-tuple-element.44.n_ref, ...), custom_call_target="tpu_custom_call" | custom-call | flops 976748544 | bytes 4194304 | tf_op jit(solution)/shard_map/pallas_call | solution.py:476
  10.4 2.2 %collective-permute-start.2 = (f32[72,640]{1,0:T(8,128)S(1)}, f32[72,640]{1,0:T(8,128)S(1)}, u32[]{:S(2)}, u32[]{:S(2)}) collective-permute-start(f32[72,640]{1,0:T(8,128)S(1)} %get-tuple-element.49), channel_id=1, source_target_pairs={{0,4},{4,0},{8,12},{12,8},{16,20},{20,16},{24,28},{28,24},{1,5},{5... | collective-permute-start | bytes 552968 | tf_op jit(solution)/shard_map/ppermute | solution.py:398
  12.6 1.6 %collective-permute-start.3 = (f32[72,640]{1,0:T(8,128)S(1)}, f32[72,640]{1,0:T(8,128)S(1)}, u32[]{:S(2)}, u32[]{:S(2)}) collective-permute-start(f32[72,640]{1,0:T(8,128)S(1)} %get-tuple-element.50), channel_id=1, source_target_pairs={{0,8},{4,12},{8,0},{12,4},{16,24},{20,28},{24,16},{28,20},{1,9},{5... | collective-permute-start | bytes 552968 | tf_op jit(solution)/shard_map/ppermute | solution.py:398
  14.2 2.8 %collective-permute-done.2.refs_1_ = f32[72,640]{1,0:T(8,128)S(1)} collective-permute-done((f32[72,640]{1,0:T(8,128)S(1)}, f32[72,640]{1,0:T(8,128)S(1)}, u32[]{:S(2)}, u32[]{:S(2)}) %collective-permute-start.2) | collective-permute-done | bytes 184352 | tf_op jit(solution)/shard_map/ppermute | solution.py:398
  17.0 2.8 %collective-permute-done.3.refs_2_ = f32[72,640]{1,0:T(8,128)S(1)} collective-permute-done((f32[72,640]{1,0:T(8,128)S(1)}, f32[72,640]{1,0:T(8,128)S(1)}, u32[]{:S(2)}, u32[]{:S(2)}) %collective-permute-start.3) | collective-permute-done | bytes 184352 | tf_op jit(solution)/shard_map/ppermute | solution.py:398
  19.7 3.1 %collective-permute-done.4.refs_3_ = f32[72,640]{1,0:T(8,128)S(1)} collective-permute-done((f32[72,640]{1,0:T(8,128)S(1)}, f32[72,640]{1,0:T(8,128)S(1)}, u32[]{:S(2)}, u32[]{:S(2)}) %collective-permute-start.4) | collective-permute-done | bytes 184352 | tf_op jit(solution)/shard_map/ppermute | solution.py:398
  22.9 3.5 %collective-permute-start.5 = (f32[72,640]{1,0:T(8,128)S(1)}, f32[72,640]{1,0:T(8,128)S(1)}, u32[]{:S(2)}, u32[]{:S(2)}) collective-permute-start(f32[72,640]{1,0:T(8,128)S(1)} %add_add_fusion), channel_id=1, source_target_pairs={{0,16},{4,20},{8,24},{12,28},{16,0},{20,4},{24,8},{28,12},{1,17},{... | collective-permute-start | bytes 552968 | tf_op jit(solution)/shard_map/ppermute | solution.py:407
  26.3 1.5 %collective-permute-start.6 = (f32[72,512]{1,0:T(8,128)S(1)}, f32[72,512]{1,0:T(8,128)S(1)}, u32[]{:S(2)}, u32[]{:S(2)}) collective-permute-start(f32[72,512]{1,0:T(8,128)S(1)} %get-tuple-element.55), channel_id=1, source_target_pairs={{0,4},{4,0},{8,12},{12,8},{16,20},{20,16},{24,28},{28,24},{1,5},{5... | collective-permute-start | bytes 442376 | tf_op jit(solution)/shard_map/ppermute | solution.py:398
  27.9 1.6 %collective-permute-start.7 = (f32[72,512]{1,0:T(8,128)S(1)}, f32[72,512]{1,0:T(8,128)S(1)}, u32[]{:S(2)}, u32[]{:S(2)}) collective-permute-start(f32[72,512]{1,0:T(8,128)S(1)} %get-tuple-element.56), channel_id=1, source_target_pairs={{0,8},{4,12},{8,0},{12,4},{16,24},{20,28},{24,16},{28,20},{1,9},{5... | collective-permute-start | bytes 442376 | tf_op jit(solution)/shard_map/ppermute | solution.py:398
  29.5 0.4 collective-permute-start.8
  29.8 0.6 %shard_map.85 = (f32[4,72,640]{2,1,0:T(8,128)S(1)}, f32[72,512]{1,0:T(8,128)S(1)}) custom-call(f32[1104,128]{1,0:T(8,128)S(1)} %get-tuple-element.34.anchor_ref, f32[72,128]{1,0:T(8,128)S(1)} %collective-permute-done.before_ref, f32[72,128]{1,0:T(8,128)S(1)} %collective-permute-done.1.after_ref, f32[72,640]{1,0:T(8,128)S(1)} %get-tuple-element.48.refs_0_, ...), custom_call_target="tpu_custom_call" | custom-call | flops 244187136 | bytes 4194304 | tf_op jit(solution)/shard_map/pallas_call | solution.py:488
  30.5 4.9 %collective-permute-done.5 = f32[72,640]{1,0:T(8,128)S(1)} collective-permute-done((f32[72,640]{1,0:T(8,128)S(1)}, f32[72,640]{1,0:T(8,128)S(1)}, u32[]{:S(2)}, u32[]{:S(2)}) %collective-permute-start.5) | collective-permute-done | bytes 184352 | tf_op jit(solution)/shard_map/ppermute | solution.py:407
  35.4 3.8 %shard_map.86.sum_ref = f32[4,72,512]{2,1,0:T(8,128)S(1)} custom-call(f32[40,128]{1,0:T(8,128)S(1)} %get-tuple-element.37.coef_ref, f32[4,72,640]{2,1,0:T(8,128)S(1)} %get-tuple-element.53.base_ref, f32[192,1]{1,0:T(8,128)S(1)} %get-tuple-element.45.column_ref, bf16[192,720]{1,0:T(8,128)(2,1)S(1)} %get-tuple-element.46.w_in_ref, ...), custom_call_target="tpu_custom_call" | custom-call | flops 976748544 | bytes 4194304 | tf_op jit(solution)/shard_map/pallas_call | solution.py:496
  39.4 1.1 %collective-permute-start.9 = (f32[72,512]{1,0:T(8,128)S(1)}, f32[72,512]{1,0:T(8,128)S(1)}, u32[]{:S(2)}, u32[]{:S(2)}) collective-permute-start(f32[72,512]{1,0:T(8,128)S(1)} %get-tuple-element.59), channel_id=1, source_target_pairs={{0,16},{4,20},{8,24},{12,28},{16,0},{20,4},{24,8},{28,12},{1,17},{... | collective-permute-start | bytes 442376 | tf_op jit(solution)/shard_map/ppermute | solution.py:407
  40.6 8.3 %collective-permute-done.9 = f32[72,512]{1,0:T(8,128)S(1)} collective-permute-done((f32[72,512]{1,0:T(8,128)S(1)}, f32[72,512]{1,0:T(8,128)S(1)}, u32[]{:S(2)}, u32[]{:S(2)}) %collective-permute-start.9) | collective-permute-done | bytes 147488 | tf_op jit(solution)/shard_map/ppermute | solution.py:407
  48.9 1.4 %collective-permute-start.10 = (f32[72,512]{1,0:T(8,128)S(1)}, f32[72,512]{1,0:T(8,128)S(1)}, u32[]{:S(2)}, u32[]{:S(2)}) collective-permute-start(f32[72,512]{1,0:T(8,128)S(1)} %get-tuple-element.64), channel_id=1, source_target_pairs={{0,4},{4,0},{8,12},{12,8},{16,20},{20,16},{24,28},{28,24},{1,5},{5... | collective-permute-start | bytes 442376 | tf_op jit(solution)/shard_map/ppermute | solution.py:398
  50.3 2.2 %collective-permute-start.12 = (f32[72,512]{1,0:T(8,128)S(1)}, f32[72,512]{1,0:T(8,128)S(1)}, u32[]{:S(2)}, u32[]{:S(2)}) collective-permute-start(f32[72,512]{1,0:T(8,128)S(1)} %get-tuple-element.63), channel_id=1, source_target_pairs={{0,12},{4,8},{8,4},{12,0},{16,28},{20,24},{24,20},{28,16},{1,13},{... | collective-permute-start | bytes 442376 | tf_op jit(solution)/shard_map/ppermute | solution.py:398
  52.5 3.2 %collective-permute-done.10.refs_1_ = f32[72,512]{1,0:T(8,128)S(1)} collective-permute-done((f32[72,512]{1,0:T(8,128)S(1)}, f32[72,512]{1,0:T(8,128)S(1)}, u32[]{:S(2)}, u32[]{:S(2)}) %collective-permute-start.10) | collective-permute-done | bytes 147488 | tf_op jit(solution)/shard_map/ppermute | solution.py:398
  55.7 2.1 %collective-permute-done.12.refs_3_ = f32[72,512]{1,0:T(8,128)S(1)} collective-permute-done((f32[72,512]{1,0:T(8,128)S(1)}, f32[72,512]{1,0:T(8,128)S(1)}, u32[]{:S(2)}, u32[]{:S(2)}) %collective-permute-start.12) | collective-permute-done | bytes 147488 | tf_op jit(solution)/shard_map/ppermute | solution.py:398
  57.8 1.0 %shard_map.88 = f32[1104,128]{1,0:T(8,128)} custom-call(f32[72,512]{1,0:T(8,128)S(1)} %get-tuple-element.66.refs_0_, f32[72,512]{1,0:T(8,128)S(1)} %collective-permute-done.10.refs_1_, f32[72,512]{1,0:T(8,128)S(1)} %collective-permute-done.11.refs_2_, f32[72,512]{1,0:T(8,128)S(1)} %collective-permute-done.12.refs_3_), custom_call_target="tpu_custom_call" | custom-call | flops 1048576 | bytes 4194304 | tf_op jit(solution)/shard_map/pallas_call | solution.py:514
  (12 shorter events, 0.9 us)
Async XLA Ops:
  2.6 4.1 %collective-permute-start = (f32[72,128]{1,0:T(8,128)S(1)}, f32[72,128]{1,0:T(8,128)S(1)}, u32[]{:S(2)}, u32[]{:S(2)}) collective-permute-start(f32[72,128]{1,0:T(8,128)S(1)} %get-tuple-element.35), channel_id=1, source_target_pairs={{0,1},{1,2},{2,3},{3,0},{4,5},{5,6},{6,7},{7,4},{8,9},{9,10},{10,1... | collective-permute-start | bytes 110600 | tf_op jit(solution)/shard_map/ppermute | solution.py:455
  3.1 3.8 %collective-permute-start.1 = (f32[72,128]{1,0:T(8,128)S(1)}, f32[72,128]{1,0:T(8,128)S(1)}, u32[]{:S(2)}, u32[]{:S(2)}) collective-permute-start(f32[72,128]{1,0:T(8,128)S(1)} %get-tuple-element.36), channel_id=1, source_target_pairs={{1,0},{2,1},{3,2},{0,3},{5,4},{6,5},{7,6},{4,7},{9,8},{10,9},{11,1... | collective-permute-start | bytes 110600 | tf_op jit(solution)/shard_map/ppermute | solution.py:456
  10.4 6.6 %collective-permute-start.2 = (f32[72,640]{1,0:T(8,128)S(1)}, f32[72,640]{1,0:T(8,128)S(1)}, u32[]{:S(2)}, u32[]{:S(2)}) collective-permute-start(f32[72,640]{1,0:T(8,128)S(1)} %get-tuple-element.49), channel_id=1, source_target_pairs={{0,4},{4,0},{8,12},{12,8},{16,20},{20,16},{24,28},{28,24},{1,5},{5... | collective-permute-start | bytes 552968 | tf_op jit(solution)/shard_map/ppermute | solution.py:398
  12.6 7.2 %collective-permute-start.3 = (f32[72,640]{1,0:T(8,128)S(1)}, f32[72,640]{1,0:T(8,128)S(1)}, u32[]{:S(2)}, u32[]{:S(2)}) collective-permute-start(f32[72,640]{1,0:T(8,128)S(1)} %get-tuple-element.50), channel_id=1, source_target_pairs={{0,8},{4,12},{8,0},{12,4},{16,24},{20,28},{24,16},{28,20},{1,9},{5... | collective-permute-start | bytes 552968 | tf_op jit(solution)/shard_map/ppermute | solution.py:398
  14.2 8.6 %collective-permute-start.4 = (f32[72,640]{1,0:T(8,128)S(1)}, f32[72,640]{1,0:T(8,128)S(1)}, u32[]{:S(2)}, u32[]{:S(2)}) collective-permute-start(f32[72,640]{1,0:T(8,128)S(1)} %get-tuple-element.51), channel_id=1, source_target_pairs={{0,12},{4,8},{8,4},{12,0},{16,28},{20,24},{24,20},{28,16},{1,13},{... | collective-permute-start | bytes 552968 | tf_op jit(solution)/shard_map/ppermute | solution.py:398
  22.9 12.5 %collective-permute-start.5 = (f32[72,640]{1,0:T(8,128)S(1)}, f32[72,640]{1,0:T(8,128)S(1)}, u32[]{:S(2)}, u32[]{:S(2)}) collective-permute-start(f32[72,640]{1,0:T(8,128)S(1)} %add_add_fusion), channel_id=1, source_target_pairs={{0,16},{4,20},{8,24},{12,28},{16,0},{20,4},{24,8},{28,12},{1,17},{... | collective-permute-start | bytes 552968 | tf_op jit(solution)/shard_map/ppermute | solution.py:407
  26.3 12.9 %collective-permute-start.6 = (f32[72,512]{1,0:T(8,128)S(1)}, f32[72,512]{1,0:T(8,128)S(1)}, u32[]{:S(2)}, u32[]{:S(2)}) collective-permute-start(f32[72,512]{1,0:T(8,128)S(1)} %get-tuple-element.55), channel_id=1, source_target_pairs={{0,4},{4,0},{8,12},{12,8},{16,20},{20,16},{24,28},{28,24},{1,5},{5... | collective-permute-start | bytes 442376 | tf_op jit(solution)/shard_map/ppermute | solution.py:398
  27.9 11.3 %collective-permute-start.7 = (f32[72,512]{1,0:T(8,128)S(1)}, f32[72,512]{1,0:T(8,128)S(1)}, u32[]{:S(2)}, u32[]{:S(2)}) collective-permute-start(f32[72,512]{1,0:T(8,128)S(1)} %get-tuple-element.56), channel_id=1, source_target_pairs={{0,8},{4,12},{8,0},{12,4},{16,24},{20,28},{24,16},{28,20},{1,9},{5... | collective-permute-start | bytes 442376 | tf_op jit(solution)/shard_map/ppermute | solution.py:398
  29.5 9.8 %collective-permute-start.8 = (f32[72,512]{1,0:T(8,128)S(1)}, f32[72,512]{1,0:T(8,128)S(1)}, u32[]{:S(2)}, u32[]{:S(2)}) collective-permute-start(f32[72,512]{1,0:T(8,128)S(1)} %get-tuple-element.57), channel_id=1, source_target_pairs={{0,12},{4,8},{8,4},{12,0},{16,28},{20,24},{24,20},{28,16},{1,13},{... | collective-permute-start | bytes 442376 | tf_op jit(solution)/shard_map/ppermute | solution.py:398
  39.4 9.4 %collective-permute-start.9 = (f32[72,512]{1,0:T(8,128)S(1)}, f32[72,512]{1,0:T(8,128)S(1)}, u32[]{:S(2)}, u32[]{:S(2)}) collective-permute-start(f32[72,512]{1,0:T(8,128)S(1)} %get-tuple-element.59), channel_id=1, source_target_pairs={{0,16},{4,20},{8,24},{12,28},{16,0},{20,4},{24,8},{28,12},{1,17},{... | collective-permute-start | bytes 442376 | tf_op jit(solution)/shard_map/ppermute | solution.py:407
  48.9 6.8 %collective-permute-start.10 = (f32[72,512]{1,0:T(8,128)S(1)}, f32[72,512]{1,0:T(8,128)S(1)}, u32[]{:S(2)}, u32[]{:S(2)}) collective-permute-start(f32[72,512]{1,0:T(8,128)S(1)} %get-tuple-element.64), channel_id=1, source_target_pairs={{0,4},{4,0},{8,12},{12,8},{16,20},{20,16},{24,28},{28,24},{1,5},{5... | collective-permute-start | bytes 442376 | tf_op jit(solution)/shard_map/ppermute | solution.py:398
  50.3 5.4 %collective-permute-start.11 = (f32[72,512]{1,0:T(8,128)S(1)}, f32[72,512]{1,0:T(8,128)S(1)}, u32[]{:S(2)}, u32[]{:S(2)}) collective-permute-start(f32[72,512]{1,0:T(8,128)S(1)} %get-tuple-element.65), channel_id=1, source_target_pairs={{0,8},{4,12},{8,0},{12,4},{16,24},{20,28},{24,16},{28,20},{1,9},{5... | collective-permute-start | bytes 442376 | tf_op jit(solution)/shard_map/ppermute | solution.py:398
  50.3 7.5 %collective-permute-start.12 = (f32[72,512]{1,0:T(8,128)S(1)}, f32[72,512]{1,0:T(8,128)S(1)}, u32[]{:S(2)}, u32[]{:S(2)}) collective-permute-start(f32[72,512]{1,0:T(8,128)S(1)} %get-tuple-element.63), channel_id=1, source_target_pairs={{0,12},{4,8},{8,4},{12,0},{16,28},{20,24},{24,20},{28,16},{1,13},{... | collective-permute-start | bytes 442376 | tf_op jit(solution)/shard_map/ppermute | solution.py:398

commit v5 on v4

--- a/solution.py
+++ b/solution.py
@@ -46,6 +46,12 @@
 
 def lanes_of(x):
     return lax.broadcasted_iota(jnp.int32, x.shape, 1)
+
+
+def place():
+    level = lax.axis_index("lvl")
+    mine = lax.rem(level, GROUP)
+    return mine, lax.bitwise_xor(mine, lax.rem(level // GROUP, 2) * (GROUP // 2))
 
 
 def between(lane, low, high):
@@ -167,7 +173,7 @@
         for q in range(GROUP):
             for t, tile in enumerate(tiled(rolled, pitch, turn * q)):
                 target[q, 0:chans, t * width : (t + 1) * width] = tile
-    me = lax.rem(lax.axis_index("lvl"), GROUP)
+    _, quarter = place()
     in_ref[...] = jnp.zeros_like(in_ref)
     out_ref[...] = jnp.zeros_like(out_ref)
     for b in range(3):
@@ -186,7 +192,7 @@
         for q, line in enumerate(swapped(lines)):
             wave_ref[q, 0:chans, t * width : (t + 1) * width] = line
     for m in range(GROUP):
-        waves[m][...] = wave_ref[lax.bitwise_xor(me, m)]
+        waves[m][...] = wave_ref[lax.bitwise_xor(quarter, m)]
 
 
 def lat_shifted(x, pitch, first):
@@ -255,7 +261,7 @@
     sub = width // GROUP
     pitch = strip // lat
     turn = turn_of(pitch, sub, width)
-    me = lax.rem(lax.axis_index("lvl"), GROUP)
+    _, quarter = place()
     half, drift, spread, time = [coef_ref[r : r + 1, 0:1] for r in range(4)]
     shift = column_ref[...] * time
     before = before_ref[...]
@@ -281,7 +287,7 @@
         for q, score, other in zip(quarters, scores, others):
             inc_ref[q] = roll(other + drift * score, -pitch * turn * q)
     for m in range(GROUP):
-        outs[m][...] = inc_ref[lax.bitwise_xor(me, m)]
+        outs[m][...] = inc_ref[lax.bitwise_xor(quarter, m)]
 
 
 def base_kernel(lat, anchor_ref, before_ref, after_ref, *refs):
@@ -292,14 +298,14 @@
     sub = width // GROUP
     strip = base_ref.shape[2]
     pitch = strip // lat
-    me = lax.rem(lax.axis_index("lvl"), GROUP)
+    mine, quarter = place()
     for m in range(GROUP):
-        inc_ref[lax.bitwise_xor(me, m)] = incs[m][...]
+        inc_ref[lax.bitwise_xor(mine, m)] = incs[m][...]
     anc_ref[chans // ROWS * ROWS :, :] = jnp.zeros_like(anc_ref[chans // ROWS * ROWS :, :])
     tight_ref[chans // ROWS * ROWS :, :] = jnp.zeros_like(tight_ref[chans // ROWS * ROWS :, :])
     turned = []
     for l in range(lat):
-        turned.append(pltpu.roll(anchor_ref[pl.ds(l, chans, stride=lat), :], lax.rem(width - me * sub, width), 1))
+        turned.append(pltpu.roll(anchor_ref[pl.ds(l, chans, stride=lat), :], lax.rem(width - quarter * sub, width), 1))
     for t, tile in enumerate(tiled([roll(line, pitch * l + EDGE) for l, line in enumerate(turned)], pitch, 0)):
         anc_ref[0:chans, t * width : (t + 1) * width] = tile
     block = lanes_of(turned[0]) // sub
@@ -308,8 +314,8 @@
         for i in range(1, GROUP):
             tile = jnp.where(block == i, roll(turned[GROUP * t + i], i * sub), tile)
         tight_ref[0:chans, t * width : (t + 1) * width] = tile
-    state = edged(anc_ref[...], before_ref[...], pitch, 0, 6, 2, 2, me == 0)
-    state = edged(state, after_ref[...], pitch, 0, 2, pitch - EDGE, 2, me == GROUP - 1)
+    state = edged(anc_ref[...], before_ref[...], pitch, 0, 6, 2, 2, quarter == 0)
+    state = edged(state, after_ref[...], pitch, 0, 2, pitch - EDGE, 2, quarter == GROUP - 1)
     for j in range(GROUP):
         base_ref[j] = state
         if j + 1 < GROUP:
@@ -354,9 +360,9 @@
     waves = refs[:GROUP]
     outs = refs[GROUP : 2 * GROUP]
     total_ref, wave_ref = refs[2 * GROUP :]
-    me = lax.rem(lax.axis_index("lvl"), GROUP)
+    mine, _ = place()
     for m in range(GROUP):
-        wave_ref[lax.bitwise_xor(me, m)] = waves[m][...]
+        wave_ref[lax.bitwise_xor(mine, m)] = waves[m][...]
     noise = jnp.zeros(total_ref.shape, F32)
     for j in range(GROUP):
         noise = noise + wave_ref[j]
@@ -364,7 +370,7 @@
         wave_ref[j] = tight_ref[...] + share
     total_ref[...] = share
     for m in range(GROUP):
-        outs[m][...] = wave_ref[lax.bitwise_xor(me, m)]
+        outs[m][...] = wave_ref[lax.bitwise_xor(mine, m)]
 
 
 def last_kernel(lat, *refs):
@@ -372,9 +378,9 @@
     out_any, all_ref, line_ref, sems = refs[GROUP:]
     chans = line_ref.shape[0] // lat
     width = line_ref.shape[1]
-    me = lax.rem(lax.axis_index("lvl"), GROUP)
+    _, quarter = place()
     for m in range(GROUP):
-        all_ref[lax.bitwise_xor(me, m)] = parts[m][...]
+        all_ref[lax.bitwise_xor(quarter, m)] = parts[m][...]
     size = up_to(-(-chans // 3), ROWS)
     copies = []
     for i, low in enumerate(range(0, chans, size)):
@@ -404,7 +410,12 @@
     blocks = count // GROUP
     carry = jnp.zeros_like(total)
     for s in range(1, blocks):
-        moved = lax.ppermute(total, "lvl", [(k, (k + s * GROUP) % count) for k in range(count)])
+        pairs = []
+        for k in range(count):
+            target = (k // GROUP + s) % blocks
+            turn = (k // GROUP + target) % 2 * (GROUP // 2)
+            pairs.append((k, target * GROUP + (k % GROUP ^ turn)))
+        moved = lax.ppermute(total, "lvl", pairs)
         carry = carry + jnp.where(block >= s, moved, 0.0)
     return carry
 

time: 59 us -> 58.3 us (0.988)
  waiting for transfers between devices: 27.6 us -> 24.8 us
  starting transfers between devices: 17.9 us -> 20.1 us
    ppermute x2, waiting for transfers between devices: 13.2 us -> 7.13 us  [carried(): moved = lax.ppermute(total, 'lvl', pairs)]
    ppermute x9, waiting for transfers between devices: 14 us -> 17.1 us  [exchange(): lax.ppermute(pieces[m], 'lvl', [(k, k ^ m) for k in range(count)])]
    ppermute x2, starting transfers between devices: 4.6 us -> 6.52 us  [carried(): moved = lax.ppermute(total, 'lvl', pairs)]
  transfers between devices with their start and end apart: 13 -> 13, of which waited for: 9 -> 11; matrix products, arithmetic and copies ran while one was open for 0% -> 0% of each run, Pallas kernels for 10% -> 10%
where the time goes in v5:
time: 58.3 us; the launch traced here: 58.1 us
  waiting for transfers between devices  24.8 us (43%)
  starting transfers between devices  20.1 us (34%)
  Pallas kernels  12.4 us (21%)
  between operations  0.73 us (1%)
    ppermute x9, waiting for transfers between devices, exchange(): lax.ppermute(pieces[m], 'lvl', [(k, k ^ m) for k in range(count)])  17.1 us
    ppermute x9, starting transfers between devices, exchange(): lax.ppermute(pieces[m], 'lvl', [(k, k ^ m) for k in range(count)])  11 us
    ppermute x2, waiting for transfers between devices, carried(): moved = lax.ppermute(total, 'lvl', pairs)  7.13 us
    ppermute x2, starting transfers between devices, carried(): moved = lax.ppermute(total, 'lvl', pairs)  6.52 us
    pallas_call x1, Pallas kernels, body(): call(functools.partial(second_kernel, lat), [(GROUP,) + tight], [VM] * 6,...  3.79 us
    pallas_call x1, Pallas kernels, body(): call(functools.partial(first_kernel, lat), [wide] * GROUP, [VM] * 8, [plt...  3.48 us
    ppermute x1, starting transfers between devices, body(): lax.ppermute(first, 'lon', [((k + 1) % count, k) for k in range(count)])  1.98 us
    pallas_call x1, Pallas kernels, body(): call(functools.partial(edges_kernel, lat), [edge, edge, (COEFS * (GROUP +...  1.92 us
  transfers between devices with their start and end apart: 13, of which 11 were waited for; matrix products, arithmetic and copies ran while one was open for 0% of the time, Pallas kernels for 10%

profile of v5, /device:TPU:0, one launch (start us, length us, event | category | flops | bytes accessed | tf_op | source)
XLA Modules:
  0.0 58.1 jit_solution(14764395089729892479)
XLA Ops:
  0.7 1.9 %shard_map.82 = (f32[72,128]{1,0:T(8,128)S(1)}, f32[72,128]{1,0:T(8,128)S(1)}, f32[40,128]{1,0:T(8,128)S(1)}, f32[1104,128]{1,0:T(8,128)S(1)}, f32[1104,128]{1,0...) custom-call(s32[1]{0:T(128)S(6)} %copy.9.start_ref, ...), custom_call_target="tpu_custom_call" | custom-call | flops 1048576 | bytes 4194304 | tf_op jit(solution)/shard_map/pallas_call | solution.py:440
  3.1 2.0 %collective-permute-start.1 = (f32[72,128]{1,0:T(8,128)S(1)}, f32[72,128]{1,0:T(8,128)S(1)}, u32[]{:S(2)}, u32[]{:S(2)}) collective-permute-start(f32[72,128]{1,0:T(8,128)S(1)} %get-tuple-element.36), channel_id=1, source_target_pairs={{1,0},{2,1},{3,2},{0,3},{5,4},{6,5},{7,6},{4,7},{9,8},{10,9},{11,1... | collective-permute-start | bytes 110600 | tf_op jit(solution)/shard_map/ppermute | solution.py:467
  5.1 1.3 %shard_map.83 = (bf16[192,720]{1,0:T(8,128)(2,1)S(1)}, bf16[216,576]{1,0:T(8,128)(2,1)S(1)}, f32[192,1]{1,0:T(8,128)S(1)}, f32[4,80,640]{2,1,0:T(8,128)S(1)}, f3...) custom-call(f32[40,128]{1,0:T(8,128)S(1)} %get-tuple-element.37.coef, ...), custom_call_target="tpu_custom_call" | custom-call | flops 244187136 | bytes 4194304 | tf_op jit(solution)/shard_map/pallas_call | solution.py:468
  6.9 3.5 %shard_map.84 = (f32[72,640]{1,0:T(8,128)S(1)}, f32[72,640]{1,0:T(8,128)S(1)}, f32[72,640]{1,0:T(8,128)S(1)}, f32[72,640]{1,0:T(8,128)S(1)}) custom-call(f32[40,128]{1,0:T(8,128)S(1)} %get-tuple-element.37.coef_ref, f32[4,80,640]{2,1,0:T(8,128)S(1)} %get-tuple-element.43.x_ref, f32[4,72,640]{2,1,0:T(8,128)S(1)} %get-tuple-element.44.n_ref, ...), custom_call_target="tpu_custom_call" | custom-call | flops 976748544 | bytes 4194304 | tf_op jit(solution)/shard_map/pallas_call | solution.py:487
  10.4 2.2 %collective-permute-start.2 = (f32[72,640]{1,0:T(8,128)S(1)}, f32[72,640]{1,0:T(8,128)S(1)}, u32[]{:S(2)}, u32[]{:S(2)}) collective-permute-start(f32[72,640]{1,0:T(8,128)S(1)} %get-tuple-element.49), channel_id=1, source_target_pairs={{0,4},{4,0},{8,12},{12,8},{16,20},{20,16},{24,28},{28,24},{1,5},{5... | collective-permute-start | bytes 552968 | tf_op jit(solution)/shard_map/ppermute | solution.py:404
  12.6 1.6 %collective-permute-start.3 = (f32[72,640]{1,0:T(8,128)S(1)}, f32[72,640]{1,0:T(8,128)S(1)}, u32[]{:S(2)}, u32[]{:S(2)}) collective-permute-start(f32[72,640]{1,0:T(8,128)S(1)} %get-tuple-element.50), channel_id=1, source_target_pairs={{0,8},{4,12},{8,0},{12,4},{16,24},{20,28},{24,16},{28,20},{1,9},{5... | collective-permute-start | bytes 552968 | tf_op jit(solution)/shard_map/ppermute | solution.py:404
  14.1 2.8 %collective-permute-done.2.refs_1_ = f32[72,640]{1,0:T(8,128)S(1)} collective-permute-done((f32[72,640]{1,0:T(8,128)S(1)}, f32[72,640]{1,0:T(8,128)S(1)}, u32[]{:S(2)}, u32[]{:S(2)}) %collective-permute-start.2) | collective-permute-done | bytes 184352 | tf_op jit(solution)/shard_map/ppermute | solution.py:404
  17.0 2.8 %collective-permute-done.3.refs_2_ = f32[72,640]{1,0:T(8,128)S(1)} collective-permute-done((f32[72,640]{1,0:T(8,128)S(1)}, f32[72,640]{1,0:T(8,128)S(1)}, u32[]{:S(2)}, u32[]{:S(2)}) %collective-permute-start.3) | collective-permute-done | bytes 184352 | tf_op jit(solution)/shard_map/ppermute | solution.py:404
  19.7 3.0 %collective-permute-done.4.refs_3_ = f32[72,640]{1,0:T(8,128)S(1)} collective-permute-done((f32[72,640]{1,0:T(8,128)S(1)}, f32[72,640]{1,0:T(8,128)S(1)}, u32[]{:S(2)}, u32[]{:S(2)}) %collective-permute-start.4) | collective-permute-done | bytes 184352 | tf_op jit(solution)/shard_map/ppermute | solution.py:404
  22.8 4.5 %collective-permute-start.5 = (f32[72,640]{1,0:T(8,128)S(1)}, f32[72,640]{1,0:T(8,128)S(1)}, u32[]{:S(2)}, u32[]{:S(2)}) collective-permute-start(f32[72,640]{1,0:T(8,128)S(1)} %add_add_fusion), channel_id=1, source_target_pairs={{0,24},{4,28},{8,16},{12,20},{16,8},{20,12},{24,0},{28,4},{1,25},{... | collective-permute-start | bytes 552968 | tf_op jit(solution)/shard_map/ppermute | solution.py:418
  27.4 1.5 %collective-permute-start.6 = (f32[72,512]{1,0:T(8,128)S(1)}, f32[72,512]{1,0:T(8,128)S(1)}, u32[]{:S(2)}, u32[]{:S(2)}) collective-permute-start(f32[72,512]{1,0:T(8,128)S(1)} %get-tuple-element.55), channel_id=1, source_target_pairs={{0,4},{4,0},{8,12},{12,8},{16,20},{20,16},{24,28},{28,24},{1,5},{5... | collective-permute-start | bytes 442376 | tf_op jit(solution)/shard_map/ppermute | solution.py:404
  28.9 2.0 %collective-permute-start.8 = (f32[72,512]{1,0:T(8,128)S(1)}, f32[72,512]{1,0:T(8,128)S(1)}, u32[]{:S(2)}, u32[]{:S(2)}) collective-permute-start(f32[72,512]{1,0:T(8,128)S(1)} %get-tuple-element.57), channel_id=1, source_target_pairs={{0,12},{4,8},{8,4},{12,0},{16,28},{20,24},{24,20},{28,16},{1,13},{... | collective-permute-start | bytes 442376 | tf_op jit(solution)/shard_map/ppermute | solution.py:404
  30.8 0.6 %shard_map.85 = (f32[4,72,640]{2,1,0:T(8,128)S(1)}, f32[72,512]{1,0:T(8,128)S(1)}) custom-call(f32[1104,128]{1,0:T(8,128)S(1)} %get-tuple-element.34.anchor_ref, f32[72,128]{1,0:T(8,128)S(1)} %collective-permute-done.before_ref, f32[72,128]{1,0:T(8,128)S(1)} %collective-permute-done.1.after_ref, f32[72,640]{1,0:T(8,128)S(1)} %get-tuple-element.48.refs_0_, ...), custom_call_target="tpu_custom_call" | custom-call | flops 244187136 | bytes 4194304 | tf_op jit(solution)/shard_map/pallas_call | solution.py:499
  31.5 1.4 %collective-permute-done.5 = f32[72,640]{1,0:T(8,128)S(1)} collective-permute-done((f32[72,640]{1,0:T(8,128)S(1)}, f32[72,640]{1,0:T(8,128)S(1)}, u32[]{:S(2)}, u32[]{:S(2)}) %collective-permute-start.5) | collective-permute-done | bytes 184352 | tf_op jit(solution)/shard_map/ppermute | solution.py:418
  32.9 3.8 %shard_map.86.sum_ref = f32[4,72,512]{2,1,0:T(8,128)S(1)} custom-call(f32[40,128]{1,0:T(8,128)S(1)} %get-tuple-element.37.coef_ref, f32[4,72,640]{2,1,0:T(8,128)S(1)} %get-tuple-element.53.base_ref, f32[192,1]{1,0:T(8,128)S(1)} %get-tuple-element.45.column_ref, bf16[192,720]{1,0:T(8,128)(2,1)S(1)} %get-tuple-element.46.w_in_ref, ...), custom_call_target="tpu_custom_call" | custom-call | flops 976748544 | bytes 4194304 | tf_op jit(solution)/shard_map/pallas_call | solution.py:507
  36.7 3.0 %collective-permute-done.8.refs_3_ = f32[72,512]{1,0:T(8,128)S(1)} collective-permute-done((f32[72,512]{1,0:T(8,128)S(1)}, f32[72,512]{1,0:T(8,128)S(1)}, u32[]{:S(2)}, u32[]{:S(2)}) %collective-permute-start.8) | collective-permute-done | bytes 147488 | tf_op jit(solution)/shard_map/ppermute | solution.py:404
  39.9 2.0 %collective-permute-start.9 = (f32[72,512]{1,0:T(8,128)S(1)}, f32[72,512]{1,0:T(8,128)S(1)}, u32[]{:S(2)}, u32[]{:S(2)}) collective-permute-start(f32[72,512]{1,0:T(8,128)S(1)} %get-tuple-element.59), channel_id=1, source_target_pairs={{0,24},{4,28},{8,16},{12,20},{16,8},{20,12},{24,0},{28,4},{1,25},{... | collective-permute-start | bytes 442376 | tf_op jit(solution)/shard_map/ppermute | solution.py:418
  41.9 5.7 %collective-permute-done.9 = f32[72,512]{1,0:T(8,128)S(1)} collective-permute-done((f32[72,512]{1,0:T(8,128)S(1)}, f32[72,512]{1,0:T(8,128)S(1)}, u32[]{:S(2)}, u32[]{:S(2)}) %collective-permute-start.9) | collective-permute-done | bytes 147488 | tf_op jit(solution)/shard_map/ppermute | solution.py:418
  48.2 2.4 %collective-permute-start.11 = (f32[72,512]{1,0:T(8,128)S(1)}, f32[72,512]{1,0:T(8,128)S(1)}, u32[]{:S(2)}, u32[]{:S(2)}) collective-permute-start(f32[72,512]{1,0:T(8,128)S(1)} %get-tuple-element.65), channel_id=1, source_target_pairs={{0,8},{4,12},{8,0},{12,4},{16,24},{20,28},{24,16},{28,20},{1,9},{5... | collective-permute-start | bytes 442376 | tf_op jit(solution)/shard_map/ppermute | solution.py:404
  50.6 1.0 %collective-permute-start.12 = (f32[72,512]{1,0:T(8,128)S(1)}, f32[72,512]{1,0:T(8,128)S(1)}, u32[]{:S(2)}, u32[]{:S(2)}) collective-permute-start(f32[72,512]{1,0:T(8,128)S(1)} %get-tuple-element.63), channel_id=1, source_target_pairs={{0,12},{4,8},{8,4},{12,0},{16,28},{20,24},{24,20},{28,16},{1,13},{... | collective-permute-start | bytes 442376 | tf_op jit(solution)/shard_map/ppermute | solution.py:404
  51.5 2.8 %collective-permute-done.10.refs_1_ = f32[72,512]{1,0:T(8,128)S(1)} collective-permute-done((f32[72,512]{1,0:T(8,128)S(1)}, f32[72,512]{1,0:T(8,128)S(1)}, u32[]{:S(2)}, u32[]{:S(2)}) %collective-permute-start.10) | collective-permute-done | bytes 147488 | tf_op jit(solution)/shard_map/ppermute | solution.py:404
  54.3 0.8 %collective-permute-done.11.refs_2_ = f32[72,512]{1,0:T(8,128)S(1)} collective-permute-done((f32[72,512]{1,0:T(8,128)S(1)}, f32[72,512]{1,0:T(8,128)S(1)}, u32[]{:S(2)}, u32[]{:S(2)}) %collective-permute-start.11) | collective-permute-done | bytes 147488 | tf_op jit(solution)/shard_map/ppermute | solution.py:404
  55.2 1.9 %collective-permute-done.12.refs_3_ = f32[72,512]{1,0:T(8,128)S(1)} collective-permute-done((f32[72,512]{1,0:T(8,128)S(1)}, f32[72,512]{1,0:T(8,128)S(1)}, u32[]{:S(2)}, u32[]{:S(2)}) %collective-permute-start.12) | collective-permute-done | bytes 147488 | tf_op jit(solution)/shard_map/ppermute | solution.py:404
  57.0 1.0 %shard_map.88 = f32[1104,128]{1,0:T(8,128)} custom-call(f32[72,512]{1,0:T(8,128)S(1)} %get-tuple-element.66.refs_0_, f32[72,512]{1,0:T(8,128)S(1)} %collective-permute-done.10.refs_1_, f32[72,512]{1,0:T(8,128)S(1)} %collective-permute-done.11.refs_2_, f32[72,512]{1,0:T(8,128)S(1)} %collective-permute-done.12.refs_3_), custom_call_target="tpu_custom_call" | custom-call | flops 1048576 | bytes 4194304 | tf_op jit(solution)/shard_map/pallas_call | solution.py:525
  (12 shorter events, 1.9 us)
Async XLA Ops:
  2.6 4.1 %collective-permute-start = (f32[72,128]{1,0:T(8,128)S(1)}, f32[72,128]{1,0:T(8,128)S(1)}, u32[]{:S(2)}, u32[]{:S(2)}) collective-permute-start(f32[72,128]{1,0:T(8,128)S(1)} %get-tuple-element.35), channel_id=1, source_target_pairs={{0,1},{1,2},{2,3},{3,0},{4,5},{5,6},{6,7},{7,4},{8,9},{9,10},{10,1... | collective-permute-start | bytes 110600 | tf_op jit(solution)/shard_map/ppermute | solution.py:466
  3.1 3.8 %collective-permute-start.1 = (f32[72,128]{1,0:T(8,128)S(1)}, f32[72,128]{1,0:T(8,128)S(1)}, u32[]{:S(2)}, u32[]{:S(2)}) collective-permute-start(f32[72,128]{1,0:T(8,128)S(1)} %get-tuple-element.36), channel_id=1, source_target_pairs={{1,0},{2,1},{3,2},{0,3},{5,4},{6,5},{7,6},{4,7},{9,8},{10,9},{11,1... | collective-permute-start | bytes 110600 | tf_op jit(solution)/shard_map/ppermute | solution.py:467
  10.4 6.6 %collective-permute-start.2 = (f32[72,640]{1,0:T(8,128)S(1)}, f32[72,640]{1,0:T(8,128)S(1)}, u32[]{:S(2)}, u32[]{:S(2)}) collective-permute-start(f32[72,640]{1,0:T(8,128)S(1)} %get-tuple-element.49), channel_id=1, source_target_pairs={{0,4},{4,0},{8,12},{12,8},{16,20},{20,16},{24,28},{28,24},{1,5},{5... | collective-permute-start | bytes 552968 | tf_op jit(solution)/shard_map/ppermute | solution.py:404
  12.6 7.2 %collective-permute-start.3 = (f32[72,640]{1,0:T(8,128)S(1)}, f32[72,640]{1,0:T(8,128)S(1)}, u32[]{:S(2)}, u32[]{:S(2)}) collective-permute-start(f32[72,640]{1,0:T(8,128)S(1)} %get-tuple-element.50), channel_id=1, source_target_pairs={{0,8},{4,12},{8,0},{12,4},{16,24},{20,28},{24,16},{28,20},{1,9},{5... | collective-permute-start | bytes 552968 | tf_op jit(solution)/shard_map/ppermute | solution.py:404
  14.1 8.6 %collective-permute-start.4 = (f32[72,640]{1,0:T(8,128)S(1)}, f32[72,640]{1,0:T(8,128)S(1)}, u32[]{:S(2)}, u32[]{:S(2)}) collective-permute-start(f32[72,640]{1,0:T(8,128)S(1)} %get-tuple-element.51), channel_id=1, source_target_pairs={{0,12},{4,8},{8,4},{12,0},{16,28},{20,24},{24,20},{28,16},{1,13},{... | collective-permute-start | bytes 552968 | tf_op jit(solution)/shard_map/ppermute | solution.py:404
  22.8 10.1 %collective-permute-start.5 = (f32[72,640]{1,0:T(8,128)S(1)}, f32[72,640]{1,0:T(8,128)S(1)}, u32[]{:S(2)}, u32[]{:S(2)}) collective-permute-start(f32[72,640]{1,0:T(8,128)S(1)} %add_add_fusion), channel_id=1, source_target_pairs={{0,24},{4,28},{8,16},{12,20},{16,8},{20,12},{24,0},{28,4},{1,25},{... | collective-permute-start | bytes 552968 | tf_op jit(solution)/shard_map/ppermute | solution.py:418
  27.4 9.4 %collective-permute-start.6 = (f32[72,512]{1,0:T(8,128)S(1)}, f32[72,512]{1,0:T(8,128)S(1)}, u32[]{:S(2)}, u32[]{:S(2)}) collective-permute-start(f32[72,512]{1,0:T(8,128)S(1)} %get-tuple-element.55), channel_id=1, source_target_pairs={{0,4},{4,0},{8,12},{12,8},{16,20},{20,16},{24,28},{28,24},{1,5},{5... | collective-permute-start | bytes 442376 | tf_op jit(solution)/shard_map/ppermute | solution.py:404
  28.9 7.8 %collective-permute-start.7 = (f32[72,512]{1,0:T(8,128)S(1)}, f32[72,512]{1,0:T(8,128)S(1)}, u32[]{:S(2)}, u32[]{:S(2)}) collective-permute-start(f32[72,512]{1,0:T(8,128)S(1)} %get-tuple-element.56), channel_id=1, source_target_pairs={{0,8},{4,12},{8,0},{12,4},{16,24},{20,28},{24,16},{28,20},{1,9},{5... | collective-permute-start | bytes 442376 | tf_op jit(solution)/shard_map/ppermute | solution.py:404
  28.9 10.8 %collective-permute-start.8 = (f32[72,512]{1,0:T(8,128)S(1)}, f32[72,512]{1,0:T(8,128)S(1)}, u32[]{:S(2)}, u32[]{:S(2)}) collective-permute-start(f32[72,512]{1,0:T(8,128)S(1)} %get-tuple-element.57), channel_id=1, source_target_pairs={{0,12},{4,8},{8,4},{12,0},{16,28},{20,24},{24,20},{28,16},{1,13},{... | collective-permute-start | bytes 442376 | tf_op jit(solution)/shard_map/ppermute | solution.py:404
  39.9 7.7 %collective-permute-start.9 = (f32[72,512]{1,0:T(8,128)S(1)}, f32[72,512]{1,0:T(8,128)S(1)}, u32[]{:S(2)}, u32[]{:S(2)}) collective-permute-start(f32[72,512]{1,0:T(8,128)S(1)} %get-tuple-element.59), channel_id=1, source_target_pairs={{0,24},{4,28},{8,16},{12,20},{16,8},{20,12},{24,0},{28,4},{1,25},{... | collective-permute-start | bytes 442376 | tf_op jit(solution)/shard_map/ppermute | solution.py:418
  47.7 6.6 %collective-permute-start.10 = (f32[72,512]{1,0:T(8,128)S(1)}, f32[72,512]{1,0:T(8,128)S(1)}, u32[]{:S(2)}, u32[]{:S(2)}) collective-permute-start(f32[72,512]{1,0:T(8,128)S(1)} %get-tuple-element.64), channel_id=1, source_target_pairs={{0,4},{4,0},{8,12},{12,8},{16,20},{20,16},{24,28},{28,24},{1,5},{5... | collective-permute-start | bytes 442376 | tf_op jit(solution)/shard_map/ppermute | solution.py:404
  48.2 7.0 %collective-permute-start.11 = (f32[72,512]{1,0:T(8,128)S(1)}, f32[72,512]{1,0:T(8,128)S(1)}, u32[]{:S(2)}, u32[]{:S(2)}) collective-permute-start(f32[72,512]{1,0:T(8,128)S(1)} %get-tuple-element.65), channel_id=1, source_target_pairs={{0,8},{4,12},{8,0},{12,4},{16,24},{20,28},{24,16},{28,20},{1,9},{5... | collective-permute-start | bytes 442376 | tf_op jit(solution)/shard_map/ppermute | solution.py:404
  50.6 6.5 %collective-permute-start.12 = (f32[72,512]{1,0:T(8,128)S(1)}, f32[72,512]{1,0:T(8,128)S(1)}, u32[]{:S(2)}, u32[]{:S(2)}) collective-permute-start(f32[72,512]{1,0:T(8,128)S(1)} %get-tuple-element.63), channel_id=1, source_target_pairs={{0,12},{4,8},{8,4},{12,0},{16,28},{20,24},{24,20},{28,16},{1,13},{... | collective-permute-start | bytes 442376 | tf_op jit(solution)/shard_map/ppermute | solution.py:404

commit v6 on v5

--- a/solution.py
+++ b/solution.py
@@ -267,25 +267,24 @@
     before = before_ref[...]
     after = after_ref[...]
     tail = x_ref.shape[1] - rows
-    for part in range(GROUP // 2):
-        quarters = (2 * part, 2 * part + 1)
-        strips = []
-        others = []
-        for q in quarters:
-            x = x_ref[q, 0:rows]
-            noise = n_ref[q]
-            if q == 0:
-                x = edged(x, before, pitch, turn * q, 0, 0, 4)
-                noise = edged(noise, before, pitch, turn * q, 4, 2, 2)
-            if q == GROUP - 1:
-                x = edged(x, after, pitch, turn * q, 4, pitch - EDGE, 4)
-                noise = edged(noise, after, pitch, turn * q, 0, pitch - EDGE, 2)
-            strips.append(jnp.concatenate([x, jnp.zeros((tail, strip), F32)], axis=0))
-            others.append(x * half + noise * spread)
-        firsts = [(turn * q) % lat for q in quarters]
-        scores = scores_of(strips, [shift, shift], firsts, w_in_ref, w_out_ref, pitch)
-        for q, score, other in zip(quarters, scores, others):
-            inc_ref[q] = roll(other + drift * score, -pitch * turn * q)
+    quarters = range(GROUP)
+    strips = []
+    others = []
+    for q in quarters:
+        x = x_ref[q, 0:rows]
+        noise = n_ref[q]
+        if q == 0:
+            x = edged(x, before, pitch, turn * q, 0, 0, 4)
+            noise = edged(noise, before, pitch, turn * q, 4, 2, 2)
+        if q == GROUP - 1:
+            x = edged(x, after, pitch, turn * q, 4, pitch - EDGE, 4)
+            noise = edged(noise, after, pitch, turn * q, 0, pitch - EDGE, 2)
+        strips.append(jnp.concatenate([x, jnp.zeros((tail, strip), F32)], axis=0))
+        others.append(x * half + noise * spread)
+    firsts = [(turn * q) % lat for q in quarters]
+    scores = scores_of(strips, [shift] * GROUP, firsts, w_in_ref, w_out_ref, pitch)
+    for q, score, other in zip(quarters, scores, others):
+        inc_ref[q] = roll(other + drift * score, -pitch * turn * q)
     for m in range(GROUP):
         outs[m][...] = inc_ref[lax.bitwise_xor(quarter, m)]
 
@@ -344,16 +343,15 @@
         return jnp.concatenate(outs, axis=1)
 
     running = jnp.zeros(sum_ref.shape[1:], F32)
-    for part in range(GROUP // 2):
-        levels = (2 * part, 2 * part + 1)
-        states = [base_ref[j] + carry for j in levels]
-        strips = [jnp.concatenate([x, jnp.zeros((tail, strip), F32)], axis=0) for x in states]
-        coefs = [[coef_ref[COEFS * (j + 1) + r : COEFS * (j + 1) + r + 1, 0:1] for r in range(4)] for j in levels]
-        shifts = [column_ref[...] * coef[3] for coef in coefs]
-        scores = scores_of(strips, shifts, [0, 0], w_in_ref, w_out_ref, pitch)
-        for j, x, score, coef in zip(levels, states, scores, coefs):
-            running = running + packed(x * coef[0] + score * coef[1])
-            sum_ref[j] = running
+    levels = range(GROUP)
+    states = [base_ref[j] + carry for j in levels]
+    strips = [jnp.concatenate([x, jnp.zeros((tail, strip), F32)], axis=0) for x in states]
+    coefs = [[coef_ref[COEFS * (j + 1) + r : COEFS * (j + 1) + r + 1, 0:1] for r in range(4)] for j in levels]
+    shifts = [column_ref[...] * coef[3] for coef in coefs]
+    scores = scores_of(strips, shifts, [0] * GROUP, w_in_ref, w_out_ref, pitch)
+    for j, x, score, coef in zip(levels, states, scores, coefs):
+        running = running + packed(x * coef[0] + score * coef[1])
+        sum_ref[j] = running
 
 
 def share_kernel(tight_ref, sum_ref, *refs):
@@ -381,7 +379,7 @@
     _, quarter = place()
     for m in range(GROUP):
         all_ref[lax.bitwise_xor(quarter, m)] = parts[m][...]
-    size = up_to(-(-chans // 3), ROWS)
+    size = up_to(-(-chans // sems.shape[0]), ROWS)
     copies = []
     for i, low in enumerate(range(0, chans, size)):
         high = min(low + size, chans)
@@ -526,7 +524,7 @@
         functools.partial(last_kernel, lat),
         [(chans * lat, width)],
         [VM] * GROUP,
-        [pltpu.VMEM((GROUP,) + tight, F32), pltpu.VMEM((chans * lat, width), F32), pltpu.SemaphoreType.DMA((3,))],
+        [pltpu.VMEM((GROUP,) + tight, F32), pltpu.VMEM((chans * lat, width), F32), pltpu.SemaphoreType.DMA((5,))],
         1 << 20,
         8,
         [HBM],

time: 58.3 us -> 58.1 us (level)
  transfers between devices with their start and end apart: 13 -> 13, of which waited for: 11 -> 11; matrix products, arithmetic and copies ran while one was open for 0% -> 0% of each run, Pallas kernels for 10% -> 9%
where the time goes in v6:
time: 58.1 us; the launch traced here: 58 us
  waiting for transfers between devices  25.2 us (43%)
  starting transfers between devices  20 us (34%)
  Pallas kernels  11.9 us (20%)
  between operations  0.73 us (1%)
    ppermute x9, waiting for transfers between devices, exchange(): lax.ppermute(pieces[m], 'lvl', [(k, k ^ m) for k in range(count)])  17.5 us
    ppermute x9, starting transfers between devices, exchange(): lax.ppermute(pieces[m], 'lvl', [(k, k ^ m) for k in range(count)])  11 us
    ppermute x2, waiting for transfers between devices, carried(): moved = lax.ppermute(total, 'lvl', pairs)  7.14 us
    ppermute x2, starting transfers between devices, carried(): moved = lax.ppermute(total, 'lvl', pairs)  6.49 us
    pallas_call x1, Pallas kernels, body(): call(functools.partial(second_kernel, lat), [(GROUP,) + tight], [VM] * 6,...  3.41 us
    pallas_call x1, Pallas kernels, body(): call(functools.partial(first_kernel, lat), [wide] * GROUP, [VM] * 8, [plt...  3.37 us
    ppermute x1, starting transfers between devices, body(): lax.ppermute(first, 'lon', [((k + 1) % count, k) for k in range(count)])  1.98 us
    pallas_call x1, Pallas kernels, body(): call(functools.partial(edges_kernel, lat), [edge, edge, (COEFS * (GROUP +...  1.92 us
  transfers between devices with their start and end apart: 13, of which 11 were waited for; matrix products, arithmetic and copies ran while one was open for 0% of the time, Pallas kernels for 9%

profile of v6, /device:TPU:0, one launch (start us, length us, event | category | flops | bytes accessed | tf_op | source)
XLA Modules:
  0.0 58.0 jit_solution(7764575678335562551)
XLA Ops:
  0.7 1.9 %shard_map.82 = (f32[72,128]{1,0:T(8,128)S(1)}, f32[72,128]{1,0:T(8,128)S(1)}, f32[40,128]{1,0:T(8,128)S(1)}, f32[1104,128]{1,0:T(8,128)S(1)}, f32[1104,128]{1,0...) custom-call(s32[1]{0:T(128)S(6)} %copy.9.start_ref, ...), custom_call_target="tpu_custom_call" | custom-call | flops 1048576 | bytes 4194304 | tf_op jit(solution)/shard_map/pallas_call | solution.py:438
  3.1 2.0 %collective-permute-start.1 = (f32[72,128]{1,0:T(8,128)S(1)}, f32[72,128]{1,0:T(8,128)S(1)}, u32[]{:S(2)}, u32[]{:S(2)}) collective-permute-start(f32[72,128]{1,0:T(8,128)S(1)} %get-tuple-element.36), channel_id=1, source_target_pairs={{1,0},{2,1},{3,2},{0,3},{5,4},{6,5},{7,6},{4,7},{9,8},{10,9},{11,1... | collective-permute-start | bytes 110600 | tf_op jit(solution)/shard_map/ppermute | solution.py:465
  5.1 1.3 %shard_map.83 = (bf16[192,720]{1,0:T(8,128)(2,1)S(1)}, bf16[216,576]{1,0:T(8,128)(2,1)S(1)}, f32[192,1]{1,0:T(8,128)S(1)}, f32[4,80,640]{2,1,0:T(8,128)S(1)}, f3...) custom-call(f32[40,128]{1,0:T(8,128)S(1)} %get-tuple-element.37.coef, ...), custom_call_target="tpu_custom_call" | custom-call | flops 244187136 | bytes 4194304 | tf_op jit(solution)/shard_map/pallas_call | solution.py:466
  6.9 3.4 %shard_map.84 = (f32[72,640]{1,0:T(8,128)S(1)}, f32[72,640]{1,0:T(8,128)S(1)}, f32[72,640]{1,0:T(8,128)S(1)}, f32[72,640]{1,0:T(8,128)S(1)}) custom-call(f32[40,128]{1,0:T(8,128)S(1)} %get-tuple-element.37.coef_ref, f32[4,80,640]{2,1,0:T(8,128)S(1)} %get-tuple-element.43.x_ref, f32[4,72,640]{2,1,0:T(8,128)S(1)} %get-tuple-element.44.n_ref, ...), custom_call_target="tpu_custom_call" | custom-call | flops 976748544 | bytes 4194304 | tf_op jit(solution)/shard_map/pallas_call | solution.py:485
  10.3 2.2 %collective-permute-start.2 = (f32[72,640]{1,0:T(8,128)S(1)}, f32[72,640]{1,0:T(8,128)S(1)}, u32[]{:S(2)}, u32[]{:S(2)}) collective-permute-start(f32[72,640]{1,0:T(8,128)S(1)} %get-tuple-element.49), channel_id=1, source_target_pairs={{0,4},{4,0},{8,12},{12,8},{16,20},{20,16},{24,28},{28,24},{1,5},{5... | collective-permute-start | bytes 552968 | tf_op jit(solution)/shard_map/ppermute | solution.py:402
  12.5 1.6 %collective-permute-start.3 = (f32[72,640]{1,0:T(8,128)S(1)}, f32[72,640]{1,0:T(8,128)S(1)}, u32[]{:S(2)}, u32[]{:S(2)}) collective-permute-start(f32[72,640]{1,0:T(8,128)S(1)} %get-tuple-element.50), channel_id=1, source_target_pairs={{0,8},{4,12},{8,0},{12,4},{16,24},{20,28},{24,16},{28,20},{1,9},{5... | collective-permute-start | bytes 552968 | tf_op jit(solution)/shard_map/ppermute | solution.py:402
  14.0 2.8 %collective-permute-done.2.refs_1_ = f32[72,640]{1,0:T(8,128)S(1)} collective-permute-done((f32[72,640]{1,0:T(8,128)S(1)}, f32[72,640]{1,0:T(8,128)S(1)}, u32[]{:S(2)}, u32[]{:S(2)}) %collective-permute-start.2) | collective-permute-done | bytes 184352 | tf_op jit(solution)/shard_map/ppermute | solution.py:402
  16.9 2.8 %collective-permute-done.3.refs_2_ = f32[72,640]{1,0:T(8,128)S(1)} collective-permute-done((f32[72,640]{1,0:T(8,128)S(1)}, f32[72,640]{1,0:T(8,128)S(1)}, u32[]{:S(2)}, u32[]{:S(2)}) %collective-permute-start.3) | collective-permute-done | bytes 184352 | tf_op jit(solution)/shard_map/ppermute | solution.py:402
  19.6 3.1 %collective-permute-done.4.refs_3_ = f32[72,640]{1,0:T(8,128)S(1)} collective-permute-done((f32[72,640]{1,0:T(8,128)S(1)}, f32[72,640]{1,0:T(8,128)S(1)}, u32[]{:S(2)}, u32[]{:S(2)}) %collective-permute-start.4) | collective-permute-done | bytes 184352 | tf_op jit(solution)/shard_map/ppermute | solution.py:402
  22.8 4.5 %collective-permute-start.5 = (f32[72,640]{1,0:T(8,128)S(1)}, f32[72,640]{1,0:T(8,128)S(1)}, u32[]{:S(2)}, u32[]{:S(2)}) collective-permute-start(f32[72,640]{1,0:T(8,128)S(1)} %add_add_fusion), channel_id=1, source_target_pairs={{0,24},{4,28},{8,16},{12,20},{16,8},{20,12},{24,0},{28,4},{1,25},{... | collective-permute-start | bytes 552968 | tf_op jit(solution)/shard_map/ppermute | solution.py:416
  27.2 1.5 %collective-permute-start.6 = (f32[72,512]{1,0:T(8,128)S(1)}, f32[72,512]{1,0:T(8,128)S(1)}, u32[]{:S(2)}, u32[]{:S(2)}) collective-permute-start(f32[72,512]{1,0:T(8,128)S(1)} %get-tuple-element.55), channel_id=1, source_target_pairs={{0,4},{4,0},{8,12},{12,8},{16,20},{20,16},{24,28},{28,24},{1,5},{5... | collective-permute-start | bytes 442376 | tf_op jit(solution)/shard_map/ppermute | solution.py:402
  28.8 2.0 %collective-permute-start.8 = (f32[72,512]{1,0:T(8,128)S(1)}, f32[72,512]{1,0:T(8,128)S(1)}, u32[]{:S(2)}, u32[]{:S(2)}) collective-permute-start(f32[72,512]{1,0:T(8,128)S(1)} %get-tuple-element.57), channel_id=1, source_target_pairs={{0,12},{4,8},{8,4},{12,0},{16,28},{20,24},{24,20},{28,16},{1,13},{... | collective-permute-start | bytes 442376 | tf_op jit(solution)/shard_map/ppermute | solution.py:402
  30.7 0.6 %shard_map.85 = (f32[4,72,640]{2,1,0:T(8,128)S(1)}, f32[72,512]{1,0:T(8,128)S(1)}) custom-call(f32[1104,128]{1,0:T(8,128)S(1)} %get-tuple-element.34.anchor_ref, f32[72,128]{1,0:T(8,128)S(1)} %collective-permute-done.before_ref, f32[72,128]{1,0:T(8,128)S(1)} %collective-permute-done.1.after_ref, f32[72,640]{1,0:T(8,128)S(1)} %get-tuple-element.48.refs_0_, ...), custom_call_target="tpu_custom_call" | custom-call | flops 244187136 | bytes 4194304 | tf_op jit(solution)/shard_map/pallas_call | solution.py:497
  31.4 1.4 %collective-permute-done.5 = f32[72,640]{1,0:T(8,128)S(1)} collective-permute-done((f32[72,640]{1,0:T(8,128)S(1)}, f32[72,640]{1,0:T(8,128)S(1)}, u32[]{:S(2)}, u32[]{:S(2)}) %collective-permute-start.5) | collective-permute-done | bytes 184352 | tf_op jit(solution)/shard_map/ppermute | solution.py:416
  32.8 3.4 %shard_map.86.sum_ref = f32[4,72,512]{2,1,0:T(8,128)S(1)} custom-call(f32[40,128]{1,0:T(8,128)S(1)} %get-tuple-element.37.coef_ref, f32[4,72,640]{2,1,0:T(8,128)S(1)} %get-tuple-element.53.base_ref, f32[192,1]{1,0:T(8,128)S(1)} %get-tuple-element.45.column_ref, bf16[192,720]{1,0:T(8,128)(2,1)S(1)} %get-tuple-element.46.w_in_ref, ...), custom_call_target="tpu_custom_call" | custom-call | flops 976748544 | bytes 4194304 | tf_op jit(solution)/shard_map/pallas_call | solution.py:505
  36.2 3.4 %collective-permute-done.8.refs_3_ = f32[72,512]{1,0:T(8,128)S(1)} collective-permute-done((f32[72,512]{1,0:T(8,128)S(1)}, f32[72,512]{1,0:T(8,128)S(1)}, u32[]{:S(2)}, u32[]{:S(2)}) %collective-permute-start.8) | collective-permute-done | bytes 147488 | tf_op jit(solution)/shard_map/ppermute | solution.py:402
  39.8 2.0 %collective-permute-start.9 = (f32[72,512]{1,0:T(8,128)S(1)}, f32[72,512]{1,0:T(8,128)S(1)}, u32[]{:S(2)}, u32[]{:S(2)}) collective-permute-start(f32[72,512]{1,0:T(8,128)S(1)} %get-tuple-element.59), channel_id=1, source_target_pairs={{0,24},{4,28},{8,16},{12,20},{16,8},{20,12},{24,0},{28,4},{1,25},{... | collective-permute-start | bytes 442376 | tf_op jit(solution)/shard_map/ppermute | solution.py:416
  41.8 5.7 %collective-permute-done.9 = f32[72,512]{1,0:T(8,128)S(1)} collective-permute-done((f32[72,512]{1,0:T(8,128)S(1)}, f32[72,512]{1,0:T(8,128)S(1)}, u32[]{:S(2)}, u32[]{:S(2)}) %collective-permute-start.9) | collective-permute-done | bytes 147488 | tf_op jit(solution)/shard_map/ppermute | solution.py:416
  48.1 2.4 %collective-permute-start.11 = (f32[72,512]{1,0:T(8,128)S(1)}, f32[72,512]{1,0:T(8,128)S(1)}, u32[]{:S(2)}, u32[]{:S(2)}) collective-permute-start(f32[72,512]{1,0:T(8,128)S(1)} %get-tuple-element.65), channel_id=1, source_target_pairs={{0,8},{4,12},{8,0},{12,4},{16,24},{20,28},{24,16},{28,20},{1,9},{5... | collective-permute-start | bytes 442376 | tf_op jit(solution)/shard_map/ppermute | solution.py:402
  50.5 1.0 %collective-permute-start.12 = (f32[72,512]{1,0:T(8,128)S(1)}, f32[72,512]{1,0:T(8,128)S(1)}, u32[]{:S(2)}, u32[]{:S(2)}) collective-permute-start(f32[72,512]{1,0:T(8,128)S(1)} %get-tuple-element.63), channel_id=1, source_target_pairs={{0,12},{4,8},{8,4},{12,0},{16,28},{20,24},{24,20},{28,16},{1,13},{... | collective-permute-start | bytes 442376 | tf_op jit(solution)/shard_map/ppermute | solution.py:402
  51.4 2.8 %collective-permute-done.10.refs_1_ = f32[72,512]{1,0:T(8,128)S(1)} collective-permute-done((f32[72,512]{1,0:T(8,128)S(1)}, f32[72,512]{1,0:T(8,128)S(1)}, u32[]{:S(2)}, u32[]{:S(2)}) %collective-permute-start.10) | collective-permute-done | bytes 147488 | tf_op jit(solution)/shard_map/ppermute | solution.py:402
  54.3 0.8 %collective-permute-done.11.refs_2_ = f32[72,512]{1,0:T(8,128)S(1)} collective-permute-done((f32[72,512]{1,0:T(8,128)S(1)}, f32[72,512]{1,0:T(8,128)S(1)}, u32[]{:S(2)}, u32[]{:S(2)}) %collective-permute-start.11) | collective-permute-done | bytes 147488 | tf_op jit(solution)/shard_map/ppermute | solution.py:402
  55.1 1.9 %collective-permute-done.12.refs_3_ = f32[72,512]{1,0:T(8,128)S(1)} collective-permute-done((f32[72,512]{1,0:T(8,128)S(1)}, f32[72,512]{1,0:T(8,128)S(1)}, u32[]{:S(2)}, u32[]{:S(2)}) %collective-permute-start.12) | collective-permute-done | bytes 147488 | tf_op jit(solution)/shard_map/ppermute | solution.py:402
  56.9 1.0 %shard_map.88 = f32[1104,128]{1,0:T(8,128)} custom-call(f32[72,512]{1,0:T(8,128)S(1)} %get-tuple-element.66.refs_0_, f32[72,512]{1,0:T(8,128)S(1)} %collective-permute-done.10.refs_1_, f32[72,512]{1,0:T(8,128)S(1)} %collective-permute-done.11.refs_2_, f32[72,512]{1,0:T(8,128)S(1)} %collective-permute-done.12.refs_3_), custom_call_target="tpu_custom_call" | custom-call | flops 1048576 | bytes 4194304 | tf_op jit(solution)/shard_map/pallas_call | solution.py:523
  (12 shorter events, 1.9 us)
Async XLA Ops:
  2.6 4.1 %collective-permute-start = (f32[72,128]{1,0:T(8,128)S(1)}, f32[72,128]{1,0:T(8,128)S(1)}, u32[]{:S(2)}, u32[]{:S(2)}) collective-permute-start(f32[72,128]{1,0:T(8,128)S(1)} %get-tuple-element.35), channel_id=1, source_target_pairs={{0,1},{1,2},{2,3},{3,0},{4,5},{5,6},{6,7},{7,4},{8,9},{9,10},{10,1... | collective-permute-start | bytes 110600 | tf_op jit(solution)/shard_map/ppermute | solution.py:464
  3.1 3.8 %collective-permute-start.1 = (f32[72,128]{1,0:T(8,128)S(1)}, f32[72,128]{1,0:T(8,128)S(1)}, u32[]{:S(2)}, u32[]{:S(2)}) collective-permute-start(f32[72,128]{1,0:T(8,128)S(1)} %get-tuple-element.36), channel_id=1, source_target_pairs={{1,0},{2,1},{3,2},{0,3},{5,4},{6,5},{7,6},{4,7},{9,8},{10,9},{11,1... | collective-permute-start | bytes 110600 | tf_op jit(solution)/shard_map/ppermute | solution.py:465
  10.3 6.6 %collective-permute-start.2 = (f32[72,640]{1,0:T(8,128)S(1)}, f32[72,640]{1,0:T(8,128)S(1)}, u32[]{:S(2)}, u32[]{:S(2)}) collective-permute-start(f32[72,640]{1,0:T(8,128)S(1)} %get-tuple-element.49), channel_id=1, source_target_pairs={{0,4},{4,0},{8,12},{12,8},{16,20},{20,16},{24,28},{28,24},{1,5},{5... | collective-permute-start | bytes 552968 | tf_op jit(solution)/shard_map/ppermute | solution.py:402
  12.5 7.2 %collective-permute-start.3 = (f32[72,640]{1,0:T(8,128)S(1)}, f32[72,640]{1,0:T(8,128)S(1)}, u32[]{:S(2)}, u32[]{:S(2)}) collective-permute-start(f32[72,640]{1,0:T(8,128)S(1)} %get-tuple-element.50), channel_id=1, source_target_pairs={{0,8},{4,12},{8,0},{12,4},{16,24},{20,28},{24,16},{28,20},{1,9},{5... | collective-permute-start | bytes 552968 | tf_op jit(solution)/shard_map/ppermute | solution.py:402
  14.0 8.6 %collective-permute-start.4 = (f32[72,640]{1,0:T(8,128)S(1)}, f32[72,640]{1,0:T(8,128)S(1)}, u32[]{:S(2)}, u32[]{:S(2)}) collective-permute-start(f32[72,640]{1,0:T(8,128)S(1)} %get-tuple-element.51), channel_id=1, source_target_pairs={{0,12},{4,8},{8,4},{12,0},{16,28},{20,24},{24,20},{28,16},{1,13},{... | collective-permute-start | bytes 552968 | tf_op jit(solution)/shard_map/ppermute | solution.py:402
  22.8 10.0 %collective-permute-start.5 = (f32[72,640]{1,0:T(8,128)S(1)}, f32[72,640]{1,0:T(8,128)S(1)}, u32[]{:S(2)}, u32[]{:S(2)}) collective-permute-start(f32[72,640]{1,0:T(8,128)S(1)} %add_add_fusion), channel_id=1, source_target_pairs={{0,24},{4,28},{8,16},{12,20},{16,8},{20,12},{24,0},{28,4},{1,25},{... | collective-permute-start | bytes 552968 | tf_op jit(solution)/shard_map/ppermute | solution.py:416
  27.2 9.0 %collective-permute-start.6 = (f32[72,512]{1,0:T(8,128)S(1)}, f32[72,512]{1,0:T(8,128)S(1)}, u32[]{:S(2)}, u32[]{:S(2)}) collective-permute-start(f32[72,512]{1,0:T(8,128)S(1)} %get-tuple-element.55), channel_id=1, source_target_pairs={{0,4},{4,0},{8,12},{12,8},{16,20},{20,16},{24,28},{28,24},{1,5},{5... | collective-permute-start | bytes 442376 | tf_op jit(solution)/shard_map/ppermute | solution.py:402
  28.8 7.5 %collective-permute-start.7 = (f32[72,512]{1,0:T(8,128)S(1)}, f32[72,512]{1,0:T(8,128)S(1)}, u32[]{:S(2)}, u32[]{:S(2)}) collective-permute-start(f32[72,512]{1,0:T(8,128)S(1)} %get-tuple-element.56), channel_id=1, source_target_pairs={{0,8},{4,12},{8,0},{12,4},{16,24},{20,28},{24,16},{28,20},{1,9},{5... | collective-permute-start | bytes 442376 | tf_op jit(solution)/shard_map/ppermute | solution.py:402
  28.8 10.8 %collective-permute-start.8 = (f32[72,512]{1,0:T(8,128)S(1)}, f32[72,512]{1,0:T(8,128)S(1)}, u32[]{:S(2)}, u32[]{:S(2)}) collective-permute-start(f32[72,512]{1,0:T(8,128)S(1)} %get-tuple-element.57), channel_id=1, source_target_pairs={{0,12},{4,8},{8,4},{12,0},{16,28},{20,24},{24,20},{28,16},{1,13},{... | collective-permute-start | bytes 442376 | tf_op jit(solution)/shard_map/ppermute | solution.py:402
  39.8 7.7 %collective-permute-start.9 = (f32[72,512]{1,0:T(8,128)S(1)}, f32[72,512]{1,0:T(8,128)S(1)}, u32[]{:S(2)}, u32[]{:S(2)}) collective-permute-start(f32[72,512]{1,0:T(8,128)S(1)} %get-tuple-element.59), channel_id=1, source_target_pairs={{0,24},{4,28},{8,16},{12,20},{16,8},{20,12},{24,0},{28,4},{1,25},{... | collective-permute-start | bytes 442376 | tf_op jit(solution)/shard_map/ppermute | solution.py:416
  47.6 6.6 %collective-permute-start.10 = (f32[72,512]{1,0:T(8,128)S(1)}, f32[72,512]{1,0:T(8,128)S(1)}, u32[]{:S(2)}, u32[]{:S(2)}) collective-permute-start(f32[72,512]{1,0:T(8,128)S(1)} %get-tuple-element.64), channel_id=1, source_target_pairs={{0,4},{4,0},{8,12},{12,8},{16,20},{20,16},{24,28},{28,24},{1,5},{5... | collective-permute-start | bytes 442376 | tf_op jit(solution)/shard_map/ppermute | solution.py:402
  48.1 7.0 %collective-permute-start.11 = (f32[72,512]{1,0:T(8,128)S(1)}, f32[72,512]{1,0:T(8,128)S(1)}, u32[]{:S(2)}, u32[]{:S(2)}) collective-permute-start(f32[72,512]{1,0:T(8,128)S(1)} %get-tuple-element.65), channel_id=1, source_target_pairs={{0,8},{4,12},{8,0},{12,4},{16,24},{20,28},{24,16},{28,20},{1,9},{5... | collective-permute-start | bytes 442376 | tf_op jit(solution)/shard_map/ppermute | solution.py:402
  50.5 6.5 %collective-permute-start.12 = (f32[72,512]{1,0:T(8,128)S(1)}, f32[72,512]{1,0:T(8,128)S(1)}, u32[]{:S(2)}, u32[]{:S(2)}) collective-permute-start(f32[72,512]{1,0:T(8,128)S(1)} %get-tuple-element.63), channel_id=1, source_target_pairs={{0,12},{4,8},{8,4},{12,0},{16,28},{20,24},{24,20},{28,16},{1,13},{... | collective-permute-start | bytes 442376 | tf_op jit(solution)/shard_map/ppermute | solution.py:402

commit v7 on v6

--- a/solution.py
+++ b/solution.py
@@ -357,16 +357,14 @@
 def share_kernel(tight_ref, sum_ref, *refs):
     waves = refs[:GROUP]
     outs = refs[GROUP : 2 * GROUP]
-    total_ref, wave_ref = refs[2 * GROUP :]
+    (wave_ref,) = refs[2 * GROUP :]
     mine, _ = place()
     for m in range(GROUP):
         wave_ref[lax.bitwise_xor(mine, m)] = waves[m][...]
-    noise = jnp.zeros(total_ref.shape, F32)
+    noise = jnp.zeros(tight_ref.shape, F32)
     for j in range(GROUP):
         noise = noise + wave_ref[j]
-        share = sum_ref[j] + noise
-        wave_ref[j] = tight_ref[...] + share
-    total_ref[...] = share
+        wave_ref[j] = tight_ref[...] + (sum_ref[j] + noise)
     for m in range(GROUP):
         outs[m][...] = wave_ref[lax.bitwise_xor(mine, m)]
 
@@ -510,16 +508,16 @@
         flops,
         20,
     )(coefs, base, column, w_in, w_out, carry)
+    carry = carried(sums[GROUP - 1] + (waves[0] + waves[1] + waves[2] + waves[3]), block)
     done = call(
         share_kernel,
-        [tight] * (GROUP + 1),
+        [tight] * GROUP,
         [VM] * (2 + GROUP),
         [pltpu.VMEM((GROUP,) + tight, F32)],
-        1 << 20,
+        flops // 4,
         4,
     )(packed, sums, *waves)
-    carry = carried(done[GROUP], block)
-    parts = exchange([part + carry for part in done[:GROUP]])
+    parts = exchange([part + carry for part in done])
     (out,) = call(
         functools.partial(last_kernel, lat),
         [(chans * lat, width)],

time: 58.1 us -> 58 us (level)
  transfers between devices with their start and end apart: 13 -> 13, of which waited for: 11 -> 11; matrix products, arithmetic and copies ran while one was open for 0% -> 0% of each run, Pallas kernels for 9% -> 10%
where the time goes in v7:
time: 58 us; the launch traced here: 57.8 us
  waiting for transfers between devices  24.9 us (43%)
  starting transfers between devices  20 us (34%)
  Pallas kernels  11.9 us (21%)
  between operations  0.73 us (1%)
    ppermute x9, waiting for transfers between devices, exchange(): lax.ppermute(pieces[m], 'lvl', [(k, k ^ m) for k in range(count)])  17.5 us
    ppermute x9, starting transfers between devices, exchange(): lax.ppermute(pieces[m], 'lvl', [(k, k ^ m) for k in range(count)])  11 us
    ppermute x2, waiting for transfers between devices, carried(): moved = lax.ppermute(total, 'lvl', pairs)  6.91 us
    ppermute x2, starting transfers between devices, carried(): moved = lax.ppermute(total, 'lvl', pairs)  6.49 us
    pallas_call x1, Pallas kernels, body(): call(functools.partial(second_kernel, lat), [(GROUP,) + tight], [VM] * 6,...  3.41 us
    pallas_call x1, Pallas kernels, body(): call(functools.partial(first_kernel, lat), [wide] * GROUP, [VM] * 8, [plt...  3.37 us
    ppermute x1, starting transfers between devices, body(): lax.ppermute(first, 'lon', [((k + 1) % count, k) for k in range(count)])  1.98 us
    pallas_call x1, Pallas kernels, body(): call(functools.partial(edges_kernel, lat), [edge, edge, (COEFS * (GROUP +...  1.92 us
  transfers between devices with their start and end apart: 13, of which 11 were waited for; matrix products, arithmetic and copies ran while one was open for 0% of the time, Pallas kernels for 10%

profile of v7, /device:TPU:0, one launch (start us, length us, event | category | flops | bytes accessed | tf_op | source)
XLA Modules:
  0.0 57.8 jit_solution(3189341714708949015)
XLA Ops:
  0.7 1.9 %shard_map.82 = (f32[72,128]{1,0:T(8,128)S(1)}, f32[72,128]{1,0:T(8,128)S(1)}, f32[40,128]{1,0:T(8,128)S(1)}, f32[1104,128]{1,0:T(8,128)S(1)}, f32[1104,128]{1,0...) custom-call(s32[1]{0:T(128)S(6)} %copy.9.start_ref, ...), custom_call_target="tpu_custom_call" | custom-call | flops 1048576 | bytes 4194304 | tf_op jit(solution)/shard_map/pallas_call | solution.py:436
  3.1 2.0 %collective-permute-start.1 = (f32[72,128]{1,0:T(8,128)S(1)}, f32[72,128]{1,0:T(8,128)S(1)}, u32[]{:S(2)}, u32[]{:S(2)}) collective-permute-start(f32[72,128]{1,0:T(8,128)S(1)} %get-tuple-element.35), channel_id=1, source_target_pairs={{1,0},{2,1},{3,2},{0,3},{5,4},{6,5},{7,6},{4,7},{9,8},{10,9},{11,1... | collective-permute-start | bytes 110600 | tf_op jit(solution)/shard_map/ppermute | solution.py:463
  5.1 1.3 %shard_map.83 = (bf16[192,720]{1,0:T(8,128)(2,1)S(1)}, bf16[216,576]{1,0:T(8,128)(2,1)S(1)}, f32[192,1]{1,0:T(8,128)S(1)}, f32[4,80,640]{2,1,0:T(8,128)S(1)}, f3...) custom-call(f32[40,128]{1,0:T(8,128)S(1)} %get-tuple-element.36.coef, ...), custom_call_target="tpu_custom_call" | custom-call | flops 244187136 | bytes 4194304 | tf_op jit(solution)/shard_map/pallas_call | solution.py:464
  6.9 3.4 %shard_map.84 = (f32[72,640]{1,0:T(8,128)S(1)}, f32[72,640]{1,0:T(8,128)S(1)}, f32[72,640]{1,0:T(8,128)S(1)}, f32[72,640]{1,0:T(8,128)S(1)}) custom-call(f32[40,128]{1,0:T(8,128)S(1)} %get-tuple-element.36.coef_ref, f32[4,80,640]{2,1,0:T(8,128)S(1)} %get-tuple-element.42.x_ref, f32[4,72,640]{2,1,0:T(8,128)S(1)} %get-tuple-element.43.n_ref, ...), custom_call_target="tpu_custom_call" | custom-call | flops 976748544 | bytes 4194304 | tf_op jit(solution)/shard_map/pallas_call | solution.py:483
  10.3 2.2 %collective-permute-start.2 = (f32[72,640]{1,0:T(8,128)S(1)}, f32[72,640]{1,0:T(8,128)S(1)}, u32[]{:S(2)}, u32[]{:S(2)}) collective-permute-start(f32[72,640]{1,0:T(8,128)S(1)} %get-tuple-element.48), channel_id=1, source_target_pairs={{0,4},{4,0},{8,12},{12,8},{16,20},{20,16},{24,28},{28,24},{1,5},{5... | collective-permute-start | bytes 552968 | tf_op jit(solution)/shard_map/ppermute | solution.py:400
  12.5 1.6 %collective-permute-start.3 = (f32[72,640]{1,0:T(8,128)S(1)}, f32[72,640]{1,0:T(8,128)S(1)}, u32[]{:S(2)}, u32[]{:S(2)}) collective-permute-start(f32[72,640]{1,0:T(8,128)S(1)} %get-tuple-element.49), channel_id=1, source_target_pairs={{0,8},{4,12},{8,0},{12,4},{16,24},{20,28},{24,16},{28,20},{1,9},{5... | collective-permute-start | bytes 552968 | tf_op jit(solution)/shard_map/ppermute | solution.py:400
  14.0 2.8 %collective-permute-done.2.refs_1_ = f32[72,640]{1,0:T(8,128)S(1)} collective-permute-done((f32[72,640]{1,0:T(8,128)S(1)}, f32[72,640]{1,0:T(8,128)S(1)}, u32[]{:S(2)}, u32[]{:S(2)}) %collective-permute-start.2) | collective-permute-done | bytes 184352 | tf_op jit(solution)/shard_map/ppermute | solution.py:400
  16.9 2.8 %collective-permute-done.3.refs_2_ = f32[72,640]{1,0:T(8,128)S(1)} collective-permute-done((f32[72,640]{1,0:T(8,128)S(1)}, f32[72,640]{1,0:T(8,128)S(1)}, u32[]{:S(2)}, u32[]{:S(2)}) %collective-permute-start.3) | collective-permute-done | bytes 184352 | tf_op jit(solution)/shard_map/ppermute | solution.py:400
  19.6 3.1 %collective-permute-done.4.refs_3_ = f32[72,640]{1,0:T(8,128)S(1)} collective-permute-done((f32[72,640]{1,0:T(8,128)S(1)}, f32[72,640]{1,0:T(8,128)S(1)}, u32[]{:S(2)}, u32[]{:S(2)}) %collective-permute-start.4) | collective-permute-done | bytes 184352 | tf_op jit(solution)/shard_map/ppermute | solution.py:400
  22.8 4.5 %collective-permute-start.5 = (f32[72,640]{1,0:T(8,128)S(1)}, f32[72,640]{1,0:T(8,128)S(1)}, u32[]{:S(2)}, u32[]{:S(2)}) collective-permute-start(f32[72,640]{1,0:T(8,128)S(1)} %add_add_fusion), channel_id=1, source_target_pairs={{0,24},{4,28},{8,16},{12,20},{16,8},{20,12},{24,0},{28,4},{1,25},{... | collective-permute-start | bytes 552968 | tf_op jit(solution)/shard_map/ppermute | solution.py:414
  27.2 1.5 %collective-permute-start.6 = (f32[72,512]{1,0:T(8,128)S(1)}, f32[72,512]{1,0:T(8,128)S(1)}, u32[]{:S(2)}, u32[]{:S(2)}) collective-permute-start(f32[72,512]{1,0:T(8,128)S(1)} %get-tuple-element.54), channel_id=1, source_target_pairs={{0,4},{4,0},{8,12},{12,8},{16,20},{20,16},{24,28},{28,24},{1,5},{5... | collective-permute-start | bytes 442376 | tf_op jit(solution)/shard_map/ppermute | solution.py:400
  28.8 2.0 %collective-permute-start.8 = (f32[72,512]{1,0:T(8,128)S(1)}, f32[72,512]{1,0:T(8,128)S(1)}, u32[]{:S(2)}, u32[]{:S(2)}) collective-permute-start(f32[72,512]{1,0:T(8,128)S(1)} %get-tuple-element.56), channel_id=1, source_target_pairs={{0,12},{4,8},{8,4},{12,0},{16,28},{20,24},{24,20},{28,16},{1,13},{... | collective-permute-start | bytes 442376 | tf_op jit(solution)/shard_map/ppermute | solution.py:400
  30.7 0.6 %shard_map.85 = (f32[4,72,640]{2,1,0:T(8,128)S(1)}, f32[72,512]{1,0:T(8,128)S(1)}) custom-call(f32[1104,128]{1,0:T(8,128)S(1)} %get-tuple-element.33.anchor_ref, f32[72,128]{1,0:T(8,128)S(1)} %collective-permute-done.before_ref, f32[72,128]{1,0:T(8,128)S(1)} %collective-permute-done.1.after_ref, f32[72,640]{1,0:T(8,128)S(1)} %get-tuple-element.47.refs_0_, ...), custom_call_target="tpu_custom_call" | custom-call | flops 244187136 | bytes 4194304 | tf_op jit(solution)/shard_map/pallas_call | solution.py:495
  31.4 1.4 %collective-permute-done.5 = f32[72,640]{1,0:T(8,128)S(1)} collective-permute-done((f32[72,640]{1,0:T(8,128)S(1)}, f32[72,640]{1,0:T(8,128)S(1)}, u32[]{:S(2)}, u32[]{:S(2)}) %collective-permute-start.5) | collective-permute-done | bytes 184352 | tf_op jit(solution)/shard_map/ppermute | solution.py:414
  32.8 3.4 %shard_map.86.sum_ref = f32[4,72,512]{2,1,0:T(8,128)S(1)} custom-call(f32[40,128]{1,0:T(8,128)S(1)} %get-tuple-element.36.coef_ref, f32[4,72,640]{2,1,0:T(8,128)S(1)} %get-tuple-element.52.base_ref, f32[192,1]{1,0:T(8,128)S(1)} %get-tuple-element.44.column_ref, bf16[192,720]{1,0:T(8,128)(2,1)S(1)} %get-tuple-element.45.w_in_ref, ...), custom_call_target="tpu_custom_call" | custom-call | flops 976748544 | bytes 4194304 | tf_op jit(solution)/shard_map/pallas_call | solution.py:503
  36.2 3.4 %collective-permute-done.8.refs_3_ = f32[72,512]{1,0:T(8,128)S(1)} collective-permute-done((f32[72,512]{1,0:T(8,128)S(1)}, f32[72,512]{1,0:T(8,128)S(1)}, u32[]{:S(2)}, u32[]{:S(2)}) %collective-permute-start.8) | collective-permute-done | bytes 147488 | tf_op jit(solution)/shard_map/ppermute | solution.py:400
  39.7 2.0 %collective-permute-start.9 = (f32[72,512]{1,0:T(8,128)S(1)}, f32[72,512]{1,0:T(8,128)S(1)}, u32[]{:S(2)}, u32[]{:S(2)}) collective-permute-start(f32[72,512]{1,0:T(8,128)S(1)} %fusion), channel_id=1, source_target_pairs={{0,24},{4,28},{8,16},{12,20},{16,8},{20,12},{24,0},{28,4},{1,25},{... | collective-permute-start | bytes 442376 | tf_op jit(solution)/shard_map/ppermute | solution.py:414
  41.9 5.5 %collective-permute-done.9 = f32[72,512]{1,0:T(8,128)S(1)} collective-permute-done((f32[72,512]{1,0:T(8,128)S(1)}, f32[72,512]{1,0:T(8,128)S(1)}, u32[]{:S(2)}, u32[]{:S(2)}) %collective-permute-start.9) | collective-permute-done | bytes 147488 | tf_op jit(solution)/shard_map/ppermute | solution.py:414
  47.9 2.4 %collective-permute-start.11 = (f32[72,512]{1,0:T(8,128)S(1)}, f32[72,512]{1,0:T(8,128)S(1)}, u32[]{:S(2)}, u32[]{:S(2)}) collective-permute-start(f32[72,512]{1,0:T(8,128)S(1)} %get-tuple-element.63), channel_id=1, source_target_pairs={{0,8},{4,12},{8,0},{12,4},{16,24},{20,28},{24,16},{28,20},{1,9},{5... | collective-permute-start | bytes 442376 | tf_op jit(solution)/shard_map/ppermute | solution.py:400
  50.3 1.0 %collective-permute-start.12 = (f32[72,512]{1,0:T(8,128)S(1)}, f32[72,512]{1,0:T(8,128)S(1)}, u32[]{:S(2)}, u32[]{:S(2)}) collective-permute-start(f32[72,512]{1,0:T(8,128)S(1)} %get-tuple-element.61), channel_id=1, source_target_pairs={{0,12},{4,8},{8,4},{12,0},{16,28},{20,24},{24,20},{28,16},{1,13},{... | collective-permute-start | bytes 442376 | tf_op jit(solution)/shard_map/ppermute | solution.py:400
  51.3 2.8 %collective-permute-done.10.refs_1_ = f32[72,512]{1,0:T(8,128)S(1)} collective-permute-done((f32[72,512]{1,0:T(8,128)S(1)}, f32[72,512]{1,0:T(8,128)S(1)}, u32[]{:S(2)}, u32[]{:S(2)}) %collective-permute-start.10) | collective-permute-done | bytes 147488 | tf_op jit(solution)/shard_map/ppermute | solution.py:400
  54.1 0.8 %collective-permute-done.11.refs_2_ = f32[72,512]{1,0:T(8,128)S(1)} collective-permute-done((f32[72,512]{1,0:T(8,128)S(1)}, f32[72,512]{1,0:T(8,128)S(1)}, u32[]{:S(2)}, u32[]{:S(2)}) %collective-permute-start.11) | collective-permute-done | bytes 147488 | tf_op jit(solution)/shard_map/ppermute | solution.py:400
  54.9 1.9 %collective-permute-done.12.refs_3_ = f32[72,512]{1,0:T(8,128)S(1)} collective-permute-done((f32[72,512]{1,0:T(8,128)S(1)}, f32[72,512]{1,0:T(8,128)S(1)}, u32[]{:S(2)}, u32[]{:S(2)}) %collective-permute-start.12) | collective-permute-done | bytes 147488 | tf_op jit(solution)/shard_map/ppermute | solution.py:400
  56.8 1.0 %shard_map.88 = f32[1104,128]{1,0:T(8,128)} custom-call(f32[72,512]{1,0:T(8,128)S(1)} %get-tuple-element.64.refs_0_, f32[72,512]{1,0:T(8,128)S(1)} %collective-permute-done.10.refs_1_, f32[72,512]{1,0:T(8,128)S(1)} %collective-permute-done.11.refs_2_, f32[72,512]{1,0:T(8,128)S(1)} %collective-permute-done.12.refs_3_), custom_call_target="tpu_custom_call" | custom-call | flops 1048576 | bytes 4194304 | tf_op jit(solution)/shard_map/pallas_call | solution.py:521
  (13 shorter events, 1.9 us)
Async XLA Ops:
  2.6 4.1 %collective-permute-start = (f32[72,128]{1,0:T(8,128)S(1)}, f32[72,128]{1,0:T(8,128)S(1)}, u32[]{:S(2)}, u32[]{:S(2)}) collective-permute-start(f32[72,128]{1,0:T(8,128)S(1)} %get-tuple-element.34), channel_id=1, source_target_pairs={{0,1},{1,2},{2,3},{3,0},{4,5},{5,6},{6,7},{7,4},{8,9},{9,10},{10,1... | collective-permute-start | bytes 110600 | tf_op jit(solution)/shard_map/ppermute | solution.py:462
  3.1 3.8 %collective-permute-start.1 = (f32[72,128]{1,0:T(8,128)S(1)}, f32[72,128]{1,0:T(8,128)S(1)}, u32[]{:S(2)}, u32[]{:S(2)}) collective-permute-start(f32[72,128]{1,0:T(8,128)S(1)} %get-tuple-element.35), channel_id=1, source_target_pairs={{1,0},{2,1},{3,2},{0,3},{5,4},{6,5},{7,6},{4,7},{9,8},{10,9},{11,1... | collective-permute-start | bytes 110600 | tf_op jit(solution)/shard_map/ppermute | solution.py:463
  10.3 6.6 %collective-permute-start.2 = (f32[72,640]{1,0:T(8,128)S(1)}, f32[72,640]{1,0:T(8,128)S(1)}, u32[]{:S(2)}, u32[]{:S(2)}) collective-permute-start(f32[72,640]{1,0:T(8,128)S(1)} %get-tuple-element.48), channel_id=1, source_target_pairs={{0,4},{4,0},{8,12},{12,8},{16,20},{20,16},{24,28},{28,24},{1,5},{5... | collective-permute-start | bytes 552968 | tf_op jit(solution)/shard_map/ppermute | solution.py:400
  12.5 7.2 %collective-permute-start.3 = (f32[72,640]{1,0:T(8,128)S(1)}, f32[72,640]{1,0:T(8,128)S(1)}, u32[]{:S(2)}, u32[]{:S(2)}) collective-permute-start(f32[72,640]{1,0:T(8,128)S(1)} %get-tuple-element.49), channel_id=1, source_target_pairs={{0,8},{4,12},{8,0},{12,4},{16,24},{20,28},{24,16},{28,20},{1,9},{5... | collective-permute-start | bytes 552968 | tf_op jit(solution)/shard_map/ppermute | solution.py:400
  14.0 8.6 %collective-permute-start.4 = (f32[72,640]{1,0:T(8,128)S(1)}, f32[72,640]{1,0:T(8,128)S(1)}, u32[]{:S(2)}, u32[]{:S(2)}) collective-permute-start(f32[72,640]{1,0:T(8,128)S(1)} %get-tuple-element.50), channel_id=1, source_target_pairs={{0,12},{4,8},{8,4},{12,0},{16,28},{20,24},{24,20},{28,16},{1,13},{... | collective-permute-start | bytes 552968 | tf_op jit(solution)/shard_map/ppermute | solution.py:400
  22.8 10.0 %collective-permute-start.5 = (f32[72,640]{1,0:T(8,128)S(1)}, f32[72,640]{1,0:T(8,128)S(1)}, u32[]{:S(2)}, u32[]{:S(2)}) collective-permute-start(f32[72,640]{1,0:T(8,128)S(1)} %add_add_fusion), channel_id=1, source_target_pairs={{0,24},{4,28},{8,16},{12,20},{16,8},{20,12},{24,0},{28,4},{1,25},{... | collective-permute-start | bytes 552968 | tf_op jit(solution)/shard_map/ppermute | solution.py:414
  27.2 9.0 %collective-permute-start.6 = (f32[72,512]{1,0:T(8,128)S(1)}, f32[72,512]{1,0:T(8,128)S(1)}, u32[]{:S(2)}, u32[]{:S(2)}) collective-permute-start(f32[72,512]{1,0:T(8,128)S(1)} %get-tuple-element.54), channel_id=1, source_target_pairs={{0,4},{4,0},{8,12},{12,8},{16,20},{20,16},{24,28},{28,24},{1,5},{5... | collective-permute-start | bytes 442376 | tf_op jit(solution)/shard_map/ppermute | solution.py:400
  28.8 7.5 %collective-permute-start.7 = (f32[72,512]{1,0:T(8,128)S(1)}, f32[72,512]{1,0:T(8,128)S(1)}, u32[]{:S(2)}, u32[]{:S(2)}) collective-permute-start(f32[72,512]{1,0:T(8,128)S(1)} %get-tuple-element.55), channel_id=1, source_target_pairs={{0,8},{4,12},{8,0},{12,4},{16,24},{20,28},{24,16},{28,20},{1,9},{5... | collective-permute-start | bytes 442376 | tf_op jit(solution)/shard_map/ppermute | solution.py:400
  28.8 10.8 %collective-permute-start.8 = (f32[72,512]{1,0:T(8,128)S(1)}, f32[72,512]{1,0:T(8,128)S(1)}, u32[]{:S(2)}, u32[]{:S(2)}) collective-permute-start(f32[72,512]{1,0:T(8,128)S(1)} %get-tuple-element.56), channel_id=1, source_target_pairs={{0,12},{4,8},{8,4},{12,0},{16,28},{20,24},{24,20},{28,16},{1,13},{... | collective-permute-start | bytes 442376 | tf_op jit(solution)/shard_map/ppermute | solution.py:400
  39.7 7.7 %collective-permute-start.9 = (f32[72,512]{1,0:T(8,128)S(1)}, f32[72,512]{1,0:T(8,128)S(1)}, u32[]{:S(2)}, u32[]{:S(2)}) collective-permute-start(f32[72,512]{1,0:T(8,128)S(1)} %fusion), channel_id=1, source_target_pairs={{0,24},{4,28},{8,16},{12,20},{16,8},{20,12},{24,0},{28,4},{1,25},{... | collective-permute-start | bytes 442376 | tf_op jit(solution)/shard_map/ppermute | solution.py:414
  47.5 6.6 %collective-permute-start.10 = (f32[72,512]{1,0:T(8,128)S(1)}, f32[72,512]{1,0:T(8,128)S(1)}, u32[]{:S(2)}, u32[]{:S(2)}) collective-permute-start(f32[72,512]{1,0:T(8,128)S(1)} %get-tuple-element.62), channel_id=1, source_target_pairs={{0,4},{4,0},{8,12},{12,8},{16,20},{20,16},{24,28},{28,24},{1,5},{5... | collective-permute-start | bytes 442376 | tf_op jit(solution)/shard_map/ppermute | solution.py:400
  47.9 7.0 %collective-permute-start.11 = (f32[72,512]{1,0:T(8,128)S(1)}, f32[72,512]{1,0:T(8,128)S(1)}, u32[]{:S(2)}, u32[]{:S(2)}) collective-permute-start(f32[72,512]{1,0:T(8,128)S(1)} %get-tuple-element.63), channel_id=1, source_target_pairs={{0,8},{4,12},{8,0},{12,4},{16,24},{20,28},{24,16},{28,20},{1,9},{5... | collective-permute-start | bytes 442376 | tf_op jit(solution)/shard_map/ppermute | solution.py:400
  50.3 6.5 %collective-permute-start.12 = (f32[72,512]{1,0:T(8,128)S(1)}, f32[72,512]{1,0:T(8,128)S(1)}, u32[]{:S(2)}, u32[]{:S(2)}) collective-permute-start(f32[72,512]{1,0:T(8,128)S(1)} %get-tuple-element.61), channel_id=1, source_target_pairs={{0,12},{4,8},{8,4},{12,0},{16,28},{20,24},{24,20},{28,16},{1,13},{... | collective-permute-start | bytes 442376 | tf_op jit(solution)/shard_map/ppermute | solution.py:400
